TPU v7x, 128 devices: a whole 4x4x4 slice. The times are simulated.
128 devices in a mesh: row: 16 (over y, z), col: 8 (over x, core).
Axes of the slice: x: 4, y: 4, z: 4, core: 2. Of those that a mesh axis runs over, the one named last changes fastest.
Arguments:
- root_rhs: bfloat16 [8, 8192], replicated, may hold values from -6 to 6
- diag_inv: bfloat16 [16, 512, 512], replicated, may hold values from -1 to 2
- tile_u: bfloat16 [16, 8, 1, 2, 128, 512], P('row', 'col'), may hold values from -0.1875 to 0.1875
- tile_v: bfloat16 [16, 8, 1, 2, 512, 128], P('row', 'col'), may hold values from -0.25 to 0.25
- tile_rank: int32 [16, 8, 1, 2], P('row', 'col'), may hold values from 16 to 128
- child_x: bfloat16 [128, 8, 512], P(('row', 'col')), may hold values from -6 to 6
- border_t: bfloat16 [128, 512, 1024], P(('row', 'col')), may hold values from -0.09375 to 0.09375
- child_inv: bfloat16 [128, 512, 512], P(('row', 'col')), may hold values from -1 to 2
- child_blocks: int32 [128, 8], P(('row', 'col')), may hold values from 0 to 63
Outputs:
- root_solution: float32 [8, 8192], P(None, ('row', 'col'))
- child_out: float32 [128, 8, 512], P(('row', 'col'))
All inputs are finite; a program needn't handle non-finite values.
Results may differ from a plain program's by a relative error of at most 0.017.
Values sent between devices are 32-bit elements; how exact they have to be, the bound alone decides.
No kernel may reach another device: no remote copies, remote signals or barrier semaphores. Data moves between devices by JAX's collectives and lax.ppermute only.
A program may use at most 64 MiB of HBM per device.

v0:
```python
import jax
import jax.numpy as jnp
from jax import lax
from jax.sharding import Mesh
from jax.sharding import PartitionSpec as P

BLK = 128
BB = 8
ROW = ("row_0", "row_1")
COL = ("col_0", "col_1")
ROW_COL = ("row_0", "row_1", "col_0", "col_1")


def copy_for_each(array, axis):
    copies = jnp.broadcast_to(array, (lax.axis_size(axis), *array.shape))
    return lax.all_to_all(copies, axis, split_axis=0, concat_axis=0, tiled=True)


def over_copies(array, axis):
    return copy_for_each(array, axis).sum(axis=0)


def by_axis(array, axes):
    far, near = axes
    return over_copies(over_copies(array, near), far)


def per_device(
    root_rhs, diag_inv, tile_u, tile_v, tile_rank, child_x, border_t, child_inv, child_blocks
):
    n_row = lax.axis_size(ROW)
    n_col = lax.axis_size(COL)
    my_row = lax.axis_index(ROW)
    my_col = lax.axis_index(COL)
    ntile = diag_inv.shape[0]
    tile = diag_inv.shape[1]
    rhs_count = root_rhs.shape[0]
    rank_max = tile_u.shape[4]
    t_rows = tile_u.shape[2]
    t_cols = tile_u.shape[3]
    left_tiles = tile_u[0, 0]
    right_tiles = tile_v[0, 0]
    tile_ranks = tile_rank[0, 0]
    blocks_per_front = tile // BLK
    n_child = child_x.shape[0]
    upward = jnp.einsum("crs,csb->crb", child_x, border_t, preferred_element_type=jnp.float32)
    pieces = (
        upward.reshape(n_child, rhs_count, BB, BLK)
        .transpose(1, 0, 2, 3)
        .reshape(rhs_count, n_child * BB, BLK)
    )
    flat_blocks = child_blocks.reshape(-1)
    dense_sum = (
        jnp.zeros((rhs_count, ntile * blocks_per_front, BLK), jnp.float32)
        .at[:, flat_blocks, :]
        .add(pieces)
    )
    dense_sum = dense_sum.reshape(rhs_count, ntile, tile)
    right_side = root_rhs.reshape(rhs_count, ntile, tile)
    col_ids = my_col + n_col * jnp.arange(t_cols)
    row_ids = my_row + n_row * jnp.arange(t_rows)
    rank_iota = jnp.arange(rank_max)

    def forward(column, solved_rows):
        owner_slot = column // n_row
        on_row = column % n_row == my_row
        known_cols = jnp.take(solved_rows, col_ids, axis=1).astype(jnp.bfloat16)
        right_row = lax.dynamic_index_in_dim(right_tiles, owner_slot, 0, keepdims=False)
        left_row_index = lax.dynamic_index_in_dim(left_tiles, owner_slot, 0, keepdims=False)
        rank_row = lax.dynamic_index_in_dim(tile_ranks, owner_slot, 0, keepdims=False)
        live_mask = (rank_iota[None, :] < rank_row[:, None]) & (col_ids[:, None] < column) & on_row
        coefficient_values = jnp.einsum(
            "rbt,btq->rbq", known_cols, right_row, preferred_element_type=jnp.float32
        )
        coefficient_values = jnp.where(live_mask[None], coefficient_values, 0.0).astype(
            jnp.bfloat16
        )
        partial_value = jnp.einsum(
            "rbq,bqt->rt", coefficient_values, left_row_index, preferred_element_type=jnp.float32
        )
        carried = lax.dynamic_index_in_dim(dense_sum, column, 1, keepdims=False)
        row_total = by_axis(partial_value + carried, (("row_0", "row_1"), ("col_0", "col_1")))
        block_rhs = lax.dynamic_index_in_dim(right_side, column, 1, keepdims=False).astype(
            jnp.float32
        )
        inverse = lax.dynamic_index_in_dim(diag_inv, column, 0, keepdims=False).astype(jnp.float32)
        fresh = jnp.dot(block_rhs - row_total, inverse)
        return lax.dynamic_update_index_in_dim(solved_rows, fresh, column, 1)

    solved_rows = lax.fori_loop(0, ntile, forward, jnp.zeros((rhs_count, ntile, tile), jnp.float32))

    def backward(sweep, result):
        column = ntile - 1 - sweep
        owner_slot = column // n_col
        on_col = column % n_col == my_col
        known_rows = jnp.take(result, row_ids, axis=1).astype(jnp.bfloat16)
        left_col = lax.dynamic_index_in_dim(left_tiles, owner_slot, 1, keepdims=False)
        right_col = lax.dynamic_index_in_dim(right_tiles, owner_slot, 1, keepdims=False)
        rank_col = lax.dynamic_index_in_dim(tile_ranks, owner_slot, 1, keepdims=False)
        live_mask = (rank_iota[None, :] < rank_col[:, None]) & (row_ids[:, None] > column) & on_col
        coefficient_values = jnp.einsum(
            "rat,aqt->raq", known_rows, left_col, preferred_element_type=jnp.float32
        )
        coefficient_values = jnp.where(live_mask[None], coefficient_values, 0.0).astype(
            jnp.bfloat16
        )
        partial_value = jnp.einsum(
            "raq,atq->rt", coefficient_values, right_col, preferred_element_type=jnp.float32
        )
        col_total = by_axis(partial_value, (("row_0", "row_1"), ("col_0", "col_1")))
        block_solved = lax.dynamic_index_in_dim(solved_rows, column, 1, keepdims=False)
        inverse = lax.dynamic_index_in_dim(diag_inv, column, 0, keepdims=False).astype(jnp.float32)
        fresh = jnp.dot(block_solved - col_total, inverse.T)
        return lax.dynamic_update_index_in_dim(result, fresh, column, 1)

    result = lax.fori_loop(0, ntile, backward, jnp.zeros((rhs_count, ntile, tile), jnp.float32))
    share = ntile * tile // (n_row * n_col)
    start = (my_row * n_col + my_col) * share
    root_part = lax.dynamic_slice_in_dim(result.reshape(rhs_count, ntile * tile), start, share, 1)
    gathered = result.reshape(rhs_count, ntile * blocks_per_front, BLK)[:, flat_blocks, :]
    gathered = gathered.reshape(rhs_count, n_child, BB * BLK).astype(jnp.bfloat16)
    returned = jnp.einsum("rcb,csb->crs", gathered, border_t, preferred_element_type=jnp.float32)
    child_out = child_x.astype(jnp.float32) - jnp.einsum(
        "crs,cst->crt", returned, child_inv.astype(jnp.float32)
    )
    return (root_part, child_out)


def solution(mesh):
    finer = Mesh(mesh.devices.reshape(4, 4, 4, 2), ("row_0", "row_1", "col_0", "col_1"))
    in_specs = (
        P(),
        P(),
        P(ROW, COL, None, None, None, None),
        P(ROW, COL, None, None, None, None),
        P(ROW, COL, None, None),
        P(ROW_COL, None, None),
        P(ROW_COL, None, None),
        P(ROW_COL, None, None),
        P(ROW_COL, None),
    )
    out_specs = (P(None, ROW_COL), P(ROW_COL, None, None))
    return jax.shard_map(
        per_device, mesh=finer, in_specs=in_specs, out_specs=out_specs, check_vma=False
    )
```

profile of v0, /device:TPU:0, one launch (start us, length us, event | category | flops | bytes accessed | tf_op | source)
XLA Modules:
  0.0 835.6 jit_solution(1126638640614776455)
XLA Ops:
  4.8 411.7 %while.33 = (s32[]{:T(128)}, f32[8,16,512]{2,0,1:T(8,128)S(1)}, bf16[8,16,512]{2,0,1:T(8,128)(2,1)}, s32[1,2]{1,0:T(1,128)}, s32[]{:T(128)}, /*index=5*/bf16[1,2...) while((s32[]{:T(128)}, f32[8,16,512]{2,0,1:T(8,128)S(1)}, ...), condition=%wide.region_4.5_spmd.clone, body=%wide.region_1.4_spmd.clone.sunk | while | flops 8505125 | bytes 3078457 | solution.py:90
  7.5 10.3 %all_to_all.56 = f32[8,8,512]{2,1,0:T(8,128)S(1)} all-to-all(f32[8,8,512]{2,1,0:T(8,128)S(1)} %broadcast_in_dim.236), channel_id=1, replica_groups=mesh['row_0'=4,'row_1'=4,'col_0'=4,'col_1'=2] {'col_0','col_1'}, dimensions={0} | all-to-all | bytes 262144 | tf_op jit(solution)/shard_map/while/body/eval_jaxpr/all_to_all | solution.py:16
  26.6 8.5 %all-to-all-done.1 = f32[16,8,512]{2,1,0:T(8,128)S(1)} async-done(((f32[16,8,512]{2,1,0:T(8,128)}), f32[16,8,512]{2,1,0:T(8,128)S(1)}, u32[]{:S(2)}, u32[]{:S(2)}) %all-to-all-start.1) | async-done | bytes 262176 | tf_op jit(solution)/shard_map/while/body/eval_jaxpr/all_to_all | solution.py:16
  39.1 8.5 %all_to_all.56 = f32[8,8,512]{2,1,0:T(8,128)S(1)} all-to-all(f32[8,8,512]{2,1,0:T(8,128)S(1)} %broadcast_in_dim.236), channel_id=1, replica_groups=mesh['row_0'=4,'row_1'=4,'col_0'=4,'col_1'=2] {'col_0','col_1'}, dimensions={0} | all-to-all | bytes 262144 | tf_op jit(solution)/shard_map/while/body/eval_jaxpr/all_to_all | solution.py:16
  52.0 8.5 %all-to-all-done.1 = f32[16,8,512]{2,1,0:T(8,128)S(1)} async-done(((f32[16,8,512]{2,1,0:T(8,128)}), f32[16,8,512]{2,1,0:T(8,128)S(1)}, u32[]{:S(2)}, u32[]{:S(2)}) %all-to-all-start.1) | async-done | bytes 262176 | tf_op jit(solution)/shard_map/while/body/eval_jaxpr/all_to_all | solution.py:16
  64.4 8.5 %all_to_all.56 = f32[8,8,512]{2,1,0:T(8,128)S(1)} all-to-all(f32[8,8,512]{2,1,0:T(8,128)S(1)} %broadcast_in_dim.236), channel_id=1, replica_groups=mesh['row_0'=4,'row_1'=4,'col_0'=4,'col_1'=2] {'col_0','col_1'}, dimensions={0} | all-to-all | bytes 262144 | tf_op jit(solution)/shard_map/while/body/eval_jaxpr/all_to_all | solution.py:16
  77.3 8.5 %all-to-all-done.1 = f32[16,8,512]{2,1,0:T(8,128)S(1)} async-done(((f32[16,8,512]{2,1,0:T(8,128)}), f32[16,8,512]{2,1,0:T(8,128)S(1)}, u32[]{:S(2)}, u32[]{:S(2)}) %all-to-all-start.1) | async-done | bytes 262176 | tf_op jit(solution)/shard_map/while/body/eval_jaxpr/all_to_all | solution.py:16
  89.8 8.5 %all_to_all.56 = f32[8,8,512]{2,1,0:T(8,128)S(1)} all-to-all(f32[8,8,512]{2,1,0:T(8,128)S(1)} %broadcast_in_dim.236), channel_id=1, replica_groups=mesh['row_0'=4,'row_1'=4,'col_0'=4,'col_1'=2] {'col_0','col_1'}, dimensions={0} | all-to-all | bytes 262144 | tf_op jit(solution)/shard_map/while/body/eval_jaxpr/all_to_all | solution.py:16
  102.6 8.5 %all-to-all-done.1 = f32[16,8,512]{2,1,0:T(8,128)S(1)} async-done(((f32[16,8,512]{2,1,0:T(8,128)}), f32[16,8,512]{2,1,0:T(8,128)S(1)}, u32[]{:S(2)}, u32[]{:S(2)}) %all-to-all-start.1) | async-done | bytes 262176 | tf_op jit(solution)/shard_map/while/body/eval_jaxpr/all_to_all | solution.py:16
  115.1 8.5 %all_to_all.56 = f32[8,8,512]{2,1,0:T(8,128)S(1)} all-to-all(f32[8,8,512]{2,1,0:T(8,128)S(1)} %broadcast_in_dim.236), channel_id=1, replica_groups=mesh['row_0'=4,'row_1'=4,'col_0'=4,'col_1'=2] {'col_0','col_1'}, dimensions={0} | all-to-all | bytes 262144 | tf_op jit(solution)/shard_map/while/body/eval_jaxpr/all_to_all | solution.py:16
  128.0 8.5 %all-to-all-done.1 = f32[16,8,512]{2,1,0:T(8,128)S(1)} async-done(((f32[16,8,512]{2,1,0:T(8,128)}), f32[16,8,512]{2,1,0:T(8,128)S(1)}, u32[]{:S(2)}, u32[]{:S(2)}) %all-to-all-start.1) | async-done | bytes 262176 | tf_op jit(solution)/shard_map/while/body/eval_jaxpr/all_to_all | solution.py:16
  140.5 8.5 %all_to_all.56 = f32[8,8,512]{2,1,0:T(8,128)S(1)} all-to-all(f32[8,8,512]{2,1,0:T(8,128)S(1)} %broadcast_in_dim.236), channel_id=1, replica_groups=mesh['row_0'=4,'row_1'=4,'col_0'=4,'col_1'=2] {'col_0','col_1'}, dimensions={0} | all-to-all | bytes 262144 | tf_op jit(solution)/shard_map/while/body/eval_jaxpr/all_to_all | solution.py:16
  153.3 8.5 %all-to-all-done.1 = f32[16,8,512]{2,1,0:T(8,128)S(1)} async-done(((f32[16,8,512]{2,1,0:T(8,128)}), f32[16,8,512]{2,1,0:T(8,128)S(1)}, u32[]{:S(2)}, u32[]{:S(2)}) %all-to-all-start.1) | async-done | bytes 262176 | tf_op jit(solution)/shard_map/while/body/eval_jaxpr/all_to_all | solution.py:16
  165.8 8.5 %all_to_all.56 = f32[8,8,512]{2,1,0:T(8,128)S(1)} all-to-all(f32[8,8,512]{2,1,0:T(8,128)S(1)} %broadcast_in_dim.236), channel_id=1, replica_groups=mesh['row_0'=4,'row_1'=4,'col_0'=4,'col_1'=2] {'col_0','col_1'}, dimensions={0} | all-to-all | bytes 262144 | tf_op jit(solution)/shard_map/while/body/eval_jaxpr/all_to_all | solution.py:16
  178.7 8.5 %all-to-all-done.1 = f32[16,8,512]{2,1,0:T(8,128)S(1)} async-done(((f32[16,8,512]{2,1,0:T(8,128)}), f32[16,8,512]{2,1,0:T(8,128)S(1)}, u32[]{:S(2)}, u32[]{:S(2)}) %all-to-all-start.1) | async-done | bytes 262176 | tf_op jit(solution)/shard_map/while/body/eval_jaxpr/all_to_all | solution.py:16
  191.2 8.5 %all_to_all.56 = f32[8,8,512]{2,1,0:T(8,128)S(1)} all-to-all(f32[8,8,512]{2,1,0:T(8,128)S(1)} %broadcast_in_dim.236), channel_id=1, replica_groups=mesh['row_0'=4,'row_1'=4,'col_0'=4,'col_1'=2] {'col_0','col_1'}, dimensions={0} | all-to-all | bytes 262144 | tf_op jit(solution)/shard_map/while/body/eval_jaxpr/all_to_all | solution.py:16
  204.0 8.5 %all-to-all-done.1 = f32[16,8,512]{2,1,0:T(8,128)S(1)} async-done(((f32[16,8,512]{2,1,0:T(8,128)}), f32[16,8,512]{2,1,0:T(8,128)S(1)}, u32[]{:S(2)}, u32[]{:S(2)}) %all-to-all-start.1) | async-done | bytes 262176 | tf_op jit(solution)/shard_map/while/body/eval_jaxpr/all_to_all | solution.py:16
  216.5 8.5 %all_to_all.56 = f32[8,8,512]{2,1,0:T(8,128)S(1)} all-to-all(f32[8,8,512]{2,1,0:T(8,128)S(1)} %broadcast_in_dim.236), channel_id=1, replica_groups=mesh['row_0'=4,'row_1'=4,'col_0'=4,'col_1'=2] {'col_0','col_1'}, dimensions={0} | all-to-all | bytes 262144 | tf_op jit(solution)/shard_map/while/body/eval_jaxpr/all_to_all | solution.py:16
  229.4 8.5 %all-to-all-done.1 = f32[16,8,512]{2,1,0:T(8,128)S(1)} async-done(((f32[16,8,512]{2,1,0:T(8,128)}), f32[16,8,512]{2,1,0:T(8,128)S(1)}, u32[]{:S(2)}, u32[]{:S(2)}) %all-to-all-start.1) | async-done | bytes 262176 | tf_op jit(solution)/shard_map/while/body/eval_jaxpr/all_to_all | solution.py:16
  241.8 8.5 %all_to_all.56 = f32[8,8,512]{2,1,0:T(8,128)S(1)} all-to-all(f32[8,8,512]{2,1,0:T(8,128)S(1)} %broadcast_in_dim.236), channel_id=1, replica_groups=mesh['row_0'=4,'row_1'=4,'col_0'=4,'col_1'=2] {'col_0','col_1'}, dimensions={0} | all-to-all | bytes 262144 | tf_op jit(solution)/shard_map/while/body/eval_jaxpr/all_to_all | solution.py:16
  254.7 8.5 %all-to-all-done.1 = f32[16,8,512]{2,1,0:T(8,128)S(1)} async-done(((f32[16,8,512]{2,1,0:T(8,128)}), f32[16,8,512]{2,1,0:T(8,128)S(1)}, u32[]{:S(2)}, u32[]{:S(2)}) %all-to-all-start.1) | async-done | bytes 262176 | tf_op jit(solution)/shard_map/while/body/eval_jaxpr/all_to_all | solution.py:16
  267.2 8.5 %all_to_all.56 = f32[8,8,512]{2,1,0:T(8,128)S(1)} all-to-all(f32[8,8,512]{2,1,0:T(8,128)S(1)} %broadcast_in_dim.236), channel_id=1, replica_groups=mesh['row_0'=4,'row_1'=4,'col_0'=4,'col_1'=2] {'col_0','col_1'}, dimensions={0} | all-to-all | bytes 262144 | tf_op jit(solution)/shard_map/while/body/eval_jaxpr/all_to_all | solution.py:16
  280.0 8.5 %all-to-all-done.1 = f32[16,8,512]{2,1,0:T(8,128)S(1)} async-done(((f32[16,8,512]{2,1,0:T(8,128)}), f32[16,8,512]{2,1,0:T(8,128)S(1)}, u32[]{:S(2)}, u32[]{:S(2)}) %all-to-all-start.1) | async-done | bytes 262176 | tf_op jit(solution)/shard_map/while/body/eval_jaxpr/all_to_all | solution.py:16
  292.5 8.5 %all_to_all.56 = f32[8,8,512]{2,1,0:T(8,128)S(1)} all-to-all(f32[8,8,512]{2,1,0:T(8,128)S(1)} %broadcast_in_dim.236), channel_id=1, replica_groups=mesh['row_0'=4,'row_1'=4,'col_0'=4,'col_1'=2] {'col_0','col_1'}, dimensions={0} | all-to-all | bytes 262144 | tf_op jit(solution)/shard_map/while/body/eval_jaxpr/all_to_all | solution.py:16
  305.4 8.5 %all-to-all-done.1 = f32[16,8,512]{2,1,0:T(8,128)S(1)} async-done(((f32[16,8,512]{2,1,0:T(8,128)}), f32[16,8,512]{2,1,0:T(8,128)S(1)}, u32[]{:S(2)}, u32[]{:S(2)}) %all-to-all-start.1) | async-done | bytes 262176 | tf_op jit(solution)/shard_map/while/body/eval_jaxpr/all_to_all | solution.py:16
  317.9 8.5 %all_to_all.56 = f32[8,8,512]{2,1,0:T(8,128)S(1)} all-to-all(f32[8,8,512]{2,1,0:T(8,128)S(1)} %broadcast_in_dim.236), channel_id=1, replica_groups=mesh['row_0'=4,'row_1'=4,'col_0'=4,'col_1'=2] {'col_0','col_1'}, dimensions={0} | all-to-all | bytes 262144 | tf_op jit(solution)/shard_map/while/body/eval_jaxpr/all_to_all | solution.py:16
  330.7 8.5 %all-to-all-done.1 = f32[16,8,512]{2,1,0:T(8,128)S(1)} async-done(((f32[16,8,512]{2,1,0:T(8,128)}), f32[16,8,512]{2,1,0:T(8,128)S(1)}, u32[]{:S(2)}, u32[]{:S(2)}) %all-to-all-start.1) | async-done | bytes 262176 | tf_op jit(solution)/shard_map/while/body/eval_jaxpr/all_to_all | solution.py:16
  343.2 8.5 %all_to_all.56 = f32[8,8,512]{2,1,0:T(8,128)S(1)} all-to-all(f32[8,8,512]{2,1,0:T(8,128)S(1)} %broadcast_in_dim.236), channel_id=1, replica_groups=mesh['row_0'=4,'row_1'=4,'col_0'=4,'col_1'=2] {'col_0','col_1'}, dimensions={0} | all-to-all | bytes 262144 | tf_op jit(solution)/shard_map/while/body/eval_jaxpr/all_to_all | solution.py:16
  356.1 8.5 %all-to-all-done.1 = f32[16,8,512]{2,1,0:T(8,128)S(1)} async-done(((f32[16,8,512]{2,1,0:T(8,128)}), f32[16,8,512]{2,1,0:T(8,128)S(1)}, u32[]{:S(2)}, u32[]{:S(2)}) %all-to-all-start.1) | async-done | bytes 262176 | tf_op jit(solution)/shard_map/while/body/eval_jaxpr/all_to_all | solution.py:16
  368.6 8.5 %all_to_all.56 = f32[8,8,512]{2,1,0:T(8,128)S(1)} all-to-all(f32[8,8,512]{2,1,0:T(8,128)S(1)} %broadcast_in_dim.236), channel_id=1, replica_groups=mesh['row_0'=4,'row_1'=4,'col_0'=4,'col_1'=2] {'col_0','col_1'}, dimensions={0} | all-to-all | bytes 262144 | tf_op jit(solution)/shard_map/while/body/eval_jaxpr/all_to_all | solution.py:16
  381.4 8.5 %all-to-all-done.1 = f32[16,8,512]{2,1,0:T(8,128)S(1)} async-done(((f32[16,8,512]{2,1,0:T(8,128)}), f32[16,8,512]{2,1,0:T(8,128)S(1)}, u32[]{:S(2)}, u32[]{:S(2)}) %all-to-all-start.1) | async-done | bytes 262176 | tf_op jit(solution)/shard_map/while/body/eval_jaxpr/all_to_all | solution.py:16
  393.9 8.5 %all_to_all.56 = f32[8,8,512]{2,1,0:T(8,128)S(1)} all-to-all(f32[8,8,512]{2,1,0:T(8,128)S(1)} %broadcast_in_dim.236), channel_id=1, replica_groups=mesh['row_0'=4,'row_1'=4,'col_0'=4,'col_1'=2] {'col_0','col_1'}, dimensions={0} | all-to-all | bytes 262144 | tf_op jit(solution)/shard_map/while/body/eval_jaxpr/all_to_all | solution.py:16
  406.8 8.5 %all-to-all-done.1 = f32[16,8,512]{2,1,0:T(8,128)S(1)} async-done(((f32[16,8,512]{2,1,0:T(8,128)}), f32[16,8,512]{2,1,0:T(8,128)S(1)}, u32[]{:S(2)}, u32[]{:S(2)}) %all-to-all-start.1) | async-done | bytes 262176 | tf_op jit(solution)/shard_map/while/body/eval_jaxpr/all_to_all | solution.py:16
  416.6 416.6 %while.34 = (s32[]{:T(128)}, f32[8,16,512]{2,0,1:T(8,128)S(1)}, f32[8,16,512]{2,0,1:T(8,128)S(1)}, s32[1,2]{1,0:T(1,128)}, s32[]{:T(128)}, /*index=5*/s32[]{:T(1...) while((s32[]{:T(128)}, f32[8,16,512]{2,0,1:T(8,128)S(1)}, ...), condition=%wide.region_8.9_spmd.clone, body=%wide.region_5.8_spmd.clone.sunk | while | flops 6392221 | bytes 2765459 | solution.py:116
  420.0 8.5 %all_to_all.57 = f32[8,8,512]{2,1,0:T(8,128)S(1)} all-to-all(f32[8,8,512]{2,1,0:T(8,128)S(1)} %broadcast_in_dim.240), channel_id=1, replica_groups=mesh['row_0'=4,'row_1'=4,'col_0'=4,'col_1'=2] {'col_0','col_1'}, dimensions={0} | all-to-all | bytes 262144 | tf_op jit(solution)/shard_map/while/body/eval_jaxpr/all_to_all | solution.py:16
  432.9 8.5 %all-to-all-done.3 = f32[16,8,512]{2,1,0:T(8,128)S(1)} async-done(((f32[16,8,512]{2,1,0:T(8,128)}), f32[16,8,512]{2,1,0:T(8,128)S(1)}, u32[]{:S(2)}, u32[]{:S(2)}) %all-to-all-start.3) | async-done | bytes 262176 | tf_op jit(solution)/shard_map/while/body/eval_jaxpr/all_to_all | solution.py:16
  446.1 8.5 %all_to_all.57 = f32[8,8,512]{2,1,0:T(8,128)S(1)} all-to-all(f32[8,8,512]{2,1,0:T(8,128)S(1)} %broadcast_in_dim.240), channel_id=1, replica_groups=mesh['row_0'=4,'row_1'=4,'col_0'=4,'col_1'=2] {'col_0','col_1'}, dimensions={0} | all-to-all | bytes 262144 | tf_op jit(solution)/shard_map/while/body/eval_jaxpr/all_to_all | solution.py:16
  458.9 8.5 %all-to-all-done.3 = f32[16,8,512]{2,1,0:T(8,128)S(1)} async-done(((f32[16,8,512]{2,1,0:T(8,128)}), f32[16,8,512]{2,1,0:T(8,128)S(1)}, u32[]{:S(2)}, u32[]{:S(2)}) %all-to-all-start.3) | async-done | bytes 262176 | tf_op jit(solution)/shard_map/while/body/eval_jaxpr/all_to_all | solution.py:16
  472.1 8.5 %all_to_all.57 = f32[8,8,512]{2,1,0:T(8,128)S(1)} all-to-all(f32[8,8,512]{2,1,0:T(8,128)S(1)} %broadcast_in_dim.240), channel_id=1, replica_groups=mesh['row_0'=4,'row_1'=4,'col_0'=4,'col_1'=2] {'col_0','col_1'}, dimensions={0} | all-to-all | bytes 262144 | tf_op jit(solution)/shard_map/while/body/eval_jaxpr/all_to_all | solution.py:16
  485.0 8.5 %all-to-all-done.3 = f32[16,8,512]{2,1,0:T(8,128)S(1)} async-done(((f32[16,8,512]{2,1,0:T(8,128)}), f32[16,8,512]{2,1,0:T(8,128)S(1)}, u32[]{:S(2)}, u32[]{:S(2)}) %all-to-all-start.3) | async-done | bytes 262176 | tf_op jit(solution)/shard_map/while/body/eval_jaxpr/all_to_all | solution.py:16
  498.1 8.5 %all_to_all.57 = f32[8,8,512]{2,1,0:T(8,128)S(1)} all-to-all(f32[8,8,512]{2,1,0:T(8,128)S(1)} %broadcast_in_dim.240), channel_id=1, replica_groups=mesh['row_0'=4,'row_1'=4,'col_0'=4,'col_1'=2] {'col_0','col_1'}, dimensions={0} | all-to-all | bytes 262144 | tf_op jit(solution)/shard_map/while/body/eval_jaxpr/all_to_all | solution.py:16
  511.0 8.5 %all-to-all-done.3 = f32[16,8,512]{2,1,0:T(8,128)S(1)} async-done(((f32[16,8,512]{2,1,0:T(8,128)}), f32[16,8,512]{2,1,0:T(8,128)S(1)}, u32[]{:S(2)}, u32[]{:S(2)}) %all-to-all-start.3) | async-done | bytes 262176 | tf_op jit(solution)/shard_map/while/body/eval_jaxpr/all_to_all | solution.py:16
  524.2 8.5 %all_to_all.57 = f32[8,8,512]{2,1,0:T(8,128)S(1)} all-to-all(f32[8,8,512]{2,1,0:T(8,128)S(1)} %broadcast_in_dim.240), channel_id=1, replica_groups=mesh['row_0'=4,'row_1'=4,'col_0'=4,'col_1'=2] {'col_0','col_1'}, dimensions={0} | all-to-all | bytes 262144 | tf_op jit(solution)/shard_map/while/body/eval_jaxpr/all_to_all | solution.py:16
  537.0 8.5 %all-to-all-done.3 = f32[16,8,512]{2,1,0:T(8,128)S(1)} async-done(((f32[16,8,512]{2,1,0:T(8,128)}), f32[16,8,512]{2,1,0:T(8,128)S(1)}, u32[]{:S(2)}, u32[]{:S(2)}) %all-to-all-start.3) | async-done | bytes 262176 | tf_op jit(solution)/shard_map/while/body/eval_jaxpr/all_to_all | solution.py:16
  550.2 8.5 %all_to_all.57 = f32[8,8,512]{2,1,0:T(8,128)S(1)} all-to-all(f32[8,8,512]{2,1,0:T(8,128)S(1)} %broadcast_in_dim.240), channel_id=1, replica_groups=mesh['row_0'=4,'row_1'=4,'col_0'=4,'col_1'=2] {'col_0','col_1'}, dimensions={0} | all-to-all | bytes 262144 | tf_op jit(solution)/shard_map/while/body/eval_jaxpr/all_to_all | solution.py:16
  563.1 8.5 %all-to-all-done.3 = f32[16,8,512]{2,1,0:T(8,128)S(1)} async-done(((f32[16,8,512]{2,1,0:T(8,128)}), f32[16,8,512]{2,1,0:T(8,128)S(1)}, u32[]{:S(2)}, u32[]{:S(2)}) %all-to-all-start.3) | async-done | bytes 262176 | tf_op jit(solution)/shard_map/while/body/eval_jaxpr/all_to_all | solution.py:16
  576.2 8.5 %all_to_all.57 = f32[8,8,512]{2,1,0:T(8,128)S(1)} all-to-all(f32[8,8,512]{2,1,0:T(8,128)S(1)} %broadcast_in_dim.240), channel_id=1, replica_groups=mesh['row_0'=4,'row_1'=4,'col_0'=4,'col_1'=2] {'col_0','col_1'}, dimensions={0} | all-to-all | bytes 262144 | tf_op jit(solution)/shard_map/while/body/eval_jaxpr/all_to_all | solution.py:16
  589.1 8.5 %all-to-all-done.3 = f32[16,8,512]{2,1,0:T(8,128)S(1)} async-done(((f32[16,8,512]{2,1,0:T(8,128)}), f32[16,8,512]{2,1,0:T(8,128)S(1)}, u32[]{:S(2)}, u32[]{:S(2)}) %all-to-all-start.3) | async-done | bytes 262176 | tf_op jit(solution)/shard_map/while/body/eval_jaxpr/all_to_all | solution.py:16
  602.3 8.5 %all_to_all.57 = f32[8,8,512]{2,1,0:T(8,128)S(1)} all-to-all(f32[8,8,512]{2,1,0:T(8,128)S(1)} %broadcast_in_dim.240), channel_id=1, replica_groups=mesh['row_0'=4,'row_1'=4,'col_0'=4,'col_1'=2] {'col_0','col_1'}, dimensions={0} | all-to-all | bytes 262144 | tf_op jit(solution)/shard_map/while/body/eval_jaxpr/all_to_all | solution.py:16
  615.1 8.5 %all-to-all-done.3 = f32[16,8,512]{2,1,0:T(8,128)S(1)} async-done(((f32[16,8,512]{2,1,0:T(8,128)}), f32[16,8,512]{2,1,0:T(8,128)S(1)}, u32[]{:S(2)}, u32[]{:S(2)}) %all-to-all-start.3) | async-done | bytes 262176 | tf_op jit(solution)/shard_map/while/body/eval_jaxpr/all_to_all | solution.py:16
  628.3 8.5 %all_to_all.57 = f32[8,8,512]{2,1,0:T(8,128)S(1)} all-to-all(f32[8,8,512]{2,1,0:T(8,128)S(1)} %broadcast_in_dim.240), channel_id=1, replica_groups=mesh['row_0'=4,'row_1'=4,'col_0'=4,'col_1'=2] {'col_0','col_1'}, dimensions={0} | all-to-all | bytes 262144 | tf_op jit(solution)/shard_map/while/body/eval_jaxpr/all_to_all | solution.py:16
  641.2 8.5 %all-to-all-done.3 = f32[16,8,512]{2,1,0:T(8,128)S(1)} async-done(((f32[16,8,512]{2,1,0:T(8,128)}), f32[16,8,512]{2,1,0:T(8,128)S(1)}, u32[]{:S(2)}, u32[]{:S(2)}) %all-to-all-start.3) | async-done | bytes 262176 | tf_op jit(solution)/shard_map/while/body/eval_jaxpr/all_to_all | solution.py:16
  654.3 8.5 %all_to_all.57 = f32[8,8,512]{2,1,0:T(8,128)S(1)} all-to-all(f32[8,8,512]{2,1,0:T(8,128)S(1)} %broadcast_in_dim.240), channel_id=1, replica_groups=mesh['row_0'=4,'row_1'=4,'col_0'=4,'col_1'=2] {'col_0','col_1'}, dimensions={0} | all-to-all | bytes 262144 | tf_op jit(solution)/shard_map/while/body/eval_jaxpr/all_to_all | solution.py:16
  667.2 8.5 %all-to-all-done.3 = f32[16,8,512]{2,1,0:T(8,128)S(1)} async-done(((f32[16,8,512]{2,1,0:T(8,128)}), f32[16,8,512]{2,1,0:T(8,128)S(1)}, u32[]{:S(2)}, u32[]{:S(2)}) %all-to-all-start.3) | async-done | bytes 262176 | tf_op jit(solution)/shard_map/while/body/eval_jaxpr/all_to_all | solution.py:16
  680.3 8.5 %all_to_all.57 = f32[8,8,512]{2,1,0:T(8,128)S(1)} all-to-all(f32[8,8,512]{2,1,0:T(8,128)S(1)} %broadcast_in_dim.240), channel_id=1, replica_groups=mesh['row_0'=4,'row_1'=4,'col_0'=4,'col_1'=2] {'col_0','col_1'}, dimensions={0} | all-to-all | bytes 262144 | tf_op jit(solution)/shard_map/while/body/eval_jaxpr/all_to_all | solution.py:16
  693.2 8.5 %all-to-all-done.3 = f32[16,8,512]{2,1,0:T(8,128)S(1)} async-done(((f32[16,8,512]{2,1,0:T(8,128)}), f32[16,8,512]{2,1,0:T(8,128)S(1)}, u32[]{:S(2)}, u32[]{:S(2)}) %all-to-all-start.3) | async-done | bytes 262176 | tf_op jit(solution)/shard_map/while/body/eval_jaxpr/all_to_all | solution.py:16
  719.2 8.5 %all-to-all-done.3 = f32[16,8,512]{2,1,0:T(8,128)S(1)} async-done(((f32[16,8,512]{2,1,0:T(8,128)}), f32[16,8,512]{2,1,0:T(8,128)S(1)}, u32[]{:S(2)}, u32[]{:S(2)}) %all-to-all-start.3) | async-done | bytes 262176 | tf_op jit(solution)/shard_map/while/body/eval_jaxpr/all_to_all | solution.py:16
  732.4 8.5 %all_to_all.57 = f32[8,8,512]{2,1,0:T(8,128)S(1)} all-to-all(f32[8,8,512]{2,1,0:T(8,128)S(1)} %broadcast_in_dim.240), channel_id=1, replica_groups=mesh['row_0'=4,'row_1'=4,'col_0'=4,'col_1'=2] {'col_0','col_1'}, dimensions={0} | all-to-all | bytes 262144 | tf_op jit(solution)/shard_map/while/body/eval_jaxpr/all_to_all | solution.py:16
  745.3 8.5 %all-to-all-done.3 = f32[16,8,512]{2,1,0:T(8,128)S(1)} async-done(((f32[16,8,512]{2,1,0:T(8,128)}), f32[16,8,512]{2,1,0:T(8,128)S(1)}, u32[]{:S(2)}, u32[]{:S(2)}) %all-to-all-start.3) | async-done | bytes 262176 | tf_op jit(solution)/shard_map/while/body/eval_jaxpr/all_to_all | solution.py:16
  758.4 8.5 %all_to_all.57 = f32[8,8,512]{2,1,0:T(8,128)S(1)} all-to-all(f32[8,8,512]{2,1,0:T(8,128)S(1)} %broadcast_in_dim.240), channel_id=1, replica_groups=mesh['row_0'=4,'row_1'=4,'col_0'=4,'col_1'=2] {'col_0','col_1'}, dimensions={0} | all-to-all | bytes 262144 | tf_op jit(solution)/shard_map/while/body/eval_jaxpr/all_to_all | solution.py:16
  771.3 8.5 %all-to-all-done.3 = f32[16,8,512]{2,1,0:T(8,128)S(1)} async-done(((f32[16,8,512]{2,1,0:T(8,128)}), f32[16,8,512]{2,1,0:T(8,128)S(1)}, u32[]{:S(2)}, u32[]{:S(2)}) %all-to-all-start.3) | async-done | bytes 262176 | tf_op jit(solution)/shard_map/while/body/eval_jaxpr/all_to_all | solution.py:16
  797.3 8.5 %all-to-all-done.3 = f32[16,8,512]{2,1,0:T(8,128)S(1)} async-done(((f32[16,8,512]{2,1,0:T(8,128)}), f32[16,8,512]{2,1,0:T(8,128)S(1)}, u32[]{:S(2)}, u32[]{:S(2)}) %all-to-all-start.3) | async-done | bytes 262176 | tf_op jit(solution)/shard_map/while/body/eval_jaxpr/all_to_all | solution.py:16
  810.5 8.5 %all_to_all.57 = f32[8,8,512]{2,1,0:T(8,128)S(1)} all-to-all(f32[8,8,512]{2,1,0:T(8,128)S(1)} %broadcast_in_dim.240), channel_id=1, replica_groups=mesh['row_0'=4,'row_1'=4,'col_0'=4,'col_1'=2] {'col_0','col_1'}, dimensions={0} | all-to-all | bytes 262144 | tf_op jit(solution)/shard_map/while/body/eval_jaxpr/all_to_all | solution.py:16
  823.4 8.5 %all-to-all-done.3 = f32[16,8,512]{2,1,0:T(8,128)S(1)} async-done(((f32[16,8,512]{2,1,0:T(8,128)}), f32[16,8,512]{2,1,0:T(8,128)S(1)}, u32[]{:S(2)}, u32[]{:S(2)}) %all-to-all-start.3) | async-done | bytes 262176 | tf_op jit(solution)/shard_map/while/body/eval_jaxpr/all_to_all | solution.py:16
  (355 shorter events, 304.5 us)
Async XLA Ops:
  0.6 833.1 %copy-start = (bf16[1,512,512]{2,1,0:T(8,128)(2,1)S(1)}, bf16[1,512,512]{2,1,0:T(8,128)(2,1)}, u32[]{:S(2)}) copy-start(bf16[1,512,512]{2,1,0:T(8,128)(2,1)} %param.20) | copy-start | bytes 1572868
  18.6 16.6 %all-to-all-start.1 = ((f32[16,8,512]{2,1,0:T(8,128)}), f32[16,8,512]{2,1,0:T(8,128)S(1)}, u32[]{:S(2)}, u32[]{:S(2)}) async-start(f32[16,8,512]{2,1,0:T(8,128)} %broadcast_in_dim.237), calls=%async_computation.1 | async-start | bytes 524288 | tf_op jit(solution)/shard_map/while/body/eval_jaxpr/all_to_all | solution.py:16
  48.3 12.1 %all-to-all-start.1 = ((f32[16,8,512]{2,1,0:T(8,128)}), f32[16,8,512]{2,1,0:T(8,128)S(1)}, u32[]{:S(2)}, u32[]{:S(2)}) async-start(f32[16,8,512]{2,1,0:T(8,128)} %broadcast_in_dim.237), calls=%async_computation.1 | async-start | bytes 524288 | tf_op jit(solution)/shard_map/while/body/eval_jaxpr/all_to_all | solution.py:16
  73.7 12.1 %all-to-all-start.1 = ((f32[16,8,512]{2,1,0:T(8,128)}), f32[16,8,512]{2,1,0:T(8,128)S(1)}, u32[]{:S(2)}, u32[]{:S(2)}) async-start(f32[16,8,512]{2,1,0:T(8,128)} %broadcast_in_dim.237), calls=%async_computation.1 | async-start | bytes 524288 | tf_op jit(solution)/shard_map/while/body/eval_jaxpr/all_to_all | solution.py:16
  99.0 12.1 %all-to-all-start.1 = ((f32[16,8,512]{2,1,0:T(8,128)}), f32[16,8,512]{2,1,0:T(8,128)S(1)}, u32[]{:S(2)}, u32[]{:S(2)}) async-start(f32[16,8,512]{2,1,0:T(8,128)} %broadcast_in_dim.237), calls=%async_computation.1 | async-start | bytes 524288 | tf_op jit(solution)/shard_map/while/body/eval_jaxpr/all_to_all | solution.py:16
  124.3 12.1 %all-to-all-start.1 = ((f32[16,8,512]{2,1,0:T(8,128)}), f32[16,8,512]{2,1,0:T(8,128)S(1)}, u32[]{:S(2)}, u32[]{:S(2)}) async-start(f32[16,8,512]{2,1,0:T(8,128)} %broadcast_in_dim.237), calls=%async_computation.1 | async-start | bytes 524288 | tf_op jit(solution)/shard_map/while/body/eval_jaxpr/all_to_all | solution.py:16
  149.7 12.1 %all-to-all-start.1 = ((f32[16,8,512]{2,1,0:T(8,128)}), f32[16,8,512]{2,1,0:T(8,128)S(1)}, u32[]{:S(2)}, u32[]{:S(2)}) async-start(f32[16,8,512]{2,1,0:T(8,128)} %broadcast_in_dim.237), calls=%async_computation.1 | async-start | bytes 524288 | tf_op jit(solution)/shard_map/while/body/eval_jaxpr/all_to_all | solution.py:16
  175.0 12.1 %all-to-all-start.1 = ((f32[16,8,512]{2,1,0:T(8,128)}), f32[16,8,512]{2,1,0:T(8,128)S(1)}, u32[]{:S(2)}, u32[]{:S(2)}) async-start(f32[16,8,512]{2,1,0:T(8,128)} %broadcast_in_dim.237), calls=%async_computation.1 | async-start | bytes 524288 | tf_op jit(solution)/shard_map/while/body/eval_jaxpr/all_to_all | solution.py:16
  200.4 12.1 %all-to-all-start.1 = ((f32[16,8,512]{2,1,0:T(8,128)}), f32[16,8,512]{2,1,0:T(8,128)S(1)}, u32[]{:S(2)}, u32[]{:S(2)}) async-start(f32[16,8,512]{2,1,0:T(8,128)} %broadcast_in_dim.237), calls=%async_computation.1 | async-start | bytes 524288 | tf_op jit(solution)/shard_map/while/body/eval_jaxpr/all_to_all | solution.py:16
  225.7 12.1 %all-to-all-start.1 = ((f32[16,8,512]{2,1,0:T(8,128)}), f32[16,8,512]{2,1,0:T(8,128)S(1)}, u32[]{:S(2)}, u32[]{:S(2)}) async-start(f32[16,8,512]{2,1,0:T(8,128)} %broadcast_in_dim.237), calls=%async_computation.1 | async-start | bytes 524288 | tf_op jit(solution)/shard_map/while/body/eval_jaxpr/all_to_all | solution.py:16
  251.1 12.1 %all-to-all-start.1 = ((f32[16,8,512]{2,1,0:T(8,128)}), f32[16,8,512]{2,1,0:T(8,128)S(1)}, u32[]{:S(2)}, u32[]{:S(2)}) async-start(f32[16,8,512]{2,1,0:T(8,128)} %broadcast_in_dim.237), calls=%async_computation.1 | async-start | bytes 524288 | tf_op jit(solution)/shard_map/while/body/eval_jaxpr/all_to_all | solution.py:16
  276.4 12.1 %all-to-all-start.1 = ((f32[16,8,512]{2,1,0:T(8,128)}), f32[16,8,512]{2,1,0:T(8,128)S(1)}, u32[]{:S(2)}, u32[]{:S(2)}) async-start(f32[16,8,512]{2,1,0:T(8,128)} %broadcast_in_dim.237), calls=%async_computation.1 | async-start | bytes 524288 | tf_op jit(solution)/shard_map/while/body/eval_jaxpr/all_to_all | solution.py:16
  301.8 12.1 %all-to-all-start.1 = ((f32[16,8,512]{2,1,0:T(8,128)}), f32[16,8,512]{2,1,0:T(8,128)S(1)}, u32[]{:S(2)}, u32[]{:S(2)}) async-start(f32[16,8,512]{2,1,0:T(8,128)} %broadcast_in_dim.237), calls=%async_computation.1 | async-start | bytes 524288 | tf_op jit(solution)/shard_map/while/body/eval_jaxpr/all_to_all | solution.py:16
  327.1 12.1 %all-to-all-start.1 = ((f32[16,8,512]{2,1,0:T(8,128)}), f32[16,8,512]{2,1,0:T(8,128)S(1)}, u32[]{:S(2)}, u32[]{:S(2)}) async-start(f32[16,8,512]{2,1,0:T(8,128)} %broadcast_in_dim.237), calls=%async_computation.1 | async-start | bytes 524288 | tf_op jit(solution)/shard_map/while/body/eval_jaxpr/all_to_all | solution.py:16
  352.4 12.1 %all-to-all-start.1 = ((f32[16,8,512]{2,1,0:T(8,128)}), f32[16,8,512]{2,1,0:T(8,128)S(1)}, u32[]{:S(2)}, u32[]{:S(2)}) async-start(f32[16,8,512]{2,1,0:T(8,128)} %broadcast_in_dim.237), calls=%async_computation.1 | async-start | bytes 524288 | tf_op jit(solution)/shard_map/while/body/eval_jaxpr/all_to_all | solution.py:16
  377.8 12.1 %all-to-all-start.1 = ((f32[16,8,512]{2,1,0:T(8,128)}), f32[16,8,512]{2,1,0:T(8,128)S(1)}, u32[]{:S(2)}, u32[]{:S(2)}) async-start(f32[16,8,512]{2,1,0:T(8,128)} %broadcast_in_dim.237), calls=%async_computation.1 | async-start | bytes 524288 | tf_op jit(solution)/shard_map/while/body/eval_jaxpr/all_to_all | solution.py:16
  403.1 12.1 %all-to-all-start.1 = ((f32[16,8,512]{2,1,0:T(8,128)}), f32[16,8,512]{2,1,0:T(8,128)S(1)}, u32[]{:S(2)}, u32[]{:S(2)}) async-start(f32[16,8,512]{2,1,0:T(8,128)} %broadcast_in_dim.237), calls=%async_computation.1 | async-start | bytes 524288 | tf_op jit(solution)/shard_map/while/body/eval_jaxpr/all_to_all | solution.py:16
  416.5 417.2 %copy-start.1 = (bf16[1,512,1024]{2,1,0:T(8,128)(2,1)S(1)}, bf16[1,512,1024]{2,1,0:T(8,128)(2,1)}, u32[]{:S(2)}) copy-start(bf16[1,512,1024]{2,1,0:T(8,128)(2,1)} %param.19) | copy-start | bytes 3145732
  416.5 417.2 %copy-start.2 = (bf16[1,8,512]{2,1,0:T(8,128)(2,1)S(1)}, bf16[1,8,512]{2,1,0:T(8,128)(2,1)}, u32[]{:S(2)}) copy-start(bf16[1,8,512]{2,1,0:T(8,128)(2,1)} %param.18) | copy-start | bytes 24580
  429.3 12.1 %all-to-all-start.3 = ((f32[16,8,512]{2,1,0:T(8,128)}), f32[16,8,512]{2,1,0:T(8,128)S(1)}, u32[]{:S(2)}, u32[]{:S(2)}) async-start(f32[16,8,512]{2,1,0:T(8,128)} %broadcast_in_dim.241), calls=%async_computation.3 | async-start | bytes 524288 | tf_op jit(solution)/shard_map/while/body/eval_jaxpr/all_to_all | solution.py:16
  455.3 12.1 %all-to-all-start.3 = ((f32[16,8,512]{2,1,0:T(8,128)}), f32[16,8,512]{2,1,0:T(8,128)S(1)}, u32[]{:S(2)}, u32[]{:S(2)}) async-start(f32[16,8,512]{2,1,0:T(8,128)} %broadcast_in_dim.241), calls=%async_computation.3 | async-start | bytes 524288 | tf_op jit(solution)/shard_map/while/body/eval_jaxpr/all_to_all | solution.py:16
  481.3 12.1 %all-to-all-start.3 = ((f32[16,8,512]{2,1,0:T(8,128)}), f32[16,8,512]{2,1,0:T(8,128)S(1)}, u32[]{:S(2)}, u32[]{:S(2)}) async-start(f32[16,8,512]{2,1,0:T(8,128)} %broadcast_in_dim.241), calls=%async_computation.3 | async-start | bytes 524288 | tf_op jit(solution)/shard_map/while/body/eval_jaxpr/all_to_all | solution.py:16
  507.4 12.1 %all-to-all-start.3 = ((f32[16,8,512]{2,1,0:T(8,128)}), f32[16,8,512]{2,1,0:T(8,128)S(1)}, u32[]{:S(2)}, u32[]{:S(2)}) async-start(f32[16,8,512]{2,1,0:T(8,128)} %broadcast_in_dim.241), calls=%async_computation.3 | async-start | bytes 524288 | tf_op jit(solution)/shard_map/while/body/eval_jaxpr/all_to_all | solution.py:16
  533.4 12.1 %all-to-all-start.3 = ((f32[16,8,512]{2,1,0:T(8,128)}), f32[16,8,512]{2,1,0:T(8,128)S(1)}, u32[]{:S(2)}, u32[]{:S(2)}) async-start(f32[16,8,512]{2,1,0:T(8,128)} %broadcast_in_dim.241), calls=%async_computation.3 | async-start | bytes 524288 | tf_op jit(solution)/shard_map/while/body/eval_jaxpr/all_to_all | solution.py:16
  559.4 12.1 %all-to-all-start.3 = ((f32[16,8,512]{2,1,0:T(8,128)}), f32[16,8,512]{2,1,0:T(8,128)S(1)}, u32[]{:S(2)}, u32[]{:S(2)}) async-start(f32[16,8,512]{2,1,0:T(8,128)} %broadcast_in_dim.241), calls=%async_computation.3 | async-start | bytes 524288 | tf_op jit(solution)/shard_map/while/body/eval_jaxpr/all_to_all | solution.py:16
  585.4 12.1 %all-to-all-start.3 = ((f32[16,8,512]{2,1,0:T(8,128)}), f32[16,8,512]{2,1,0:T(8,128)S(1)}, u32[]{:S(2)}, u32[]{:S(2)}) async-start(f32[16,8,512]{2,1,0:T(8,128)} %broadcast_in_dim.241), calls=%async_computation.3 | async-start | bytes 524288 | tf_op jit(solution)/shard_map/while/body/eval_jaxpr/all_to_all | solution.py:16
  611.5 12.1 %all-to-all-start.3 = ((f32[16,8,512]{2,1,0:T(8,128)}), f32[16,8,512]{2,1,0:T(8,128)S(1)}, u32[]{:S(2)}, u32[]{:S(2)}) async-start(f32[16,8,512]{2,1,0:T(8,128)} %broadcast_in_dim.241), calls=%async_computation.3 | async-start | bytes 524288 | tf_op jit(solution)/shard_map/while/body/eval_jaxpr/all_to_all | solution.py:16
  637.5 12.1 %all-to-all-start.3 = ((f32[16,8,512]{2,1,0:T(8,128)}), f32[16,8,512]{2,1,0:T(8,128)S(1)}, u32[]{:S(2)}, u32[]{:S(2)}) async-start(f32[16,8,512]{2,1,0:T(8,128)} %broadcast_in_dim.241), calls=%async_computation.3 | async-start | bytes 524288 | tf_op jit(solution)/shard_map/while/body/eval_jaxpr/all_to_all | solution.py:16
  663.5 12.1 %all-to-all-start.3 = ((f32[16,8,512]{2,1,0:T(8,128)}), f32[16,8,512]{2,1,0:T(8,128)S(1)}, u32[]{:S(2)}, u32[]{:S(2)}) async-start(f32[16,8,512]{2,1,0:T(8,128)} %broadcast_in_dim.241), calls=%async_computation.3 | async-start | bytes 524288 | tf_op jit(solution)/shard_map/while/body/eval_jaxpr/all_to_all | solution.py:16
  689.6 12.1 %all-to-all-start.3 = ((f32[16,8,512]{2,1,0:T(8,128)}), f32[16,8,512]{2,1,0:T(8,128)S(1)}, u32[]{:S(2)}, u32[]{:S(2)}) async-start(f32[16,8,512]{2,1,0:T(8,128)} %broadcast_in_dim.241), calls=%async_computation.3 | async-start | bytes 524288 | tf_op jit(solution)/shard_map/while/body/eval_jaxpr/all_to_all | solution.py:16
  715.6 12.1 %all-to-all-start.3 = ((f32[16,8,512]{2,1,0:T(8,128)}), f32[16,8,512]{2,1,0:T(8,128)S(1)}, u32[]{:S(2)}, u32[]{:S(2)}) async-start(f32[16,8,512]{2,1,0:T(8,128)} %broadcast_in_dim.241), calls=%async_computation.3 | async-start | bytes 524288 | tf_op jit(solution)/shard_map/while/body/eval_jaxpr/all_to_all | solution.py:16
  741.6 12.1 %all-to-all-start.3 = ((f32[16,8,512]{2,1,0:T(8,128)}), f32[16,8,512]{2,1,0:T(8,128)S(1)}, u32[]{:S(2)}, u32[]{:S(2)}) async-start(f32[16,8,512]{2,1,0:T(8,128)} %broadcast_in_dim.241), calls=%async_computation.3 | async-start | bytes 524288 | tf_op jit(solution)/shard_map/while/body/eval_jaxpr/all_to_all | solution.py:16
  767.7 12.1 %all-to-all-start.3 = ((f32[16,8,512]{2,1,0:T(8,128)}), f32[16,8,512]{2,1,0:T(8,128)S(1)}, u32[]{:S(2)}, u32[]{:S(2)}) async-start(f32[16,8,512]{2,1,0:T(8,128)} %broadcast_in_dim.241), calls=%async_computation.3 | async-start | bytes 524288 | tf_op jit(solution)/shard_map/while/body/eval_jaxpr/all_to_all | solution.py:16
  793.7 12.1 %all-to-all-start.3 = ((f32[16,8,512]{2,1,0:T(8,128)}), f32[16,8,512]{2,1,0:T(8,128)S(1)}, u32[]{:S(2)}, u32[]{:S(2)}) async-start(f32[16,8,512]{2,1,0:T(8,128)} %broadcast_in_dim.241), calls=%async_computation.3 | async-start | bytes 524288 | tf_op jit(solution)/shard_map/while/body/eval_jaxpr/all_to_all | solution.py:16
  819.7 12.1 %all-to-all-start.3 = ((f32[16,8,512]{2,1,0:T(8,128)}), f32[16,8,512]{2,1,0:T(8,128)S(1)}, u32[]{:S(2)}, u32[]{:S(2)}) async-start(f32[16,8,512]{2,1,0:T(8,128)} %broadcast_in_dim.241), calls=%async_computation.3 | async-start | bytes 524288 | tf_op jit(solution)/shard_map/while/body/eval_jaxpr/all_to_all | solution.py:16
where the time goes:
time: 842 us; the launch traced here: 836 us
  blocking collectives  273 us (32%)
  waiting for transfers between devices  272 us (32%)
  starting transfers between devices  120 us (14%)
  matrix products  84 us (10%)
  local copies, waits for them, and re-layouts  57 us (7%)
  other arithmetic  26 us (3%)
    all_to_all x32, blocking collectives, copy_for_each(): return lax.all_to_all(copies, axis, split_axis=0, concat_axis=0, tiled=True)  273 us
    all_to_all x32, waiting for transfers between devices, copy_for_each(): return lax.all_to_all(copies, axis, split_axis=0, concat_axis=0, tiled=True)  272 us
    all_to_all x32, starting transfers between devices, copy_for_each(): return lax.all_to_all(copies, axis, split_axis=0, concat_axis=0, tiled=True)  120 us
    broadcast_in_dim x64, local copies, waits for them, and re-layouts, copy_for_each(): copies = jnp.broadcast_to(array, (lax.axis_size(axis), *array.shape))  23.9 us
    dynamic_slice x16, local copies, waits for them, and re-layouts, backward(): lax.dynamic_index_in_dim(tile_ranks, owner_slot, 1, keepdims=False)  21.4 us
    dot_general x16, matrix products, forward(): jnp.einsum('rbq,bqt->rt', coefficient_values, left_row_index, preferred_e...  21.3 us
    dot_general x16, matrix products, backward(): fresh = jnp.dot(block_solved - col_total, inverse.T)  20.4 us
    dot_general x16, matrix products, backward(): jnp.einsum('raq,atq->rt', coefficient_values, right_col, preferred_elemen...  20.4 us
  transfers between devices with their start and end apart: 32, of which 32 were waited for; matrix products, arithmetic and copies ran while one was open for 0% of the time, Pallas kernels for 0%

commit v1 on v0

v1 whole, which is shorter than its diff:
```python
import functools

import jax
import jax.numpy as jnp
from jax import lax
from jax.experimental import pallas as pl
from jax.experimental.layout import Layout, with_layout_constraint
from jax.experimental.pallas import tpu as pltpu
from jax.sharding import Mesh
from jax.sharding import PartitionSpec as P

BLK = 128
BB = 8
ROW = ("y", "z")
COL = ("x", "c")
ALL = ("y", "z", "x", "c")
HALF = 8
BF = jnp.bfloat16
F32 = jnp.float32
ROWS = Layout((0, 1))


def copies(v, axis):
    n = lax.axis_size(axis)
    stacked = jnp.broadcast_to(v, (n, *v.shape))
    return lax.all_to_all(stacked, axis, split_axis=0, concat_axis=0, tiled=True)


def dot_nn(a, b):
    return lax.dot_general(a, b, (((1,), (0,)), ((), ())), preferred_element_type=F32)


def dot_nt(a, b):
    return lax.dot_general(a, b, (((1,), (1,)), ((), ())), preferred_element_type=F32)


def exact(dot, a, b):
    high = a.astype(BF)
    low = (a - high.astype(F32)).astype(BF)
    both = dot(jnp.concatenate([high, low], axis=0), b)
    n = a.shape[0]
    return both[:n] + both[n:]


def first_tile(row):
    return row * (row - 1) // 2


class Leaf:
    def __init__(self, half, tiles, inv, left, right, diag, sems, dsems, order):
        self.left, self.right, self.diag = left, right, diag
        self.copies = {}
        for n in order:
            items = [pltpu.make_async_copy(inv.at[HALF * half + n], diag.at[n], dsems.at[n])]
            if n:
                base = first_tile(n)
                at = 64 * half + 8 * n
                mirrored = 64 * half + 8 * (7 - n) + 8 - n
                items.append(
                    pltpu.make_async_copy(
                        tiles.at[pl.ds(at, n)], left.at[pl.ds(base, n)], sems.at[0, n]
                    )
                )
                items.append(
                    pltpu.make_async_copy(
                        tiles.at[pl.ds(mirrored, n)], right.at[pl.ds(base, n)], sems.at[1, n]
                    )
                )
            self.copies[n] = items
        for n in order:
            for item in self.copies[n]:
                item.start()

    def wait(self, n):
        for item in self.copies[n]:
            item.wait()

    def u(self, i, k):
        return self.left[first_tile(i) + k].astype(BF)

    def vt(self, i, k):
        return self.right[first_tile(i) + i - 1 - k].astype(BF)


def forward(leaf, rhs_ref, wait=True):
    solved = []
    narrow = []
    for i in range(HALF):
        if wait:
            leaf.wait(i)
        acc = rhs_ref[i]
        for k in range(i):
            p = dot_nt(narrow[k], leaf.vt(i, k)).astype(BF)
            acc = acc - dot_nn(p, leaf.u(i, k))
        x = exact(dot_nn, acc, leaf.diag[i])
        solved.append(x)
        narrow.append(x.astype(BF))
    return solved


def backward(leaf, rhs, wait):
    solved = {}
    narrow = {}
    for j in reversed(range(HALF)):
        if wait:
            leaf.wait(j)
        acc = rhs[j]
        for i in reversed(range(j + 1, HALF)):
            q = dot_nt(narrow[i], leaf.u(i, j)).astype(BF)
            acc = acc - dot_nn(q, leaf.vt(i, j))
        z = exact(dot_nt, acc, leaf.diag[j])
        solved[j] = z
        narrow[j] = z.astype(BF)
    return solved


def forward_kernel(half, tiles, inv, rhs, out, left, right, diag, sems, dsems):
    leaf = Leaf(half, tiles, inv, left, right, diag, sems, dsems, range(HALF))
    for i, x in enumerate(forward(leaf, rhs)):
        out[i] = x


def both_kernel(half, tiles, inv, rhs, out, left, right, diag, sems, dsems):
    leaf = Leaf(half, tiles, inv, left, right, diag, sems, dsems, range(HALF))
    solved = forward(leaf, rhs)
    for j, z in backward(leaf, solved, False).items():
        out[j] = z


def backward_kernel(half, tiles, inv, rhs, out, left, right, diag, sems, dsems):
    leaf = Leaf(half, tiles, inv, left, right, diag, sems, dsems, range(HALF)[::-1])
    for j, z in backward(leaf, [rhs[j] for j in range(HALF)], True).items():
        out[j] = z


def in_hbm(v):
    return pltpu.with_memory_space_constraint(v, pltpu.HBM)


def leaf_call(body, half, tiles, inv, rhs):
    count = first_tile(HALF)
    shape = tiles.shape[1:]
    tile = inv.shape[1]
    return pl.pallas_call(
        functools.partial(body, half),
        out_shape=jax.ShapeDtypeStruct(rhs.shape, F32),
        in_specs=[
            pl.BlockSpec(memory_space=pltpu.HBM),
            pl.BlockSpec(memory_space=pltpu.HBM),
            pl.BlockSpec(memory_space=pltpu.VMEM),
        ],
        out_specs=pl.BlockSpec(memory_space=pltpu.VMEM),
        scratch_shapes=[
            pltpu.VMEM((count, *shape), F32),
            pltpu.VMEM((count, *shape), F32),
            pltpu.VMEM((HALF, tile, tile), BF),
            pltpu.SemaphoreType.DMA((2, HALF)),
            pltpu.SemaphoreType.DMA((HALF,)),
        ],
        compiler_params=pltpu.CompilerParams(vmem_limit_bytes=40 * 1024 * 1024),
    )(in_hbm(tiles), in_hbm(inv), rhs)


def per_device(
    root_rhs, diag_inv, tile_u, tile_v, tile_rank, child_x, border_t, child_inv, child_blocks
):
    my_row = lax.axis_index(ROW)
    my_col = lax.axis_index(COL)
    ntile = diag_inv.shape[0]
    tile = diag_inv.shape[1]
    rhs_count = root_rhs.shape[0]
    rank_max = tile_u.shape[4]
    n_child = child_x.shape[0]
    nblk = ntile * tile // BLK
    ndev = lax.axis_size(ALL)
    upper = my_row >= HALF
    in_half = my_row % HALF

    left = tile_u[0, 0, 0]
    live = jnp.arange(rank_max)[None, None, :] < tile_rank[0, 0, 0][:, None, None]
    right = jnp.where(live, tile_v[0, 0, 0].astype(F32), 0.0)

    has_leaf = my_col < in_half
    leaf_u = jnp.where(upper, left[1], left[0]).astype(F32)
    leaf_vt = jnp.where(upper, right[1], right[0]).T
    pairs = []
    for r in range(16):
        for c in range(8):
            partner = (r // 8 * 8 + 7 - r % 8) * 8 + 7 - c
            pairs.append((r * 8 + c, partner))
    from_partner = lax.ppermute(with_layout_constraint(leaf_vt, ROWS), ALL, pairs)
    share = with_layout_constraint(jnp.where(has_leaf, leaf_u, from_partner), ROWS)
    tiles = lax.all_gather(share, ALL)

    upward = jnp.einsum("crs,csb->crb", child_x, border_t, preferred_element_type=F32)
    pieces = (
        upward.reshape(n_child, rhs_count, BB, BLK)
        .transpose(1, 0, 2, 3)
        .reshape(rhs_count, n_child * BB, BLK)
    )
    flat_blocks = child_blocks.reshape(-1)
    dense = jnp.zeros((rhs_count, nblk, BLK), F32).at[:, flat_blocks, :].add(pieces)
    width = ntile * tile // ndev
    parts = dense.reshape(rhs_count, ndev, width).transpose(1, 0, 2)
    mine = lax.all_to_all(parts, ALL, split_axis=0, concat_axis=0, tiled=True).sum(axis=0)
    child_sum = copies(mine, ALL).reshape(ndev, rhs_count, width)
    child_sum = child_sum.transpose(1, 0, 2).reshape(rhs_count, ntile, tile).transpose(1, 0, 2)
    rhs = root_rhs.reshape(rhs_count, ntile, tile).transpose(1, 0, 2).astype(F32) - child_sum

    x_low = leaf_call(forward_kernel, 0, tiles, diag_inv, rhs[:HALF])
    v0 = right[0].astype(BF)
    u0 = left[0]
    x_own = lax.dynamic_index_in_dim(x_low, my_col, 0, keepdims=False).astype(BF)
    p = dot_nn(x_own, v0).astype(BF)
    given = jnp.where(upper, dot_nn(p, u0), 0.0)
    row_sum = copies(given, COL).reshape(8, rhs_count, tile).sum(axis=0)
    row_sums = copies(row_sum, ROW).reshape(16, rhs_count, tile)
    z_high = leaf_call(both_kernel, 1, tiles, diag_inv, rhs[HALF:] - row_sums[HALF:])

    z_own = lax.dynamic_index_in_dim(z_high, in_half, 0, keepdims=False).astype(BF)
    q = dot_nt(z_own, u0).astype(BF)
    given = jnp.where(upper, dot_nt(q, v0), 0.0)
    col_sum = copies(given, ROW).reshape(16, rhs_count, tile)[HALF:].sum(axis=0)
    col_sums = copies(col_sum, COL).reshape(8, rhs_count, tile)
    z_low = leaf_call(backward_kernel, 0, tiles, diag_inv, x_low - col_sums)
    result = jnp.concatenate([z_low, z_high], axis=0).transpose(1, 0, 2)
    result = result.reshape(rhs_count, ntile * tile)

    start = (my_row * 8 + my_col) * width
    root_part = lax.dynamic_slice_in_dim(result, start, width, 1)
    gathered = result.reshape(rhs_count, nblk, BLK)[:, flat_blocks, :]
    gathered = gathered.reshape(rhs_count, n_child, BB * BLK).astype(BF)
    returned = jnp.einsum("rcb,csb->crs", gathered, border_t, preferred_element_type=F32)
    child_out = child_x.astype(F32) - jnp.einsum(
        "crs,cst->crt", returned, child_inv.astype(F32)
    )
    return (root_part, child_out)


def solution(mesh):
    finer = Mesh(mesh.devices.reshape(4, 4, 4, 2), ALL)
    in_specs = (
        P(),
        P(),
        P(ROW, COL, None, None, None, None),
        P(ROW, COL, None, None, None, None),
        P(ROW, COL, None, None),
        P(ALL, None, None),
        P(ALL, None, None),
        P(ALL, None, None),
        P(ALL, None),
    )
    out_specs = (P(None, ALL), P(ALL, None, None))
    return jax.shard_map(
        per_device, mesh=finer, in_specs=in_specs, out_specs=out_specs, check_vma=False
    )
```

time: 842 us -> 234 us (0.28)
  blocking collectives: 273 us -> 43.8 us
  waiting for transfers between devices: 272 us -> 95.9 us
  starting transfers between devices: 120 us -> 20.1 us
  matrix products: 84 us -> 2.76 us
  local copies, waits for them, and re-layouts: 57 us -> 8.36 us
  Pallas kernels: 0 us -> 39.5 us
  other arithmetic: 26 us -> 7.83 us
  between operations: 0.72 us -> 14.3 us
    all_to_all x32 -> x3, waiting for transfers between devices: 272 us -> 28.2 us  [copies(): lax.all_to_all(stacked, axis, split_axis=0, concat_axis=0, tiled=True)]
    all_to_all x32 -> x3, blocking collectives: 273 us -> 43.8 us  [the longest x2 22.1 us: copies(): lax.all_to_all(stacked, axis, split_axis=0, concat_axis=0, tiled=True)]
    all_to_all x32 -> x3, starting transfers between devices: 120 us -> 13.2 us  [copies(): lax.all_to_all(stacked, axis, split_axis=0, concat_axis=0, tiled=True)]
    dot_general x66 -> x4, matrix products: 84 us -> 2.76 us  [the longest x1 1.14 us: per_device(): jnp.einsum('crs,cst->crt', returned, child_inv.astype(F32))]
    all_gather x0 -> x1, waiting for transfers between devices: none -> 61 us  [per_device(): tiles = lax.all_gather(share, ALL)]
    pallas_call x0 -> x3, Pallas kernels: none -> 39.5 us  [leaf_call(): pl.pallas_call(functools.partial(body, half), out_shape=jax.ShapeDtypeStr...]
    and x48 -> x0, other arithmetic: 23.2 us -> none  [the longest x16 11.8 us: forward(): (rank_iota[None, :] < rank_row[:, None]) & (col_ids[:, None] < column)]
    broadcast_in_dim x65 -> x6, local copies, waits for them, and re-layouts: 24 us -> 1.55 us  [the longest x5 1.52 us: copies(): stacked = jnp.broadcast_to(v, (n, *v.shape))]
  transfers between devices with their start and end apart: 32 -> 5, of which waited for: 32 -> 5; matrix products, arithmetic and copies ran while one was open for 0% -> 5% of each run, Pallas kernels for 0% -> 0%
where the time goes in v1:
time: 234 us; the launch traced here: 233 us
  waiting for transfers between devices  95.9 us (41%)
  blocking collectives  43.8 us (19%)
  Pallas kernels  39.5 us (17%)
  starting transfers between devices  20.1 us (9%)
  between operations  14.3 us (6%)
  local copies, waits for them, and re-layouts  8.36 us (4%)
  other arithmetic  7.83 us (3%)
  matrix products  2.76 us (1%)
    all_gather x1, waiting for transfers between devices, per_device(): tiles = lax.all_gather(share, ALL)  61 us
    pallas_call x3, Pallas kernels, leaf_call(): pl.pallas_call(functools.partial(body, half), out_shape=jax.ShapeDtypeStr...  39.5 us
    all_to_all x3, waiting for transfers between devices, copies(): lax.all_to_all(stacked, axis, split_axis=0, concat_axis=0, tiled=True)  28.2 us
    all_to_all x2, blocking collectives, copies(): lax.all_to_all(stacked, axis, split_axis=0, concat_axis=0, tiled=True)  22.1 us
    all_to_all x1, blocking collectives, per_device(): lax.all_to_all(parts, ALL, split_axis=0, concat_axis=0, tiled=True)  21.8 us
    all_to_all x3, starting transfers between devices, copies(): lax.all_to_all(stacked, axis, split_axis=0, concat_axis=0, tiled=True)  13.2 us
    ppermute x1, starting transfers between devices, per_device(): lax.ppermute(with_layout_constraint(leaf_vt, ROWS), ALL, pairs)  6.88 us
    ppermute x1, waiting for transfers between devices, per_device(): lax.ppermute(with_layout_constraint(leaf_vt, ROWS), ALL, pairs)  6.7 us
  transfers between devices with their start and end apart: 5, of which 5 were waited for; matrix products, arithmetic and copies ran while one was open for 5% of the time, Pallas kernels for 0%

profile of v1, /device:TPU:0, one launch (start us, length us, event | category | flops | bytes accessed | tf_op | source)
XLA Modules:
  0.0 232.7 jit_solution(2864459414641434763)
XLA Ops:
  7.2 0.0 copy-start
  7.2 0.0 copy-start.2
  7.2 0.0 all-gather.3.cloned.1.call-start
  7.2 1.2 copy.27
  8.4 0.7 iota_compare_fusion
  9.1 0.1 convert_select_fusion
  9.3 6.9 %collective-permute-start = (f32[128,512]{1,0:T(8,128)S(1)}, f32[128,512]{1,0:T(8,128)S(1)}, u32[]{:S(2)}, u32[]{:S(2)}) collective-permute-start(f32[128,512]{1,0:T(8,128)S(1)} %fusion.12), channel_id=1, source_target_pairs={{0,63},{1,62},{2,61},{3,60},{4,59},{5,58},{6,57},{7,56},{8,55},{9,... | collective-permute-start | bytes 786440 | tf_op jit(solution)/shard_map/ppermute | solution.py:191
  16.2 6.7 %collective-permute-done = f32[128,512]{1,0:T(8,128)S(1)} collective-permute-done((f32[128,512]{1,0:T(8,128)S(1)}, f32[128,512]{1,0:T(8,128)S(1)}, u32[]{:S(2)}, u32[]{:S(2)}) %collective-permute-start) | collective-permute-done | bytes 262176 | tf_op jit(solution)/shard_map/ppermute | solution.py:191
  22.9 1.7 convert_select_fusion.1
  24.6 0.0 all-gather.3.cloned.1.call-update
  24.6 1.5 copy.35
  26.1 0.7 fusion.39
  26.8 1.1 convolution_bitcast_fusion
  27.9 0.8 scatter_fusion
  28.7 0.1 copy.29
  28.7 0.2 reshape.116
  28.9 0.3 copy.30
  29.2 0.3 reshape.140
  29.5 21.8 %all_to_all.30 = f32[128,1,512]{2,1,0:T(1,128)S(1)} all-to-all(f32[128,1,512]{2,1,0:T(1,128)S(1)} %reshape.140), channel_id=1, replica_groups=mesh['y'=4,'z'=4,'x'=4,'c'=2] {'y','z','x','c'}, dimensions={0} | all-to-all | bytes 524288 | tf_op jit(solution)/shard_map/all_to_all | solution.py:205
  51.3 0.5 broadcast.43
  51.8 1.3 reduce
  53.1 0.1 reshape.141
  53.2 0.1 reduce_sum.27
  53.4 1.0 reshape.142
  54.4 4.8 %all-to-all-start.1 = ((f32[128,1,512]{2,1,0:T(1,128)}), f32[128,1,512]{2,1,0:T(1,128)S(1)}, u32[]{:S(2)}, u32[]{:S(2)}) async-start(f32[128,1,512]{2,1,0:T(1,128)} %reshape.142), calls=%async_computation.1 | async-start | bytes 524288 | tf_op jit(solution)/shard_map/all_to_all | solution.py:26
  59.2 13.7 %all-to-all-done.1 = f32[128,1,512]{2,1,0:T(1,128)S(1)} async-done(((f32[128,1,512]{2,1,0:T(1,128)}), f32[128,1,512]{2,1,0:T(1,128)S(1)}, u32[]{:S(2)}, u32[]{:S(2)}) %all-to-all-start.1) | async-done | bytes 262176 | tf_op jit(solution)/shard_map/all_to_all | solution.py:26
  72.9 1.3 reduce.1
  74.1 0.1 reshape.143
  74.3 0.1 copy.31
  74.4 0.1 reshape.117
  74.5 1.1 fusion.13
  75.6 61.0 %all-gather.3.cloned.1.call-done = f32[16384,512]{1,0:T(8,128)} async-done(((f32[128,512]{1,0:T(8,128)}), f32[16384,512]{1,0:T(8,128)}) %all-gather.3.cloned.1.call-update) | async-done | bytes 33554448 | tf_op jit(solution)/shard_map/all_gather | solution.py:193
  136.6 10.1 %shard_map.104 = f32[8,8,512]{2,1,0:T(8,128)S(1)} custom-call(f32[128,128,512]{2,1,0:T(8,128)} %bitcast.75, bf16[16,512,512]{2,1,0:T(8,128)(2,1)} %inv.5, f32[8,8,512]{2,1,0:T(8,128)S(1)} %slice.40.rhs), custom_call_target="tpu_custom_call" | custom-call | tf_op jit(solution)/shard_map/pallas_call | solution.py:144
  146.8 0.0 copy-done.2
  146.8 0.3 convolution_select_fusion.1
  147.1 10.2 %all_to_all.31 = f32[8,8,512]{2,1,0:T(8,128)S(1)} all-to-all(f32[8,8,512]{2,1,0:T(8,128)S(1)} %broadcast_in_dim.43), channel_id=1, replica_groups=mesh['y'=4,'z'=4,'x'=4,'c'=2] {'x','c'}, dimensions={0} | all-to-all | bytes 262144 | tf_op jit(solution)/shard_map/all_to_all | solution.py:26
  157.3 0.7 broadcast_in_dim.44
  158.0 5.1 %all-to-all-start.3 = ((f32[16,8,512]{2,1,0:T(8,128)}), f32[16,8,512]{2,1,0:T(8,128)S(1)}, u32[]{:S(2)}, u32[]{:S(2)}) async-start(f32[16,8,512]{2,1,0:T(8,128)} %broadcast_in_dim.44), calls=%async_computation.3 | async-start | bytes 524288 | tf_op jit(solution)/shard_map/all_to_all | solution.py:26
  163.1 8.5 %all-to-all-done.3 = f32[16,8,512]{2,1,0:T(8,128)S(1)} async-done(((f32[16,8,512]{2,1,0:T(8,128)}), f32[16,8,512]{2,1,0:T(8,128)S(1)}, u32[]{:S(2)}, u32[]{:S(2)}) %all-to-all-start.3) | async-done | bytes 262176 | tf_op jit(solution)/shard_map/all_to_all | solution.py:26
  171.6 0.0 copy-start.1
  171.6 0.0 copy-start.3
  171.6 17.3 %shard_map.105 = f32[8,8,512]{2,1,0:T(8,128)S(1)} custom-call(f32[128,128,512]{2,1,0:T(8,128)} %bitcast.76, bf16[16,512,512]{2,1,0:T(8,128)(2,1)} %inv.5, f32[8,8,512]{2,1,0:T(8,128)S(1)} %slice_subtract_fusion.rhs), custom_call_target="tpu_custom_call" | custom-call | tf_op jit(solution)/shard_map/pallas_call | solution.py:144
  188.9 0.3 convolution_select_fusion
  189.2 0.1 broadcast_in_dim.45
  189.3 11.9 %all_to_all.32 = f32[16,8,512]{2,1,0:T(8,128)S(1)} all-to-all(f32[16,8,512]{2,1,0:T(8,128)S(1)} %broadcast_in_dim.45), channel_id=1, replica_groups=mesh['y'=4,'z'=4,'x'=4,'c'=2] {'y','z'}, dimensions={0} | all-to-all | bytes 524288 | tf_op jit(solution)/shard_map/all_to_all | solution.py:26
  201.2 0.7 broadcast_in_dim.46
  201.8 3.4 %all-to-all-start.5 = ((f32[8,8,512]{2,1,0:T(8,128)}), f32[8,8,512]{2,1,0:T(8,128)S(1)}, u32[]{:S(2)}, u32[]{:S(2)}) async-start(f32[8,8,512]{2,1,0:T(8,128)} %broadcast_in_dim.46), calls=%async_computation.5 | async-start | bytes 262144 | tf_op jit(solution)/shard_map/all_to_all | solution.py:26
  205.2 6.0 %all-to-all-done.5 = f32[8,8,512]{2,1,0:T(8,128)S(1)} async-done(((f32[8,8,512]{2,1,0:T(8,128)}), f32[8,8,512]{2,1,0:T(8,128)S(1)}, u32[]{:S(2)}, u32[]{:S(2)}) %all-to-all-start.5) | async-done | bytes 131104 | tf_op jit(solution)/shard_map/all_to_all | solution.py:26
  211.3 12.1 %shard_map.106 = f32[8,8,512]{2,1,0:T(8,128)S(1)} custom-call(f32[128,128,512]{2,1,0:T(8,128)} %bitcast.77, bf16[16,512,512]{2,1,0:T(8,128)(2,1)} %inv.5, f32[8,8,512]{2,1,0:T(8,128)S(1)} %sub.18.rhs), custom_call_target="tpu_custom_call" | custom-call | tf_op jit(solution)/shard_map/pallas_call | solution.py:144
  223.4 0.6 gather_fusion
  224.0 0.0 copy-done
  224.0 0.0 copy-done.1
  224.0 0.0 copy-done.3
  224.0 1.1 fusion.6
  225.2 0.7 constant_dynamic-slice_fusion
  (11 shorter events, 0.3 us)
Async XLA Ops:
  7.2 216.8 %copy-start = (bf16[1,512,512]{2,1,0:T(8,128)(2,1)S(1)}, bf16[1,512,512]{2,1,0:T(8,128)(2,1)}, u32[]{:S(2)}) copy-start(bf16[1,512,512]{2,1,0:T(8,128)(2,1)} %param.16) | copy-start | bytes 1572868
  7.2 139.6 %copy-start.2 = (bf16[1,1,1,2,128,512]{5,4,3,2,1,0:T(8,128)(2,1)S(1)}, bf16[1,1,1,2,128,512]{5,4,3,2,1,0:T(8,128)(2,1)}, u32[]{:S(2)}) copy-start(bf16[1,1,1,2,128,512]{5,4,3,2,1,0:T(8,128)(2,1)} %param.11) | copy-start | bytes 786436
  7.2 129.4 %all-gather.3.cloned.1.call-start = ((), (), s32[]{:S(2)}) async-start(), calls=%async_computation.6 | async-start | bytes 33816576 | tf_op jit(solution)/shard_map/all_gather | solution.py:193
  9.3 13.6 %collective-permute-start = (f32[128,512]{1,0:T(8,128)S(1)}, f32[128,512]{1,0:T(8,128)S(1)}, u32[]{:S(2)}, u32[]{:S(2)}) collective-permute-start(f32[128,512]{1,0:T(8,128)S(1)} %fusion.12), channel_id=1, source_target_pairs={{0,63},{1,62},{2,61},{3,60},{4,59},{5,58},{6,57},{7,56},{8,55},{9,... | collective-permute-start | bytes 786440 | tf_op jit(solution)/shard_map/ppermute | solution.py:191
  54.4 18.5 %all-to-all-start.1 = ((f32[128,1,512]{2,1,0:T(1,128)}), f32[128,1,512]{2,1,0:T(1,128)S(1)}, u32[]{:S(2)}, u32[]{:S(2)}) async-start(f32[128,1,512]{2,1,0:T(1,128)} %reshape.142), calls=%async_computation.1 | async-start | bytes 524288 | tf_op jit(solution)/shard_map/all_to_all | solution.py:26
  158.0 13.6 %all-to-all-start.3 = ((f32[16,8,512]{2,1,0:T(8,128)}), f32[16,8,512]{2,1,0:T(8,128)S(1)}, u32[]{:S(2)}, u32[]{:S(2)}) async-start(f32[16,8,512]{2,1,0:T(8,128)} %broadcast_in_dim.44), calls=%async_computation.3 | async-start | bytes 524288 | tf_op jit(solution)/shard_map/all_to_all | solution.py:26
  171.6 52.4 %copy-start.1 = (bf16[1,512,1024]{2,1,0:T(8,128)(2,1)S(1)}, bf16[1,512,1024]{2,1,0:T(8,128)(2,1)}, u32[]{:S(2)}) copy-start(bf16[1,512,1024]{2,1,0:T(8,128)(2,1)} %param.15) | copy-start | bytes 3145732
  171.6 52.4 %copy-start.3 = (bf16[1,8,512]{2,1,0:T(8,128)(2,1)S(1)}, bf16[1,8,512]{2,1,0:T(8,128)(2,1)}, u32[]{:S(2)}) copy-start(bf16[1,8,512]{2,1,0:T(8,128)(2,1)} %param.14) | copy-start | bytes 24580
  201.8 9.4 %all-to-all-start.5 = ((f32[8,8,512]{2,1,0:T(8,128)}), f32[8,8,512]{2,1,0:T(8,128)S(1)}, u32[]{:S(2)}, u32[]{:S(2)}) async-start(f32[8,8,512]{2,1,0:T(8,128)} %broadcast_in_dim.46), calls=%async_computation.5 | async-start | bytes 262144 | tf_op jit(solution)/shard_map/all_to_all | solution.py:26
Sparse Core Ops, SparseCore 0:
  24.7 111.8 all-gather.2

commit v2 on v1

--- a/solution.py
+++ b/solution.py
@@ -46,119 +46,157 @@
     return row * (row - 1) // 2
 
 
+SLOTS = 3
+
+
 class Leaf:
-    def __init__(self, half, tiles, inv, left, right, diag, sems, dsems, order):
-        self.left, self.right, self.diag = left, right, diag
-        self.copies = {}
-        for n in order:
-            items = [pltpu.make_async_copy(inv.at[HALF * half + n], diag.at[n], dsems.at[n])]
-            if n:
-                base = first_tile(n)
-                at = 64 * half + 8 * n
-                mirrored = 64 * half + 8 * (7 - n) + 8 - n
-                items.append(
-                    pltpu.make_async_copy(
-                        tiles.at[pl.ds(at, n)], left.at[pl.ds(base, n)], sems.at[0, n]
+    def __init__(self, rows, where, first, tiles, inv, stage, left, right, diag, sems, dsems):
+        self.rows, self.stage, self.left, self.right, self.diag = rows, stage, left, right, diag
+        self.inverse = [
+            pltpu.make_async_copy(inv.at[first + n], diag.at[n], dsems.at[n]) for n in range(rows)
+        ]
+        self.moves = {}
+        for i in range(rows):
+            self.moves[i] = []
+            for k in range(i):
+                for side in range(2):
+                    array, index = where(i, k)[side]
+                    self.moves[i].append(
+                        pltpu.make_async_copy(
+                            tiles[array].at[index],
+                            stage.at[i % SLOTS, k, side],
+                            sems.at[side, first_tile(i) + k],
+                        )
                     )
-                )
-                items.append(
-                    pltpu.make_async_copy(
-                        tiles.at[pl.ds(mirrored, n)], right.at[pl.ds(base, n)], sems.at[1, n]
-                    )
-                )
-            self.copies[n] = items
-        for n in order:
-            for item in self.copies[n]:
-                item.start()
-
-    def wait(self, n):
-        for item in self.copies[n]:
-            item.wait()
-
-    def u(self, i, k):
-        return self.left[first_tile(i) + k].astype(BF)
-
-    def vt(self, i, k):
-        return self.right[first_tile(i) + i - 1 - k].astype(BF)
-
-
-def forward(leaf, rhs_ref, wait=True):
-    solved = []
-    narrow = []
-    for i in range(HALF):
-        if wait:
-            leaf.wait(i)
-        acc = rhs_ref[i]
+
+    def start(self, i):
+        if 0 <= i < self.rows:
+            self.inverse[i].start()
+            for move in self.moves[i]:
+                move.start()
+
+    def column(self, j):
+        return sum(self.rows - 1 - m for m in range(j))
+
+    def load(self, i, step=1):
+        self.inverse[i].wait()
+        for move in self.moves[i]:
+            move.wait()
         for k in range(i):
-            p = dot_nt(narrow[k], leaf.vt(i, k)).astype(BF)
-            acc = acc - dot_nn(p, leaf.u(i, k))
+            self.left[first_tile(i) + k] = self.stage[i % SLOTS, k, 0].astype(BF)
+            self.right[self.column(k) + i - k - 1] = self.stage[i % SLOTS, k, 1].astype(BF)
+        self.start(i + step * SLOTS)
+
+    def u(self, i, k, count=1):
+        at = first_tile(i) + k
+        return self.left[at : at + count].reshape(-1, self.left.shape[2])
+
+    def vt(self, i, k, count=1):
+        at = self.column(k) + i - k - 1
+        return self.right[at : at + count].reshape(-1, self.right.shape[2])
+
+
+def forward(leaf, rhs):
+    solved, narrow = [], []
+    for i in range(min(SLOTS, leaf.rows)):
+        leaf.start(i)
+    leaf.load(0)
+    partial = rhs[0]
+    last = None
+    for i in range(leaf.rows):
+        acc = partial
+        if i:
+            acc = acc - dot_nn(last, leaf.u(i, i - 1))
         x = exact(dot_nn, acc, leaf.diag[i])
+        if i + 1 < leaf.rows:
+            leaf.load(i + 1)
+            partial = rhs[i + 1]
+            if i:
+                known = [dot_nt(narrow[k], leaf.vt(i + 1, k)).astype(BF) for k in range(i)]
+                partial = partial - dot_nn(jnp.concatenate(known, axis=1), leaf.u(i + 1, 0, i))
         solved.append(x)
         narrow.append(x.astype(BF))
+        if i + 1 < leaf.rows:
+            last = dot_nt(narrow[i], leaf.vt(i + 1, i)).astype(BF)
     return solved
 
 
-def backward(leaf, rhs, wait):
+def backward(leaf, rhs, load):
+    rows = leaf.rows
+    if load:
+        for i in range(min(SLOTS, rows)):
+            leaf.start(rows - 1 - i)
+        leaf.load(rows - 1, -1)
+    width = leaf.left.shape[1]
     solved = {}
-    narrow = {}
-    for j in reversed(range(HALF)):
-        if wait:
-            leaf.wait(j)
-        acc = rhs[j]
-        for i in reversed(range(j + 1, HALF)):
-            q = dot_nt(narrow[i], leaf.u(i, j)).astype(BF)
-            acc = acc - dot_nn(q, leaf.vt(i, j))
+    waiting = {j: [] for j in range(rows)}
+    partial = rhs[rows - 1]
+    last = None
+    for j in reversed(range(rows)):
+        acc = partial
+        if j + 1 < rows:
+            acc = acc - dot_nn(last, leaf.vt(j + 1, j))
         z = exact(dot_nt, acc, leaf.diag[j])
+        if j:
+            if load:
+                leaf.load(j - 1, -1)
+            partial = rhs[j - 1]
+            if waiting[j - 1]:
+                known = jnp.concatenate(waiting[j - 1][::-1], axis=1)
+                partial = partial - dot_nn(known, leaf.vt(j + 1, j - 1, rows - 1 - j))
         solved[j] = z
-        narrow[j] = z.astype(BF)
+        narrow = z.astype(BF)
+        if j:
+            last = dot_nt(narrow, leaf.u(j, j - 1)).astype(BF)
+        if j > 1:
+            others = dot_nt(narrow, leaf.u(j, 0, j - 1)).astype(BF)
+            for k in range(j - 1):
+                waiting[k].append(others[:, k * width : (k + 1) * width])
     return solved
 
 
-def forward_kernel(half, tiles, inv, rhs, out, left, right, diag, sems, dsems):
-    leaf = Leaf(half, tiles, inv, left, right, diag, sems, dsems, range(HALF))
-    for i, x in enumerate(forward(leaf, rhs)):
-        out[i] = x
-
-
-def both_kernel(half, tiles, inv, rhs, out, left, right, diag, sems, dsems):
-    leaf = Leaf(half, tiles, inv, left, right, diag, sems, dsems, range(HALF))
-    solved = forward(leaf, rhs)
-    for j, z in backward(leaf, solved, False).items():
-        out[j] = z
-
-
-def backward_kernel(half, tiles, inv, rhs, out, left, right, diag, sems, dsems):
-    leaf = Leaf(half, tiles, inv, left, right, diag, sems, dsems, range(HALF)[::-1])
-    for j, z in backward(leaf, [rhs[j] for j in range(HALF)], True).items():
-        out[j] = z
+def solve_kernel(rows, where, first, sweeps, narrays, *refs):
+    tiles = refs[:narrays]
+    inv, rhs, out, stage, left, right, diag, sems, dsems = refs[narrays:]
+    leaf = Leaf(rows, where, first, tiles, inv, stage, left, right, diag, sems, dsems)
+    values = [rhs[i] for i in range(rows)]
+    if sweeps != "backward":
+        values = forward(leaf, values)
+    if sweeps != "forward":
+        values = backward(leaf, values, sweeps == "backward")
+    for i in range(rows):
+        out[i] = values[i]
 
 
 def in_hbm(v):
     return pltpu.with_memory_space_constraint(v, pltpu.HBM)
 
 
-def leaf_call(body, half, tiles, inv, rhs):
-    count = first_tile(HALF)
-    shape = tiles.shape[1:]
+def solve(sweeps, rows, where, first, arrays, inv, rhs):
+    count = first_tile(rows)
+    shape = arrays[0].shape[1:]
     tile = inv.shape[1]
     return pl.pallas_call(
-        functools.partial(body, half),
+        functools.partial(solve_kernel, rows, where, first, sweeps, len(arrays)),
         out_shape=jax.ShapeDtypeStruct(rhs.shape, F32),
-        in_specs=[
-            pl.BlockSpec(memory_space=pltpu.HBM),
-            pl.BlockSpec(memory_space=pltpu.HBM),
-            pl.BlockSpec(memory_space=pltpu.VMEM),
-        ],
+        in_specs=[pl.BlockSpec(memory_space=pltpu.HBM)] * (len(arrays) + 1)
+        + [pl.BlockSpec(memory_space=pltpu.VMEM)],
         out_specs=pl.BlockSpec(memory_space=pltpu.VMEM),
         scratch_shapes=[
-            pltpu.VMEM((count, *shape), F32),
-            pltpu.VMEM((count, *shape), F32),
-            pltpu.VMEM((HALF, tile, tile), BF),
-            pltpu.SemaphoreType.DMA((2, HALF)),
-            pltpu.SemaphoreType.DMA((HALF,)),
+            pltpu.VMEM((SLOTS, rows - 1, 2, *shape), F32),
+            pltpu.VMEM((count, *shape), BF),
+            pltpu.VMEM((count, *shape), BF),
+            pltpu.VMEM((rows, tile, tile), BF),
+            pltpu.SemaphoreType.DMA((2, count)),
+            pltpu.SemaphoreType.DMA((rows,)),
         ],
-        compiler_params=pltpu.CompilerParams(vmem_limit_bytes=40 * 1024 * 1024),
-    )(in_hbm(tiles), in_hbm(inv), rhs)
+        compiler_params=pltpu.CompilerParams(vmem_limit_bytes=50 * 1024 * 1024),
+    )(*[in_hbm(v) for v in arrays], in_hbm(inv), rhs)
+
+
+def in_gathered(half, i, k):
+    at = 64 * half
+    return (0, at + 8 * i + k), (0, at + 8 * (7 - i) + 7 - k)
 
 
 def per_device(
@@ -207,7 +245,9 @@
     child_sum = child_sum.transpose(1, 0, 2).reshape(rhs_count, ntile, tile).transpose(1, 0, 2)
     rhs = root_rhs.reshape(rhs_count, ntile, tile).transpose(1, 0, 2).astype(F32) - child_sum
 
-    x_low = leaf_call(forward_kernel, 0, tiles, diag_inv, rhs[:HALF])
+    low = functools.partial(in_gathered, 0)
+    high = functools.partial(in_gathered, 1)
+    x_low = solve("forward", HALF, low, 0, [tiles], diag_inv, rhs[:HALF])
     v0 = right[0].astype(BF)
     u0 = left[0]
     x_own = lax.dynamic_index_in_dim(x_low, my_col, 0, keepdims=False).astype(BF)
@@ -215,14 +255,15 @@
     given = jnp.where(upper, dot_nn(p, u0), 0.0)
     row_sum = copies(given, COL).reshape(8, rhs_count, tile).sum(axis=0)
     row_sums = copies(row_sum, ROW).reshape(16, rhs_count, tile)
-    z_high = leaf_call(both_kernel, 1, tiles, diag_inv, rhs[HALF:] - row_sums[HALF:])
+    given_high = rhs[HALF:] - row_sums[HALF:]
+    z_high = solve("both", HALF, high, HALF, [tiles], diag_inv, given_high)
 
     z_own = lax.dynamic_index_in_dim(z_high, in_half, 0, keepdims=False).astype(BF)
     q = dot_nt(z_own, u0).astype(BF)
     given = jnp.where(upper, dot_nt(q, v0), 0.0)
     col_sum = copies(given, ROW).reshape(16, rhs_count, tile)[HALF:].sum(axis=0)
     col_sums = copies(col_sum, COL).reshape(8, rhs_count, tile)
-    z_low = leaf_call(backward_kernel, 0, tiles, diag_inv, x_low - col_sums)
+    z_low = solve("backward", HALF, low, 0, [tiles], diag_inv, x_low - col_sums)
     result = jnp.concatenate([z_low, z_high], axis=0).transpose(1, 0, 2)
     result = result.reshape(rhs_count, ntile * tile)
 

time: 234 us -> 223 us (0.953)
  Pallas kernels: 39.5 us -> 29.1 us
    pallas_call x3, Pallas kernels: 39.5 us -> 29.1 us  [solve(): pl.pallas_call(functools.partial(solve_kernel, rows, where, first, sweeps...]
where the time goes in v2:
time: 223 us; the launch traced here: 222 us
  waiting for transfers between devices  95.9 us (43%)
  blocking collectives  43.8 us (20%)
  Pallas kernels  29.1 us (13%)
  starting transfers between devices  20.1 us (9%)
  between operations  14.3 us (6%)
  local copies, waits for them, and re-layouts  8.36 us (4%)
  other arithmetic  7.83 us (4%)
  matrix products  2.76 us (1%)
    all_gather x1, waiting for transfers between devices, per_device(): tiles = lax.all_gather(share, ALL)  61 us
    pallas_call x3, Pallas kernels, solve(): pl.pallas_call(functools.partial(solve_kernel, rows, where, first, sweeps...  29.1 us
    all_to_all x3, waiting for transfers between devices, copies(): lax.all_to_all(stacked, axis, split_axis=0, concat_axis=0, tiled=True)  28.2 us
    all_to_all x2, blocking collectives, copies(): lax.all_to_all(stacked, axis, split_axis=0, concat_axis=0, tiled=True)  22.1 us
    all_to_all x1, blocking collectives, per_device(): lax.all_to_all(parts, ALL, split_axis=0, concat_axis=0, tiled=True)  21.8 us
    all_to_all x3, starting transfers between devices, copies(): lax.all_to_all(stacked, axis, split_axis=0, concat_axis=0, tiled=True)  13.2 us
    ppermute x1, starting transfers between devices, per_device(): lax.ppermute(with_layout_constraint(leaf_vt, ROWS), ALL, pairs)  6.88 us
    ppermute x1, waiting for transfers between devices, per_device(): lax.ppermute(with_layout_constraint(leaf_vt, ROWS), ALL, pairs)  6.7 us
  transfers between devices with their start and end apart: 5, of which 5 were waited for; matrix products, arithmetic and copies ran while one was open for 5% of the time, Pallas kernels for 0%

profile of v2, /device:TPU:0, one launch (start us, length us, event | category | flops | bytes accessed | tf_op | source)
XLA Modules:
  0.0 222.3 jit_solution(7748668075400249267)
XLA Ops:
  7.2 0.0 copy-start
  7.2 0.0 copy-start.2
  7.2 0.0 all-gather.3.cloned.1.call-start
  7.2 1.2 copy.27
  8.4 0.7 iota_compare_fusion
  9.1 0.1 convert_select_fusion
  9.3 6.9 %collective-permute-start = (f32[128,512]{1,0:T(8,128)S(1)}, f32[128,512]{1,0:T(8,128)S(1)}, u32[]{:S(2)}, u32[]{:S(2)}) collective-permute-start(f32[128,512]{1,0:T(8,128)S(1)} %fusion.12), channel_id=1, source_target_pairs={{0,63},{1,62},{2,61},{3,60},{4,59},{5,58},{6,57},{7,56},{8,55},{9,... | collective-permute-start | bytes 786440 | tf_op jit(solution)/shard_map/ppermute | solution.py:229
  16.2 6.7 %collective-permute-done = f32[128,512]{1,0:T(8,128)S(1)} collective-permute-done((f32[128,512]{1,0:T(8,128)S(1)}, f32[128,512]{1,0:T(8,128)S(1)}, u32[]{:S(2)}, u32[]{:S(2)}) %collective-permute-start) | collective-permute-done | bytes 262176 | tf_op jit(solution)/shard_map/ppermute | solution.py:229
  22.9 1.7 convert_select_fusion.1
  24.6 0.0 all-gather.3.cloned.1.call-update
  24.6 1.5 copy.35
  26.1 0.7 fusion.39
  26.8 1.1 convolution_bitcast_fusion
  27.9 0.8 scatter_fusion
  28.7 0.1 copy.29
  28.7 0.2 reshape.116
  28.9 0.3 copy.30
  29.2 0.3 reshape.140
  29.5 21.8 %all_to_all.30 = f32[128,1,512]{2,1,0:T(1,128)S(1)} all-to-all(f32[128,1,512]{2,1,0:T(1,128)S(1)} %reshape.140), channel_id=1, replica_groups=mesh['y'=4,'z'=4,'x'=4,'c'=2] {'y','z','x','c'}, dimensions={0} | all-to-all | bytes 524288 | tf_op jit(solution)/shard_map/all_to_all | solution.py:243
  51.3 0.5 broadcast.43
  51.8 1.3 reduce
  53.1 0.1 reshape.141
  53.2 0.1 reduce_sum.27
  53.4 1.0 reshape.142
  54.4 4.8 %all-to-all-start.1 = ((f32[128,1,512]{2,1,0:T(1,128)}), f32[128,1,512]{2,1,0:T(1,128)S(1)}, u32[]{:S(2)}, u32[]{:S(2)}) async-start(f32[128,1,512]{2,1,0:T(1,128)} %reshape.142), calls=%async_computation.1 | async-start | bytes 524288 | tf_op jit(solution)/shard_map/all_to_all | solution.py:26
  59.2 13.7 %all-to-all-done.1 = f32[128,1,512]{2,1,0:T(1,128)S(1)} async-done(((f32[128,1,512]{2,1,0:T(1,128)}), f32[128,1,512]{2,1,0:T(1,128)S(1)}, u32[]{:S(2)}, u32[]{:S(2)}) %all-to-all-start.1) | async-done | bytes 262176 | tf_op jit(solution)/shard_map/all_to_all | solution.py:26
  72.9 1.3 reduce.1
  74.1 0.1 reshape.143
  74.3 0.1 copy.31
  74.4 0.1 reshape.117
  74.5 1.1 fusion.13
  75.6 61.0 %all-gather.3.cloned.1.call-done = f32[16384,512]{1,0:T(8,128)} async-done(((f32[128,512]{1,0:T(8,128)}), f32[16384,512]{1,0:T(8,128)}) %all-gather.3.cloned.1.call-update) | async-done | bytes 33554448 | tf_op jit(solution)/shard_map/all_gather | solution.py:231
  136.6 8.3 %shard_map.104 = f32[8,8,512]{2,1,0:T(8,128)S(1)} custom-call(f32[128,128,512]{2,1,0:T(8,128)} %bitcast.75, bf16[16,512,512]{2,1,0:T(8,128)(2,1)} %refs_1_.5, f32[8,8,512]{2,1,0:T(8,128)S(1)} %slice.40.refs_2_), custom_call_target="tpu_custom_call" | custom-call | tf_op jit(solution)/shard_map/pallas_call | solution.py:179
  144.9 0.0 copy-done.2
  144.9 0.3 convolution_select_fusion.1
  145.3 10.2 %all_to_all.31 = f32[8,8,512]{2,1,0:T(8,128)S(1)} all-to-all(f32[8,8,512]{2,1,0:T(8,128)S(1)} %broadcast_in_dim.43), channel_id=1, replica_groups=mesh['y'=4,'z'=4,'x'=4,'c'=2] {'x','c'}, dimensions={0} | all-to-all | bytes 262144 | tf_op jit(solution)/shard_map/all_to_all | solution.py:26
  155.4 0.7 broadcast_in_dim.44
  156.2 5.1 %all-to-all-start.3 = ((f32[16,8,512]{2,1,0:T(8,128)}), f32[16,8,512]{2,1,0:T(8,128)S(1)}, u32[]{:S(2)}, u32[]{:S(2)}) async-start(f32[16,8,512]{2,1,0:T(8,128)} %broadcast_in_dim.44), calls=%async_computation.3 | async-start | bytes 524288 | tf_op jit(solution)/shard_map/all_to_all | solution.py:26
  161.3 8.5 %all-to-all-done.3 = f32[16,8,512]{2,1,0:T(8,128)S(1)} async-done(((f32[16,8,512]{2,1,0:T(8,128)}), f32[16,8,512]{2,1,0:T(8,128)S(1)}, u32[]{:S(2)}, u32[]{:S(2)}) %all-to-all-start.3) | async-done | bytes 262176 | tf_op jit(solution)/shard_map/all_to_all | solution.py:26
  169.8 0.0 copy-start.1
  169.8 0.0 copy-start.3
  169.8 11.8 %shard_map.105 = f32[8,8,512]{2,1,0:T(8,128)S(1)} custom-call(f32[128,128,512]{2,1,0:T(8,128)} %bitcast.76, bf16[16,512,512]{2,1,0:T(8,128)(2,1)} %refs_1_.5, f32[8,8,512]{2,1,0:T(8,128)S(1)} %slice_subtract_fusion.refs_2_), custom_call_target="tpu_custom_call" | custom-call | tf_op jit(solution)/shard_map/pallas_call | solution.py:179
  181.6 0.3 convolution_select_fusion
  181.9 0.1 broadcast_in_dim.45
  182.0 11.9 %all_to_all.32 = f32[16,8,512]{2,1,0:T(8,128)S(1)} all-to-all(f32[16,8,512]{2,1,0:T(8,128)S(1)} %broadcast_in_dim.45), channel_id=1, replica_groups=mesh['y'=4,'z'=4,'x'=4,'c'=2] {'y','z'}, dimensions={0} | all-to-all | bytes 524288 | tf_op jit(solution)/shard_map/all_to_all | solution.py:26
  193.9 0.7 broadcast_in_dim.46
  194.6 3.4 %all-to-all-start.5 = ((f32[8,8,512]{2,1,0:T(8,128)}), f32[8,8,512]{2,1,0:T(8,128)S(1)}, u32[]{:S(2)}, u32[]{:S(2)}) async-start(f32[8,8,512]{2,1,0:T(8,128)} %broadcast_in_dim.46), calls=%async_computation.5 | async-start | bytes 262144 | tf_op jit(solution)/shard_map/all_to_all | solution.py:26
  198.0 6.0 %all-to-all-done.5 = f32[8,8,512]{2,1,0:T(8,128)S(1)} async-done(((f32[8,8,512]{2,1,0:T(8,128)}), f32[8,8,512]{2,1,0:T(8,128)S(1)}, u32[]{:S(2)}, u32[]{:S(2)}) %all-to-all-start.5) | async-done | bytes 131104 | tf_op jit(solution)/shard_map/all_to_all | solution.py:26
  204.0 9.0 %shard_map.106 = f32[8,8,512]{2,1,0:T(8,128)S(1)} custom-call(f32[128,128,512]{2,1,0:T(8,128)} %bitcast.77, bf16[16,512,512]{2,1,0:T(8,128)(2,1)} %refs_1_.5, f32[8,8,512]{2,1,0:T(8,128)S(1)} %sub.18.refs_2_), custom_call_target="tpu_custom_call" | custom-call | tf_op jit(solution)/shard_map/pallas_call | solution.py:179
  213.0 0.6 gather_fusion
  213.6 0.0 copy-done
  213.6 0.0 copy-done.1
  213.6 0.0 copy-done.3
  213.6 1.1 fusion.6
  214.8 0.7 constant_dynamic-slice_fusion
  (11 shorter events, 0.3 us)
Async XLA Ops:
  7.2 206.4 %copy-start = (bf16[1,512,512]{2,1,0:T(8,128)(2,1)S(1)}, bf16[1,512,512]{2,1,0:T(8,128)(2,1)}, u32[]{:S(2)}) copy-start(bf16[1,512,512]{2,1,0:T(8,128)(2,1)} %param.16) | copy-start | bytes 1572868
  7.2 137.8 %copy-start.2 = (bf16[1,1,1,2,128,512]{5,4,3,2,1,0:T(8,128)(2,1)S(1)}, bf16[1,1,1,2,128,512]{5,4,3,2,1,0:T(8,128)(2,1)}, u32[]{:S(2)}) copy-start(bf16[1,1,1,2,128,512]{5,4,3,2,1,0:T(8,128)(2,1)} %param.11) | copy-start | bytes 786436
  7.2 129.4 %all-gather.3.cloned.1.call-start = ((), (), s32[]{:S(2)}) async-start(), calls=%async_computation.6 | async-start | bytes 33816576 | tf_op jit(solution)/shard_map/all_gather | solution.py:231
  9.3 13.6 %collective-permute-start = (f32[128,512]{1,0:T(8,128)S(1)}, f32[128,512]{1,0:T(8,128)S(1)}, u32[]{:S(2)}, u32[]{:S(2)}) collective-permute-start(f32[128,512]{1,0:T(8,128)S(1)} %fusion.12), channel_id=1, source_target_pairs={{0,63},{1,62},{2,61},{3,60},{4,59},{5,58},{6,57},{7,56},{8,55},{9,... | collective-permute-start | bytes 786440 | tf_op jit(solution)/shard_map/ppermute | solution.py:229
  54.4 18.5 %all-to-all-start.1 = ((f32[128,1,512]{2,1,0:T(1,128)}), f32[128,1,512]{2,1,0:T(1,128)S(1)}, u32[]{:S(2)}, u32[]{:S(2)}) async-start(f32[128,1,512]{2,1,0:T(1,128)} %reshape.142), calls=%async_computation.1 | async-start | bytes 524288 | tf_op jit(solution)/shard_map/all_to_all | solution.py:26
  156.2 13.6 %all-to-all-start.3 = ((f32[16,8,512]{2,1,0:T(8,128)}), f32[16,8,512]{2,1,0:T(8,128)S(1)}, u32[]{:S(2)}, u32[]{:S(2)}) async-start(f32[16,8,512]{2,1,0:T(8,128)} %broadcast_in_dim.44), calls=%async_computation.3 | async-start | bytes 524288 | tf_op jit(solution)/shard_map/all_to_all | solution.py:26
  169.8 43.8 %copy-start.1 = (bf16[1,512,1024]{2,1,0:T(8,128)(2,1)S(1)}, bf16[1,512,1024]{2,1,0:T(8,128)(2,1)}, u32[]{:S(2)}) copy-start(bf16[1,512,1024]{2,1,0:T(8,128)(2,1)} %param.15) | copy-start | bytes 3145732
  169.8 43.8 %copy-start.3 = (bf16[1,8,512]{2,1,0:T(8,128)(2,1)S(1)}, bf16[1,8,512]{2,1,0:T(8,128)(2,1)}, u32[]{:S(2)}) copy-start(bf16[1,8,512]{2,1,0:T(8,128)(2,1)} %param.14) | copy-start | bytes 24580
  194.6 9.4 %all-to-all-start.5 = ((f32[8,8,512]{2,1,0:T(8,128)}), f32[8,8,512]{2,1,0:T(8,128)S(1)}, u32[]{:S(2)}, u32[]{:S(2)}) async-start(f32[8,8,512]{2,1,0:T(8,128)} %broadcast_in_dim.46), calls=%async_computation.5 | async-start | bytes 262144 | tf_op jit(solution)/shard_map/all_to_all | solution.py:26
Sparse Core Ops, SparseCore 0:
  24.7 111.8 all-gather.2

commit v3 on v2

v3 whole, which is shorter than its diff:
```python
import functools

import jax
import jax.numpy as jnp
from jax import lax
from jax.experimental import pallas as pl
from jax.experimental.layout import Layout, with_layout_constraint
from jax.experimental.pallas import tpu as pltpu
from jax.sharding import Mesh
from jax.sharding import PartitionSpec as P

BLK = 128
BB = 8
ROW = ("yh", "yl", "z")
HALF_ROW = ("yl", "z")
COL = ("x", "c")
PLANE = ("z", "x", "c")
ALL = ("yh", "yl", "z", "x", "c")
HALF = 8
BF = jnp.bfloat16
F32 = jnp.float32
ROWS = Layout((0, 1))


def copies(v, axis):
    n = lax.axis_size(axis)
    stacked = jnp.broadcast_to(v, (n, *v.shape))
    return lax.all_to_all(stacked, axis, split_axis=0, concat_axis=0, tiled=True)


def dot_nn(a, b):
    return lax.dot_general(a, b, (((1,), (0,)), ((), ())), preferred_element_type=F32)


def dot_nt(a, b):
    return lax.dot_general(a, b, (((1,), (1,)), ((), ())), preferred_element_type=F32)


def exact(dot, a, b):
    high = a.astype(BF)
    low = (a - high.astype(F32)).astype(BF)
    both = dot(jnp.concatenate([high, low], axis=0), b)
    n = a.shape[0]
    return both[:n] + both[n:]


def first_tile(row):
    return row * (row - 1) // 2


SLOTS = 3
TILES = first_tile(HALF)
SPARE = {(1, 0): (1, 7), (2, 0): (2, 6), (2, 1): (2, 7), (3, 0): (0, 6), (3, 1): (3, 7), (3, 2): (0, 7)}


def spot(plane, i, k):
    z = i % 4
    own = i // 4 == plane
    if own or (plane == 0 and k >= z):
        return 8 * z + k
    z, k = SPARE[z, k]
    return 8 * z + k


def plane_pairs():
    pairs = []
    for half in range(2):
        for i in range(HALF):
            for k in range(i):
                plane = i // 4
                source = 64 * half + 32 * plane + spot(plane, i, k)
                target = 64 * half + 32 * (1 - plane) + spot(1 - plane, i, k)
                pairs.append((source, target))
    return pairs


class Leaf:
    def __init__(self, left, right, diag):
        self.left, self.right, self.diag = left, right, diag

    def column(self, j):
        return sum(HALF - 1 - m for m in range(j))

    def u(self, i, k, count=1):
        at = first_tile(i) + k
        return self.left[at : at + count].reshape(-1, self.left.shape[2])

    def vt(self, i, k, count=1):
        at = self.column(k) + i - k - 1
        return self.right[at : at + count].reshape(-1, self.right.shape[2])


class Moves:
    def __init__(self, rows):
        self.rows = rows

    def start(self, i):
        for move in self.rows.get(i, []):
            move.start()

    def wait(self, i):
        for move in self.rows.get(i, []):
            move.wait()


def inverse_moves(leaf, first, inv, sems):
    return Moves(
        {
            n: [pltpu.make_async_copy(inv.at[first + n], leaf.diag.at[n], sems.at[n])]
            for n in range(HALF)
        }
    )


def factor_moves(leaf, kept_left, kept_right, lsems, rsems, keep):
    rows = {}
    for i in range(1, HALF):
        at = first_tile(i)
        pairs = [(kept_left.at[pl.ds(at, i)], leaf.left.at[pl.ds(at, i)], lsems.at[i])]
        for k in range(i):
            place = leaf.column(k) + i - k - 1
            pairs.append((kept_right.at[place], leaf.right.at[place], rsems.at[place]))
        rows[i] = [
            pltpu.make_async_copy(*((b, a) if keep else (a, b)), sem) for a, b, sem in pairs
        ]
    return Moves(rows)


class Loader:
    def __init__(self, leaf, place, tiles, inv, kept, stage, sems, dsems, lsems, rsems):
        self.leaf, self.stage = leaf, stage
        rows = {}
        for i in range(1, HALF):
            rows[i] = []
            for k in range(i):
                one, two = spot(0, i, k), spot(1, i, k)
                rows[i].append(
                    pltpu.make_async_copy(
                        tiles.at[one + place[0] * (two - one)],
                        stage.at[i % SLOTS, k],
                        sems.at[first_tile(i) + k],
                    )
                )
        self.tiles = Moves(rows)
        self.inverse = inverse_moves(leaf, HALF * place[1], inv, dsems)
        self.kept = factor_moves(leaf, *kept, lsems, rsems, True)
        for i in range(SLOTS):
            self.start(i)
        self(0)

    def start(self, i):
        self.inverse.start(i)
        self.tiles.start(i)

    def __call__(self, i):
        leaf = self.leaf
        rank = leaf.left.shape[1]
        self.inverse.wait(i)
        self.tiles.wait(i)
        for k in range(i):
            leaf.left[first_tile(i) + k] = self.stage[i % SLOTS, k, :rank].astype(BF)
            leaf.right[leaf.column(k) + i - k - 1] = self.stage[i % SLOTS, k, rank:].astype(BF)
        self.kept.start(i)
        if i + SLOTS < HALF:
            self.start(i + SLOTS)

    def finish(self):
        for i in range(HALF):
            self.kept.wait(i)


class Reloader:
    def __init__(self, leaf, place, inv, kept, dsems, lsems, rsems, order):
        self.inverse = inverse_moves(leaf, HALF * place[1], inv, dsems)
        self.factors = factor_moves(leaf, *kept, lsems, rsems, False)
        for i in order:
            self.inverse.start(i)
            self.factors.start(i)
        self(order[0])

    def __call__(self, i):
        self.inverse.wait(i)
        self.factors.wait(i)


def forward(leaf, rhs, load=None):
    solved, narrow = [], []
    partial = rhs[0]
    last = None
    for i in range(HALF):
        acc = partial
        if i:
            acc = acc - dot_nn(last, leaf.u(i, i - 1))
        x = exact(dot_nn, acc, leaf.diag[i])
        if i + 1 < HALF:
            if load:
                load(i + 1)
            partial = rhs[i + 1]
            if i:
                known = [dot_nt(narrow[k], leaf.vt(i + 1, k)).astype(BF) for k in range(i)]
                partial = partial - dot_nn(jnp.concatenate(known, axis=1), leaf.u(i + 1, 0, i))
        solved.append(x)
        narrow.append(x.astype(BF))
        if i + 1 < HALF:
            last = dot_nt(narrow[i], leaf.vt(i + 1, i)).astype(BF)
    return solved


def backward(leaf, rhs, load=None):
    width = leaf.left.shape[1]
    solved = [None] * HALF
    waiting = {j: [] for j in range(HALF)}
    partial = rhs[HALF - 1]
    last = None
    for j in reversed(range(HALF)):
        acc = partial
        if j + 1 < HALF:
            acc = acc - dot_nn(last, leaf.vt(j + 1, j))
        z = exact(dot_nt, acc, leaf.diag[j])
        if j:
            if load:
                load(j - 1)
            partial = rhs[j - 1]
            if waiting[j - 1]:
                known = jnp.concatenate(waiting[j - 1][::-1], axis=1)
                partial = partial - dot_nn(known, leaf.vt(j + 1, j - 1, HALF - 1 - j))
        solved[j] = z
        narrow = z.astype(BF)
        if j:
            last = dot_nt(narrow, leaf.u(j, j - 1)).astype(BF)
        if j > 1:
            others = dot_nt(narrow, leaf.u(j, 0, j - 1)).astype(BF)
            for k in range(j - 1):
                waiting[k].append(others[:, k * width : (k + 1) * width])
    return solved


def put(out, values):
    for i in range(HALF):
        out[i] = values[i]


def load_kernel(place, tiles, inv, rhs, out, kept_left, kept_right, stage, *scratch):
    left, right, diag, sems, dsems, lsems, rsems = scratch
    leaf = Leaf(left, right, diag)
    kept = (kept_left, kept_right)
    load = Loader(leaf, place, tiles, inv, kept, stage, sems, dsems, lsems, rsems)
    put(out, forward(leaf, [rhs[i] for i in range(HALF)], load))
    load.finish()


def both_kernel(place, kept_left, kept_right, inv, rhs, out, left, right, diag, *sems):
    leaf = Leaf(left, right, diag)
    load = Reloader(leaf, place, inv, (kept_left, kept_right), *sems, range(HALF))
    put(out, backward(leaf, forward(leaf, [rhs[i] for i in range(HALF)], load)))


def backward_kernel(place, kept_left, kept_right, inv, rhs, out, left, right, diag, *sems):
    leaf = Leaf(left, right, diag)
    load = Reloader(leaf, place, inv, (kept_left, kept_right), *sems, range(HALF)[::-1])
    put(out, backward(leaf, [rhs[i] for i in range(HALF)], load))


IN_SMEM = pl.BlockSpec(memory_space=pltpu.SMEM)
IN_VMEM = pl.BlockSpec(memory_space=pltpu.VMEM)
IN_HBM = pl.BlockSpec(memory_space=pltpu.HBM)


def limit(mib):
    return pltpu.CompilerParams(vmem_limit_bytes=mib * 1024 * 1024)


def in_hbm(v):
    return pltpu.with_memory_space_constraint(v, pltpu.HBM)


def leaf_scratch(rank, tile):
    return [
        pltpu.VMEM((TILES, rank, tile), BF),
        pltpu.VMEM((TILES, rank, tile), BF),
        pltpu.VMEM((HALF, tile, tile), BF),
    ]


def leaf_sems():
    dma = pltpu.SemaphoreType.DMA
    return [dma((HALF,)), dma((HALF,)), dma((TILES,))]


def load_and_forward(place, tiles, inv, rhs):
    rank, tile = tiles.shape[1] // 2, tiles.shape[2]
    factors = pltpu.HBM((TILES, rank, tile), BF)
    return pl.pallas_call(
        load_kernel,
        out_shape=(jax.ShapeDtypeStruct(rhs.shape, F32), factors, factors),
        in_specs=[IN_SMEM, IN_HBM, IN_HBM, IN_VMEM],
        out_specs=(IN_VMEM, IN_HBM, IN_HBM),
        scratch_shapes=[
            pltpu.VMEM((SLOTS, HALF - 1, 2 * rank, tile), F32),
            *leaf_scratch(rank, tile),
            pltpu.SemaphoreType.DMA((TILES,)),
            *leaf_sems(),
        ],
        compiler_params=limit(36),
    )(place, in_hbm(tiles), in_hbm(inv), rhs)


def solve(body, place, left, right, inv, rhs):
    return pl.pallas_call(
        body,
        out_shape=jax.ShapeDtypeStruct(rhs.shape, F32),
        in_specs=[IN_SMEM, IN_HBM, IN_HBM, IN_HBM, IN_VMEM],
        out_specs=IN_VMEM,
        scratch_shapes=[*leaf_scratch(*left.shape[1:]), *leaf_sems()],
        compiler_params=limit(24),
    )(place, in_hbm(left), in_hbm(right), in_hbm(inv), rhs)


def per_device(
    root_rhs, diag_inv, tile_u, tile_v, tile_rank, child_x, border_t, child_inv, child_blocks
):
    my_row = lax.axis_index(ROW)
    my_col = lax.axis_index(COL)
    ntile = diag_inv.shape[0]
    tile = diag_inv.shape[1]
    rhs_count = root_rhs.shape[0]
    rank_max = tile_u.shape[4]
    n_child = child_x.shape[0]
    nblk = ntile * tile // BLK
    ndev = lax.axis_size(ALL)
    upper = my_row >= HALF
    in_half = my_row % HALF
    half = lax.axis_index("yh")

    left = tile_u[0, 0, 0]
    live = jnp.arange(rank_max)[None, None, :] < tile_rank[0, 0, 0][:, None, None]
    right = jnp.where(live, tile_v[0, 0, 0].astype(F32), 0.0)

    leaf_u = jnp.where(upper, left[1], left[0]).astype(F32)
    leaf_vt = jnp.where(upper, right[1], right[0]).T
    own_tile = with_layout_constraint(jnp.concatenate([leaf_u, leaf_vt], axis=0), ROWS)
    other_tile = lax.ppermute(own_tile, ALL, plane_pairs())
    share = jnp.where(my_col < in_half, own_tile, other_tile)
    share = with_layout_constraint(share, ROWS)
    tiles = lax.all_gather(share, PLANE)
    place = jnp.stack([lax.axis_index("yl"), half]).astype(jnp.int32)

    upward = jnp.einsum("crs,csb->crb", child_x, border_t, preferred_element_type=F32)
    pieces = (
        upward.reshape(n_child, rhs_count, BB, BLK)
        .transpose(1, 0, 2, 3)
        .reshape(rhs_count, n_child * BB, BLK)
    )
    flat_blocks = child_blocks.reshape(-1)
    dense = jnp.zeros((rhs_count, nblk, BLK), F32).at[:, flat_blocks, :].add(pieces)
    width = ntile * tile // ndev
    parts = dense.reshape(rhs_count, ndev, width).transpose(1, 0, 2)
    mine = lax.all_to_all(parts, ALL, split_axis=0, concat_axis=0, tiled=True).sum(axis=0)
    child_sum = copies(mine, ALL).reshape(ndev, rhs_count, width)
    child_sum = child_sum.transpose(1, 0, 2).reshape(rhs_count, ntile, tile).transpose(1, 0, 2)
    rhs = root_rhs.reshape(rhs_count, ntile, tile).transpose(1, 0, 2).astype(F32) - child_sum

    own_rhs = lax.dynamic_slice_in_dim(rhs, HALF * half, HALF, 0)
    x_low, kept_left, kept_right = load_and_forward(place, tiles, diag_inv, own_rhs)
    v0 = right[0].astype(BF)
    u0 = left[0]
    x_col = lax.dynamic_index_in_dim(x_low, my_col, 0, keepdims=False)
    x_own = lax.ppermute(x_col, "yh", [(0, 1)])
    x_own = x_own + jnp.where(upper, 0.0, x_col)
    p = dot_nn(x_own.astype(BF), v0).astype(BF)
    row_sum = copies(dot_nn(p, u0), COL).reshape(8, rhs_count, tile).sum(axis=0)
    row_sums = copies(row_sum, HALF_ROW).reshape(HALF, rhs_count, tile)
    z_high = solve(both_kernel, place, kept_left, kept_right, diag_inv, own_rhs - row_sums)

    z_own = lax.dynamic_index_in_dim(z_high, in_half, 0, keepdims=False).astype(BF)
    q = dot_nt(z_own, u0).astype(BF)
    col_sum = copies(dot_nt(q, v0), HALF_ROW).reshape(HALF, rhs_count, tile).sum(axis=0)
    col_sum = lax.ppermute(col_sum, "yh", [(1, 0)])
    col_sums = copies(col_sum, COL).reshape(8, rhs_count, tile)
    low_rhs = x_low - col_sums
    z_low = solve(backward_kernel, place, kept_left, kept_right, diag_inv, low_rhs)
    z_mine = jnp.where(upper, z_high, z_low)
    z_other = lax.ppermute(z_mine, "yh", [(0, 1), (1, 0)])
    low_part = jnp.where(upper, z_other, z_mine)
    high_part = jnp.where(upper, z_mine, z_other)
    result = jnp.concatenate([low_part, high_part], axis=0).transpose(1, 0, 2)
    result = result.reshape(rhs_count, ntile * tile)

    start = (my_row * 8 + my_col) * width
    root_part = lax.dynamic_slice_in_dim(result, start, width, 1)
    gathered = result.reshape(rhs_count, nblk, BLK)[:, flat_blocks, :]
    gathered = gathered.reshape(rhs_count, n_child, BB * BLK).astype(BF)
    returned = jnp.einsum("rcb,csb->crs", gathered, border_t, preferred_element_type=F32)
    child_out = child_x.astype(F32) - jnp.einsum(
        "crs,cst->crt", returned, child_inv.astype(F32)
    )
    return (root_part, child_out)


def solution(mesh):
    finer = Mesh(mesh.devices.reshape(2, 2, 4, 4, 2), ALL)
    in_specs = (
        P(),
        P(),
        P(ROW, COL, None, None, None, None),
        P(ROW, COL, None, None, None, None),
        P(ROW, COL, None, None),
        P(ALL, None, None),
        P(ALL, None, None),
        P(ALL, None, None),
        P(ALL, None),
    )
    out_specs = (P(None, ALL), P(ALL, None, None))
    return jax.shard_map(
        per_device, mesh=finer, in_specs=in_specs, out_specs=out_specs, check_vma=False
    )
```

time: 223 us -> 218 us (0.978)
  waiting for transfers between devices: 95.9 us -> 74 us
  blocking collectives: 43.8 us -> 65.3 us
  starting transfers between devices: 20.1 us -> 15.9 us
    all_gather x1, waiting for transfers between devices: 61 us -> 26.8 us  [per_device(): tiles = lax.all_gather(share, PLANE)]
    ppermute x1 -> x4, waiting for transfers between devices: 6.7 us -> 27.3 us  [the longest x1 13.6 us: per_device(): other_tile = lax.ppermute(own_tile, ALL, plane_pairs())]
    all_to_all x1, blocking collectives: 21.8 us -> 37.7 us  [per_device(): lax.all_to_all(parts, ALL, split_axis=0, concat_axis=0, tiled=True)]
    all_to_all x3 -> x2, waiting for transfers between devices: 28.2 us -> 19.8 us  [copies(): lax.all_to_all(stacked, axis, split_axis=0, concat_axis=0, tiled=True)]
    all_to_all x2 -> x3, blocking collectives: 22.1 us -> 27.6 us  [copies(): lax.all_to_all(stacked, axis, split_axis=0, concat_axis=0, tiled=True)]
    all_to_all x3 -> x2, starting transfers between devices: 13.2 us -> 8.17 us  [copies(): lax.all_to_all(stacked, axis, split_axis=0, concat_axis=0, tiled=True)]
    ppermute x1 -> x4, starting transfers between devices: 6.88 us -> 7.65 us  [the longest x1 4.85 us: per_device(): x_own = lax.ppermute(x_col, 'yh', [(0, 1)])]
  transfers between devices with their start and end apart: 5 -> 7, of which waited for: 5 -> 7; matrix products, arithmetic and copies ran while one was open for 5% -> 5% of each run, Pallas kernels for 0% -> 0%
where the time goes in v3:
time: 218 us; the launch traced here: 217 us
  waiting for transfers between devices  74 us (34%)
  blocking collectives  65.3 us (30%)
  Pallas kernels  29.8 us (14%)
  starting transfers between devices  15.9 us (7%)
  between operations  14.4 us (7%)
  local copies, waits for them, and re-layouts  7.68 us (4%)
  other arithmetic  7.15 us (3%)
  matrix products  2.77 us (1%)
    all_to_all x1, blocking collectives, per_device(): lax.all_to_all(parts, ALL, split_axis=0, concat_axis=0, tiled=True)  37.7 us
    all_to_all x3, blocking collectives, copies(): lax.all_to_all(stacked, axis, split_axis=0, concat_axis=0, tiled=True)  27.6 us
    all_gather x1, waiting for transfers between devices, per_device(): tiles = lax.all_gather(share, PLANE)  26.8 us
    all_to_all x2, waiting for transfers between devices, copies(): lax.all_to_all(stacked, axis, split_axis=0, concat_axis=0, tiled=True)  19.8 us
    pallas_call x2, Pallas kernels, solve(): pl.pallas_call(body, out_shape=jax.ShapeDtypeStruct(rhs.shape, F32), in_s...  18.8 us
    ppermute x1, waiting for transfers between devices, per_device(): other_tile = lax.ppermute(own_tile, ALL, plane_pairs())  13.6 us
    pallas_call x1, Pallas kernels, load_and_forward(): pl.pallas_call(load_kernel, out_shape=(jax.ShapeDtypeStruct(rhs.shape, F3...  11 us
    all_to_all x2, starting transfers between devices, copies(): lax.all_to_all(stacked, axis, split_axis=0, concat_axis=0, tiled=True)  8.17 us
  transfers between devices with their start and end apart: 7, of which 7 were waited for; matrix products, arithmetic and copies ran while one was open for 5% of the time, Pallas kernels for 0%

profile of v3, /device:TPU:0, one launch (start us, length us, event | category | flops | bytes accessed | tf_op | source)
XLA Modules:
  0.0 217.0 jit_solution(11024422110979420097)
XLA Ops:
  7.2 0.0 copy-start
  7.2 0.0 all-gather.3.cloned.1.call-start
  7.2 1.1 copy.27
  8.4 0.7 iota_compare_fusion
  9.1 0.1 convert_select_fusion
  9.3 1.0 fusion.20
  10.3 0.0 copy-start.4
  10.3 1.4 collective-permute-start
  11.8 13.6 %collective-permute-done = f32[256,512]{1,0:T(8,128)S(1)} collective-permute-done((f32[256,512]{1,0:T(8,128)S(1)}, f32[256,512]{1,0:T(8,128)S(1)}, u32[]{:S(2)}, u32[]{:S(2)}) %collective-permute-start) | collective-permute-done | bytes 524320 | tf_op jit(solution)/shard_map/ppermute | solution.py:342
  25.3 0.9 broadcast_select_fusion
  26.2 0.0 all-gather.3.cloned.1.call-update
  26.2 1.5 copy.35
  27.8 0.7 fusion.41
  28.4 1.1 convolution_bitcast_fusion
  29.5 0.8 scatter_fusion
  30.3 0.1 copy.29
  30.4 0.1 reshape.114
  30.5 0.3 copy.30
  30.8 0.3 reshape.138
  31.2 37.7 %all_to_all.30 = f32[128,1,512]{2,1,0:T(1,128)S(1)} all-to-all(f32[128,1,512]{2,1,0:T(1,128)S(1)} %reshape.138), channel_id=1, replica_groups=mesh['yh'=2,'yl'=2,'z'=4,'x'=4,'c'=2] {'yh','yl','z','x','c'}, dimensions={0} | all-to-all | bytes 524288 | tf_op jit(solution)/shard_map/all_to_all | solution.py:358
  68.8 0.6 broadcast.43
  69.4 1.2 reduce
  70.7 0.1 reshape.139
  70.8 0.1 reduce_sum.27
  71.0 1.0 reshape.140
  72.0 4.6 %all-to-all-start.1 = ((f32[128,1,512]{2,1,0:T(1,128)}), f32[128,1,512]{2,1,0:T(1,128)S(1)}, u32[]{:S(2)}, u32[]{:S(2)}) async-start(f32[128,1,512]{2,1,0:T(1,128)} %reshape.140), calls=%async_computation.1 | async-start | bytes 524288 | tf_op jit(solution)/shard_map/all_to_all | solution.py:28
  76.6 0.1 pad_add_fusion.place
  76.7 13.5 %all-to-all-done.1 = f32[128,1,512]{2,1,0:T(1,128)S(1)} async-done(((f32[128,1,512]{2,1,0:T(1,128)}), f32[128,1,512]{2,1,0:T(1,128)S(1)}, u32[]{:S(2)}, u32[]{:S(2)}) %all-to-all-start.1) | async-done | bytes 262176 | tf_op jit(solution)/shard_map/all_to_all | solution.py:28
  90.2 1.2 reduce.1
  91.5 0.1 reshape.141
  91.6 0.1 copy.31
  91.7 0.1 reshape.115
  91.9 0.0 copy-done.4
  91.9 0.1 fusion.16.rhs
  92.0 26.8 %all-gather.3.cloned.1.call-done = f32[8192,512]{1,0:T(8,128)} async-done(((f32[256,512]{1,0:T(8,128)}), f32[8192,512]{1,0:T(8,128)}) %all-gather.3.cloned.1.call-update) | async-done | bytes 16777232 | tf_op jit(solution)/shard_map/all_gather | solution.py:345
  118.8 0.0 copy-start.2
  118.8 11.0 %shard_map.104 = (f32[8,8,512]{2,1,0:T(8,128)S(1)}, bf16[28,128,512]{2,1,0:T(8,128)(2,1)}, bf16[28,128,512]{2,1,0:T(8,128)(2,1)}) custom-call(s32[2]{0:T(128)S(1)} %pad_add_fusion.place, f32[32,256,512]{2,1,0:T(8,128)} %bitcast.75, bf16[16,512,512]{2,1,0:T(8,128)(2,1)} %inv.5, f32[8,8,512]{2,1,0:T(8,128)S(1)} %fusion.16.rhs), custom_call_target="tpu_custom_call" | custom-call | tf_op jit(solution)/shard_map/pallas_call | solution.py:293
  129.9 4.9 %collective-permute-start.1 = (f32[8,512]{1,0:T(8,128)S(1)}, f32[8,512]{1,0:T(8,128)S(1)}, u32[]{:S(2)}, u32[]{:S(2)}) collective-permute-start(f32[8,512]{1,0:T(8,128)S(1)} %dynamic-slice_bitcast_fusion), channel_id=1, source_target_pairs={{0,64},{1,65},{2,66},{3,67},{4,68},{5,69},{6,70},{7,71},{8,72},{9,... | collective-permute-start | bytes 49160 | tf_op jit(solution)/shard_map/ppermute | solution.py:368
  134.7 1.4 collective-permute-done.1
  136.1 0.0 copy-done.2
  136.1 0.3 fusion.9
  136.5 10.1 %all_to_all.31 = f32[8,8,512]{2,1,0:T(8,128)S(1)} all-to-all(f32[8,8,512]{2,1,0:T(8,128)S(1)} %broadcast_in_dim.42), channel_id=1, replica_groups=mesh['yh'=2,'yl'=2,'z'=4,'x'=4,'c'=2] {'x','c'}, dimensions={0} | all-to-all | bytes 262144 | tf_op jit(solution)/shard_map/all_to_all | solution.py:28
  146.5 0.7 broadcast_in_dim.43
  147.2 3.5 %all-to-all-start.3 = ((f32[8,8,512]{2,1,0:T(8,128)}), f32[8,8,512]{2,1,0:T(8,128)S(1)}, u32[]{:S(2)}, u32[]{:S(2)}) async-start(f32[8,8,512]{2,1,0:T(8,128)} %broadcast_in_dim.43), calls=%async_computation.3 | async-start | bytes 262144 | tf_op jit(solution)/shard_map/all_to_all | solution.py:28
  150.8 6.3 %all-to-all-done.3 = f32[8,8,512]{2,1,0:T(8,128)S(1)} async-done(((f32[8,8,512]{2,1,0:T(8,128)}), f32[8,8,512]{2,1,0:T(8,128)S(1)}, u32[]{:S(2)}, u32[]{:S(2)}) %all-to-all-start.3) | async-done | bytes 131104 | tf_op jit(solution)/shard_map/all_to_all | solution.py:28
  157.1 11.2 %shard_map.105 = f32[8,8,512]{2,1,0:T(8,128)S(1)} custom-call(s32[2]{0:T(128)S(1)} %pad_add_fusion.place, bf16[28,128,512]{2,1,0:T(8,128)(2,1)} %get-tuple-element.5.kept_left, bf16[28,128,512]{2,1,0:T(8,128)(2,1)} %get-tuple-element.6.kept_right, bf16[16,512,512]{2,1,0:T(8,128)(2,1)} %inv.5, f32[8,8,512]{2,1,0:T(8,128)S(1)} %sub.14.rhs), custom_call_target="tpu_custom_call" | custom-call | tf_op jit(solution)/shard_map/pallas_call | solution.py:309
  168.3 0.3 fusion.10
  168.6 9.1 %all_to_all.32 = f32[8,8,512]{2,1,0:T(8,128)S(1)} all-to-all(f32[8,8,512]{2,1,0:T(8,128)S(1)} %broadcast_in_dim.44), channel_id=1, replica_groups=mesh['yh'=2,'yl'=2,'z'=4,'x'=4,'c'=2] {'yl','z'}, dimensions={0} | all-to-all | bytes 262144 | tf_op jit(solution)/shard_map/all_to_all | solution.py:28
  177.7 1.3 collective-permute-start.2
  179.0 5.8 %collective-permute-done.2 = f32[8,512]{1,0:T(8,128)S(1)} collective-permute-done((f32[8,512]{1,0:T(8,128)S(1)}, f32[8,512]{1,0:T(8,128)S(1)}, u32[]{:S(2)}, u32[]{:S(2)}) %collective-permute-start.2) | collective-permute-done | bytes 16416 | tf_op jit(solution)/shard_map/ppermute | solution.py:378
  184.9 8.5 %all_to_all.33 = f32[8,8,512]{2,1,0:T(8,128)S(1)} all-to-all(f32[8,8,512]{2,1,0:T(8,128)S(1)} %broadcast_in_dim.45), channel_id=1, replica_groups=mesh['yh'=2,'yl'=2,'z'=4,'x'=4,'c'=2] {'x','c'}, dimensions={0} | all-to-all | bytes 262144 | tf_op jit(solution)/shard_map/all_to_all | solution.py:28
  193.4 0.0 copy-start.1
  193.4 0.0 copy-start.3
  193.4 7.6 %shard_map.106 = f32[8,8,512]{2,1,0:T(8,128)S(1)} custom-call(s32[2]{0:T(128)S(1)} %pad_add_fusion.place, bf16[28,128,512]{2,1,0:T(8,128)(2,1)} %get-tuple-element.5.kept_left, bf16[28,128,512]{2,1,0:T(8,128)(2,1)} %get-tuple-element.6.kept_right, bf16[16,512,512]{2,1,0:T(8,128)(2,1)} %inv.5, f32[8,8,512]{2,1,0:T(8,128)S(1)} %sub.15.rhs), custom_call_target="tpu_custom_call" | custom-call | tf_op jit(solution)/shard_map/pallas_call | solution.py:309
  201.1 0.1 collective-permute-start.3
  201.2 6.5 %collective-permute-done.3 = f32[8,8,512]{2,1,0:T(8,128)S(1)} collective-permute-done((f32[8,8,512]{2,1,0:T(8,128)S(1)}, f32[8,8,512]{2,1,0:T(8,128)S(1)}, u32[]{:S(2)}, u32[]{:S(2)}) %collective-permute-start.3) | collective-permute-done | bytes 131104 | tf_op jit(solution)/shard_map/ppermute | solution.py:383
  207.7 0.6 gather_fusion
  208.3 0.0 copy-done
  208.3 0.0 copy-done.1
  208.3 0.0 copy-done.3
  208.3 1.1 fusion.6
  209.5 0.7 constant_dynamic-slice_fusion
  (17 shorter events, 0.4 us)
Async XLA Ops:
  7.2 201.1 %copy-start = (bf16[1,512,512]{2,1,0:T(8,128)(2,1)S(1)}, bf16[1,512,512]{2,1,0:T(8,128)(2,1)}, u32[]{:S(2)}) copy-start(bf16[1,512,512]{2,1,0:T(8,128)(2,1)} %param.16) | copy-start | bytes 1572868
  7.2 111.6 %all-gather.3.cloned.1.call-start = ((), (), s32[]{:S(2)}) async-start(), calls=%async_computation.6 | async-start | bytes 17301504 | tf_op jit(solution)/shard_map/all_gather | solution.py:345
  10.3 81.6 %copy-start.4 = (bf16[8,8192]{1,0:T(8,128)(2,1)S(1)}, bf16[8,8192]{1,0:T(8,128)(2,1)}, u32[]{:S(2)}) copy-start(bf16[8,8192]{1,0:T(8,128)(2,1)} %param.9) | copy-start | bytes 393220
  10.3 15.0 %collective-permute-start = (f32[256,512]{1,0:T(8,128)S(1)}, f32[256,512]{1,0:T(8,128)S(1)}, u32[]{:S(2)}, u32[]{:S(2)}) collective-permute-start(f32[256,512]{1,0:T(8,128)S(1)} %pad_maximum_fusion), channel_id=1, source_target_pairs={{8,47},{16,54},{17,55},{24,38},{25,63},{26,39},{32,0},{33,1},{34,2... | collective-permute-start | bytes 1572872 | tf_op jit(solution)/shard_map/ppermute | solution.py:342
  72.0 18.2 %all-to-all-start.1 = ((f32[128,1,512]{2,1,0:T(1,128)}), f32[128,1,512]{2,1,0:T(1,128)S(1)}, u32[]{:S(2)}, u32[]{:S(2)}) async-start(f32[128,1,512]{2,1,0:T(1,128)} %reshape.140), calls=%async_computation.1 | async-start | bytes 524288 | tf_op jit(solution)/shard_map/all_to_all | solution.py:28
  118.8 17.3 %copy-start.2 = (bf16[1,1,1,2,128,512]{5,4,3,2,1,0:T(8,128)(2,1)S(1)}, bf16[1,1,1,2,128,512]{5,4,3,2,1,0:T(8,128)(2,1)}, u32[]{:S(2)}) copy-start(bf16[1,1,1,2,128,512]{5,4,3,2,1,0:T(8,128)(2,1)} %param.11) | copy-start | bytes 786436
  129.9 6.3 %collective-permute-start.1 = (f32[8,512]{1,0:T(8,128)S(1)}, f32[8,512]{1,0:T(8,128)S(1)}, u32[]{:S(2)}, u32[]{:S(2)}) collective-permute-start(f32[8,512]{1,0:T(8,128)S(1)} %dynamic-slice_bitcast_fusion), channel_id=1, source_target_pairs={{0,64},{1,65},{2,66},{3,67},{4,68},{5,69},{6,70},{7,71},{8,72},{9,... | collective-permute-start | bytes 49160 | tf_op jit(solution)/shard_map/ppermute | solution.py:368
  147.2 9.9 %all-to-all-start.3 = ((f32[8,8,512]{2,1,0:T(8,128)}), f32[8,8,512]{2,1,0:T(8,128)S(1)}, u32[]{:S(2)}, u32[]{:S(2)}) async-start(f32[8,8,512]{2,1,0:T(8,128)} %broadcast_in_dim.43), calls=%async_computation.3 | async-start | bytes 262144 | tf_op jit(solution)/shard_map/all_to_all | solution.py:28
  177.7 7.1 %collective-permute-start.2 = (f32[8,512]{1,0:T(8,128)S(1)}, f32[8,512]{1,0:T(8,128)S(1)}, u32[]{:S(2)}, u32[]{:S(2)}) collective-permute-start(f32[8,512]{1,0:T(8,128)S(1)} %reduce_sum.29), channel_id=1, source_target_pairs={{64,0},{65,1},{66,2},{67,3},{68,4},{69,5},{70,6},{71,7},{72,8},{73... | collective-permute-start | bytes 49160 | tf_op jit(solution)/shard_map/ppermute | solution.py:378
  193.4 14.9 %copy-start.1 = (bf16[1,512,1024]{2,1,0:T(8,128)(2,1)S(1)}, bf16[1,512,1024]{2,1,0:T(8,128)(2,1)}, u32[]{:S(2)}) copy-start(bf16[1,512,1024]{2,1,0:T(8,128)(2,1)} %param.15) | copy-start | bytes 3145732
  193.4 14.9 %copy-start.3 = (bf16[1,8,512]{2,1,0:T(8,128)(2,1)S(1)}, bf16[1,8,512]{2,1,0:T(8,128)(2,1)}, u32[]{:S(2)}) copy-start(bf16[1,8,512]{2,1,0:T(8,128)(2,1)} %param.14) | copy-start | bytes 24580
  201.1 6.6 %collective-permute-start.3 = (f32[8,8,512]{2,1,0:T(8,128)S(1)}, f32[8,8,512]{2,1,0:T(8,128)S(1)}, u32[]{:S(2)}, u32[]{:S(2)}) collective-permute-start(f32[8,8,512]{2,1,0:T(8,128)S(1)} %broadcast_select_fusion.3), channel_id=1, source_target_pairs={{0,64},{64,0},{1,65},{65,1},{2,66},{66,2},{3,67},{67,3},{4,68},{68... | collective-permute-start | bytes 393224 | tf_op jit(solution)/shard_map/ppermute | solution.py:383
Sparse Core Ops, SparseCore 0:
  26.4 92.4 all-gather.2

commit v4 on v3

--- a/solution.py
+++ b/solution.py
@@ -16,6 +16,7 @@
 COL = ("x", "c")
 PLANE = ("z", "x", "c")
 ALL = ("yh", "yl", "z", "x", "c")
+HALF_ALL = ("yl", "z", "x", "c")
 HALF = 8
 BF = jnp.bfloat16
 F32 = jnp.float32
@@ -160,11 +161,12 @@
         for k in range(i):
             leaf.left[first_tile(i) + k] = self.stage[i % SLOTS, k, :rank].astype(BF)
             leaf.right[leaf.column(k) + i - k - 1] = self.stage[i % SLOTS, k, rank:].astype(BF)
-        self.kept.start(i)
+        self.kept.start(i - 1)
         if i + SLOTS < HALF:
             self.start(i + SLOTS)
 
     def finish(self):
+        self.kept.start(HALF - 1)
         for i in range(HALF):
             self.kept.wait(i)
 
@@ -340,11 +342,6 @@
     leaf_vt = jnp.where(upper, right[1], right[0]).T
     own_tile = with_layout_constraint(jnp.concatenate([leaf_u, leaf_vt], axis=0), ROWS)
     other_tile = lax.ppermute(own_tile, ALL, plane_pairs())
-    share = jnp.where(my_col < in_half, own_tile, other_tile)
-    share = with_layout_constraint(share, ROWS)
-    tiles = lax.all_gather(share, PLANE)
-    place = jnp.stack([lax.axis_index("yl"), half]).astype(jnp.int32)
-
     upward = jnp.einsum("crs,csb->crb", child_x, border_t, preferred_element_type=F32)
     pieces = (
         upward.reshape(n_child, rhs_count, BB, BLK)
@@ -356,11 +353,17 @@
     width = ntile * tile // ndev
     parts = dense.reshape(rhs_count, ndev, width).transpose(1, 0, 2)
     mine = lax.all_to_all(parts, ALL, split_axis=0, concat_axis=0, tiled=True).sum(axis=0)
-    child_sum = copies(mine, ALL).reshape(ndev, rhs_count, width)
-    child_sum = child_sum.transpose(1, 0, 2).reshape(rhs_count, ntile, tile).transpose(1, 0, 2)
-    rhs = root_rhs.reshape(rhs_count, ntile, tile).transpose(1, 0, 2).astype(F32) - child_sum
-
-    own_rhs = lax.dynamic_slice_in_dim(rhs, HALF * half, HALF, 0)
+    other_tile, mine = lax.optimization_barrier((other_tile, mine))
+    share = jnp.where(my_col < in_half, own_tile, other_tile)
+    share = with_layout_constraint(share, ROWS)
+    tiles = lax.all_gather(share, PLANE)
+    place = jnp.stack([lax.axis_index("yl"), half]).astype(jnp.int32)
+    child_sum = copies(mine, HALF_ALL).reshape(ndev // 2, rhs_count, width)
+    child_sum = child_sum.transpose(1, 0, 2).reshape(rhs_count, HALF, tile).transpose(1, 0, 2)
+    given = root_rhs.reshape(rhs_count, ntile, tile)
+    given = lax.dynamic_slice_in_dim(given, HALF * half, HALF, 1)
+    own_rhs = given.transpose(1, 0, 2).astype(F32) - child_sum
+
     x_low, kept_left, kept_right = load_and_forward(place, tiles, diag_inv, own_rhs)
     v0 = right[0].astype(BF)
     u0 = left[0]

time: 218 us -> 220 us (level)
  blocking collectives: 65.3 us -> 27.7 us
  starting transfers between devices: 15.9 us -> 35.8 us
  waiting for transfers between devices: 74 us -> 93.3 us
    all_to_all x1 -> x0, blocking collectives: 37.7 us -> none  [per_device(): lax.all_to_all(parts, ALL, split_axis=0, concat_axis=0, tiled=True)]
    all_gather x1, waiting for transfers between devices: 26.8 us -> 53.9 us  [per_device(): tiles = lax.all_gather(share, PLANE)]
    ppermute x1, waiting for transfers between devices: 13.6 us -> 0.01 us  [per_device(): other_tile = lax.ppermute(own_tile, ALL, plane_pairs())]
    all_to_all x0 -> x1, starting transfers between devices: none -> 12.7 us  [per_device(): lax.all_to_all(parts, ALL, split_axis=0, concat_axis=0, tiled=True)]
    all_to_all x0 -> x1, waiting for transfers between devices: none -> 10.6 us  [per_device(): lax.all_to_all(parts, ALL, split_axis=0, concat_axis=0, tiled=True)]
    all_to_all x2, starting transfers between devices: 8.17 us -> 15.3 us  [copies(): lax.all_to_all(stacked, axis, split_axis=0, concat_axis=0, tiled=True)]
    all_to_all x2, waiting for transfers between devices: 19.8 us -> 14.9 us  [copies(): lax.all_to_all(stacked, axis, split_axis=0, concat_axis=0, tiled=True)]
  transfers between devices with their start and end apart: 7 -> 8, of which waited for: 7 -> 7; matrix products, arithmetic and copies ran while one was open for 5% -> 4% of each run, Pallas kernels for 0% -> 0%
where the time goes in v4:
time: 220 us
  waiting for transfers between devices  93.3 us (42%)
  starting transfers between devices  35.8 us (16%)
  Pallas kernels  30.1 us (14%)
  blocking collectives  27.7 us (13%)
  between operations  14.4 us (7%)
  local copies, waits for them, and re-layouts  8.01 us (4%)
  other arithmetic  7.61 us (3%)
  matrix products  2.76 us (1%)
    all_gather x1, waiting for transfers between devices, per_device(): tiles = lax.all_gather(share, PLANE)  53.9 us
    all_to_all x3, blocking collectives, copies(): lax.all_to_all(stacked, axis, split_axis=0, concat_axis=0, tiled=True)  27.7 us
    pallas_call x2, Pallas kernels, solve(): pl.pallas_call(body, out_shape=jax.ShapeDtypeStruct(rhs.shape, F32), in_s...  18.8 us
    all_to_all x2, starting transfers between devices, copies(): lax.all_to_all(stacked, axis, split_axis=0, concat_axis=0, tiled=True)  15.3 us
    all_to_all x2, waiting for transfers between devices, copies(): lax.all_to_all(stacked, axis, split_axis=0, concat_axis=0, tiled=True)  14.9 us
    all_to_all x1, starting transfers between devices, per_device(): lax.all_to_all(parts, ALL, split_axis=0, concat_axis=0, tiled=True)  12.7 us
    pallas_call x1, Pallas kernels, load_and_forward(): pl.pallas_call(load_kernel, out_shape=(jax.ShapeDtypeStruct(rhs.shape, F3...  11.3 us
    all_to_all x1, waiting for transfers between devices, per_device(): lax.all_to_all(parts, ALL, split_axis=0, concat_axis=0, tiled=True)  10.6 us
  transfers between devices with their start and end apart: 8, of which 7 were waited for; matrix products, arithmetic and copies ran while one was open for 4% of the time, Pallas kernels for 0%

profile of v4, /device:TPU:0, one launch (start us, length us, event | category | flops | bytes accessed | tf_op | source)
XLA Modules:
  0.0 219.6 jit_solution(10934116605148454978)
XLA Ops:
  7.2 0.0 copy-start
  7.2 1.1 copy.27
  8.3 0.7 iota_compare_fusion
  9.1 0.0 copy-start.4
  9.1 0.1 convert_select_fusion
  9.2 1.0 fusion.19
  10.2 0.8 pad_maximum_fusion
  11.1 1.3 collective-permute-start
  12.3 0.7 fusion.41
  13.0 1.5 copy.35
  14.5 1.1 convolution_bitcast_fusion
  15.6 0.8 scatter_fusion
  16.4 0.1 copy.29
  16.5 0.1 reshape.114
  16.6 0.3 copy.30
  16.9 1.0 reshape.138
  17.9 12.7 %all-to-all-start = ((f32[128,1,512]{2,1,0:T(1,128)}), f32[128,1,512]{2,1,0:T(1,128)S(1)}, u32[]{:S(2)}, u32[]{:S(2)}) async-start(f32[128,1,512]{2,1,0:T(1,128)} %reshape.138), calls=%async_computation | async-start | bytes 524288 | tf_op jit(solution)/shard_map/all_to_all | solution.py:355
  30.6 0.0 all-gather.3.cloned.1.call-start
  30.7 10.6 %all-to-all-done = f32[128,1,512]{2,1,0:T(1,128)S(1)} async-done(((f32[128,1,512]{2,1,0:T(1,128)}), f32[128,1,512]{2,1,0:T(1,128)S(1)}, u32[]{:S(2)}, u32[]{:S(2)}) %all-to-all-start) | async-done | bytes 262176 | tf_op jit(solution)/shard_map/all_to_all | solution.py:355
  41.3 0.5 broadcast.43
  41.9 1.2 reduce
  43.1 0.1 reshape.139
  43.2 0.1 reduce_sum.27
  43.4 0.0 collective-permute-done
  43.4 0.9 broadcast_select_fusion
  44.3 0.0 all-gather.3.cloned.1.call-update
  44.3 0.8 reshape.140
  45.2 11.9 %all-to-all-start.1 = ((f32[64,1,512]{2,1,0:T(1,128)}), f32[64,1,512]{2,1,0:T(1,128)S(1)}, u32[]{:S(2)}, u32[]{:S(2)}) async-start(f32[64,1,512]{2,1,0:T(1,128)} %reshape.140), calls=%async_computation.1 | async-start | bytes 262144 | tf_op jit(solution)/shard_map/all_to_all | solution.py:29
  57.1 0.1 pad_add_fusion.place
  57.1 8.4 %all-to-all-done.1 = f32[64,1,512]{2,1,0:T(1,128)S(1)} async-done(((f32[64,1,512]{2,1,0:T(1,128)}), f32[64,1,512]{2,1,0:T(1,128)S(1)}, u32[]{:S(2)}, u32[]{:S(2)}) %all-to-all-start.1) | async-done | bytes 131104 | tf_op jit(solution)/shard_map/all_to_all | solution.py:29
  65.5 0.9 reduce.1
  66.5 0.1 reshape.141
  66.6 0.1 copy.31
  66.6 0.1 reshape.116
  66.7 0.0 copy-done.4
  66.7 0.1 fusion.20.rhs
  66.8 53.9 %all-gather.3.cloned.1.call-done = f32[8192,512]{1,0:T(8,128)} async-done(((f32[256,512]{1,0:T(8,128)}), f32[8192,512]{1,0:T(8,128)}) %all-gather.3.cloned.1.call-update) | async-done | bytes 16777232 | tf_op jit(solution)/shard_map/all_gather | solution.py:359
  120.8 0.0 copy-start.2
  120.8 11.3 %shard_map.104 = (f32[8,8,512]{2,1,0:T(8,128)S(1)}, bf16[28,128,512]{2,1,0:T(8,128)(2,1)}, bf16[28,128,512]{2,1,0:T(8,128)(2,1)}) custom-call(s32[2]{0:T(128)S(1)} %pad_add_fusion.place, f32[32,256,512]{2,1,0:T(8,128)} %bitcast.74, bf16[16,512,512]{2,1,0:T(8,128)(2,1)} %inv.5, f32[8,8,512]{2,1,0:T(8,128)S(1)} %fusion.20.rhs), custom_call_target="tpu_custom_call" | custom-call | tf_op jit(solution)/shard_map/pallas_call | solution.py:295
  132.1 4.9 %collective-permute-start.1 = (f32[8,512]{1,0:T(8,128)S(1)}, f32[8,512]{1,0:T(8,128)S(1)}, u32[]{:S(2)}, u32[]{:S(2)}) collective-permute-start(f32[8,512]{1,0:T(8,128)S(1)} %dynamic-slice_bitcast_fusion), channel_id=1, source_target_pairs={{0,64},{1,65},{2,66},{3,67},{4,68},{5,69},{6,70},{7,71},{8,72},{9,... | collective-permute-start | bytes 49160 | tf_op jit(solution)/shard_map/ppermute | solution.py:371
  137.0 1.4 collective-permute-done.1
  138.5 0.0 copy-done.2
  138.5 0.3 fusion.9
  138.8 10.2 %all_to_all.30 = f32[8,8,512]{2,1,0:T(8,128)S(1)} all-to-all(f32[8,8,512]{2,1,0:T(8,128)S(1)} %broadcast_in_dim.42), channel_id=1, replica_groups=mesh['yh'=2,'yl'=2,'z'=4,'x'=4,'c'=2] {'x','c'}, dimensions={0} | all-to-all | bytes 262144 | tf_op jit(solution)/shard_map/all_to_all | solution.py:29
  149.0 0.7 broadcast_in_dim.43
  149.6 3.4 %all-to-all-start.3 = ((f32[8,8,512]{2,1,0:T(8,128)}), f32[8,8,512]{2,1,0:T(8,128)S(1)}, u32[]{:S(2)}, u32[]{:S(2)}) async-start(f32[8,8,512]{2,1,0:T(8,128)} %broadcast_in_dim.43), calls=%async_computation.3 | async-start | bytes 262144 | tf_op jit(solution)/shard_map/all_to_all | solution.py:29
  153.0 6.5 %all-to-all-done.3 = f32[8,8,512]{2,1,0:T(8,128)S(1)} async-done(((f32[8,8,512]{2,1,0:T(8,128)}), f32[8,8,512]{2,1,0:T(8,128)S(1)}, u32[]{:S(2)}, u32[]{:S(2)}) %all-to-all-start.3) | async-done | bytes 131104 | tf_op jit(solution)/shard_map/all_to_all | solution.py:29
  159.5 11.2 %shard_map.105 = f32[8,8,512]{2,1,0:T(8,128)S(1)} custom-call(s32[2]{0:T(128)S(1)} %pad_add_fusion.place, bf16[28,128,512]{2,1,0:T(8,128)(2,1)} %get-tuple-element.9.kept_left, bf16[28,128,512]{2,1,0:T(8,128)(2,1)} %get-tuple-element.10.kept_right, bf16[16,512,512]{2,1,0:T(8,128)(2,1)} %inv.5, f32[8,8,512]{2,1,0:T(8,128)S(1)} %sub.16.rhs), custom_call_target="tpu_custom_call" | custom-call | tf_op jit(solution)/shard_map/pallas_call | solution.py:311
  170.7 0.3 fusion.10
  171.0 9.1 %all_to_all.31 = f32[8,8,512]{2,1,0:T(8,128)S(1)} all-to-all(f32[8,8,512]{2,1,0:T(8,128)S(1)} %broadcast_in_dim.44), channel_id=1, replica_groups=mesh['yh'=2,'yl'=2,'z'=4,'x'=4,'c'=2] {'yl','z'}, dimensions={0} | all-to-all | bytes 262144 | tf_op jit(solution)/shard_map/all_to_all | solution.py:29
  180.1 1.5 collective-permute-start.2
  181.6 5.8 %collective-permute-done.2 = f32[8,512]{1,0:T(8,128)S(1)} collective-permute-done((f32[8,512]{1,0:T(8,128)S(1)}, f32[8,512]{1,0:T(8,128)S(1)}, u32[]{:S(2)}, u32[]{:S(2)}) %collective-permute-start.2) | collective-permute-done | bytes 16416 | tf_op jit(solution)/shard_map/ppermute | solution.py:381
  187.5 8.5 %all_to_all.32 = f32[8,8,512]{2,1,0:T(8,128)S(1)} all-to-all(f32[8,8,512]{2,1,0:T(8,128)S(1)} %broadcast_in_dim.45), channel_id=1, replica_groups=mesh['yh'=2,'yl'=2,'z'=4,'x'=4,'c'=2] {'x','c'}, dimensions={0} | all-to-all | bytes 262144 | tf_op jit(solution)/shard_map/all_to_all | solution.py:29
  196.0 0.0 copy-start.1
  196.0 0.0 copy-start.3
  196.0 7.6 %shard_map.106 = f32[8,8,512]{2,1,0:T(8,128)S(1)} custom-call(s32[2]{0:T(128)S(1)} %pad_add_fusion.place, bf16[28,128,512]{2,1,0:T(8,128)(2,1)} %get-tuple-element.9.kept_left, bf16[28,128,512]{2,1,0:T(8,128)(2,1)} %get-tuple-element.10.kept_right, bf16[16,512,512]{2,1,0:T(8,128)(2,1)} %inv.5, f32[8,8,512]{2,1,0:T(8,128)S(1)} %sub.17.rhs), custom_call_target="tpu_custom_call" | custom-call | tf_op jit(solution)/shard_map/pallas_call | solution.py:311
  203.7 0.1 collective-permute-start.3
  203.8 6.5 %collective-permute-done.3 = f32[8,8,512]{2,1,0:T(8,128)S(1)} collective-permute-done((f32[8,8,512]{2,1,0:T(8,128)S(1)}, f32[8,8,512]{2,1,0:T(8,128)S(1)}, u32[]{:S(2)}, u32[]{:S(2)}) %collective-permute-start.3) | collective-permute-done | bytes 131104 | tf_op jit(solution)/shard_map/ppermute | solution.py:386
  210.3 0.6 gather_fusion
  210.9 0.0 copy-done
  210.9 0.0 copy-done.1
  210.9 0.0 copy-done.3
  210.9 1.1 fusion.6
  212.1 0.7 constant_dynamic-slice_fusion
  (15 shorter events, 0.3 us)
Async XLA Ops:
  7.2 203.7 %copy-start = (bf16[1,512,512]{2,1,0:T(8,128)(2,1)S(1)}, bf16[1,512,512]{2,1,0:T(8,128)(2,1)}, u32[]{:S(2)}) copy-start(bf16[1,512,512]{2,1,0:T(8,128)(2,1)} %param.16) | copy-start | bytes 1572868
  9.1 57.7 %copy-start.4 = (bf16[8,8192]{1,0:T(8,128)(2,1)S(1)}, bf16[8,8192]{1,0:T(8,128)(2,1)}, u32[]{:S(2)}) copy-start(bf16[8,8192]{1,0:T(8,128)(2,1)} %param.9) | copy-start | bytes 393220
  11.1 32.3 %collective-permute-start = (f32[256,512]{1,0:T(8,128)}, f32[256,512]{1,0:T(8,128)S(1)}, u32[]{:S(2)}, u32[]{:S(2)}) collective-permute-start(f32[256,512]{1,0:T(8,128)} %pad_maximum_fusion), channel_id=1, source_target_pairs={{8,47},{16,54},{17,55},{24,38},{25,63},{26,39},{32,0},{33,1},{34,2... | collective-permute-start | bytes 1572872 | tf_op jit(solution)/shard_map/ppermute | solution.py:344
  17.9 23.4 %all-to-all-start = ((f32[128,1,512]{2,1,0:T(1,128)}), f32[128,1,512]{2,1,0:T(1,128)S(1)}, u32[]{:S(2)}, u32[]{:S(2)}) async-start(f32[128,1,512]{2,1,0:T(1,128)} %reshape.138), calls=%async_computation | async-start | bytes 524288 | tf_op jit(solution)/shard_map/all_to_all | solution.py:355
  30.6 90.2 %all-gather.3.cloned.1.call-start = ((), (), s32[]{:S(2)}) async-start(), calls=%async_computation.6 | async-start | bytes 17301504 | tf_op jit(solution)/shard_map/all_gather | solution.py:359
  45.2 20.4 %all-to-all-start.1 = ((f32[64,1,512]{2,1,0:T(1,128)}), f32[64,1,512]{2,1,0:T(1,128)S(1)}, u32[]{:S(2)}, u32[]{:S(2)}) async-start(f32[64,1,512]{2,1,0:T(1,128)} %reshape.140), calls=%async_computation.1 | async-start | bytes 262144 | tf_op jit(solution)/shard_map/all_to_all | solution.py:29
  120.8 17.7 %copy-start.2 = (bf16[1,1,1,2,128,512]{5,4,3,2,1,0:T(8,128)(2,1)S(1)}, bf16[1,1,1,2,128,512]{5,4,3,2,1,0:T(8,128)(2,1)}, u32[]{:S(2)}) copy-start(bf16[1,1,1,2,128,512]{5,4,3,2,1,0:T(8,128)(2,1)} %param.11) | copy-start | bytes 786436
  132.1 6.4 %collective-permute-start.1 = (f32[8,512]{1,0:T(8,128)S(1)}, f32[8,512]{1,0:T(8,128)S(1)}, u32[]{:S(2)}, u32[]{:S(2)}) collective-permute-start(f32[8,512]{1,0:T(8,128)S(1)} %dynamic-slice_bitcast_fusion), channel_id=1, source_target_pairs={{0,64},{1,65},{2,66},{3,67},{4,68},{5,69},{6,70},{7,71},{8,72},{9,... | collective-permute-start | bytes 49160 | tf_op jit(solution)/shard_map/ppermute | solution.py:371
  149.6 9.9 %all-to-all-start.3 = ((f32[8,8,512]{2,1,0:T(8,128)}), f32[8,8,512]{2,1,0:T(8,128)S(1)}, u32[]{:S(2)}, u32[]{:S(2)}) async-start(f32[8,8,512]{2,1,0:T(8,128)} %broadcast_in_dim.43), calls=%async_computation.3 | async-start | bytes 262144 | tf_op jit(solution)/shard_map/all_to_all | solution.py:29
  180.1 7.3 %collective-permute-start.2 = (f32[8,512]{1,0:T(8,128)S(1)}, f32[8,512]{1,0:T(8,128)S(1)}, u32[]{:S(2)}, u32[]{:S(2)}) collective-permute-start(f32[8,512]{1,0:T(8,128)S(1)} %reduce_sum.29), channel_id=1, source_target_pairs={{64,0},{65,1},{66,2},{67,3},{68,4},{69,5},{70,6},{71,7},{72,8},{73... | collective-permute-start | bytes 49160 | tf_op jit(solution)/shard_map/ppermute | solution.py:381
  196.0 14.9 %copy-start.1 = (bf16[1,512,1024]{2,1,0:T(8,128)(2,1)S(1)}, bf16[1,512,1024]{2,1,0:T(8,128)(2,1)}, u32[]{:S(2)}) copy-start(bf16[1,512,1024]{2,1,0:T(8,128)(2,1)} %param.15) | copy-start | bytes 3145732
  196.0 14.9 %copy-start.3 = (bf16[1,8,512]{2,1,0:T(8,128)(2,1)S(1)}, bf16[1,8,512]{2,1,0:T(8,128)(2,1)}, u32[]{:S(2)}) copy-start(bf16[1,8,512]{2,1,0:T(8,128)(2,1)} %param.14) | copy-start | bytes 24580
  203.7 6.6 %collective-permute-start.3 = (f32[8,8,512]{2,1,0:T(8,128)S(1)}, f32[8,8,512]{2,1,0:T(8,128)S(1)}, u32[]{:S(2)}, u32[]{:S(2)}) collective-permute-start(f32[8,8,512]{2,1,0:T(8,128)S(1)} %broadcast_select_fusion.3), channel_id=1, source_target_pairs={{0,64},{64,0},{1,65},{65,1},{2,66},{66,2},{3,67},{67,3},{4,68},{68... | collective-permute-start | bytes 393224 | tf_op jit(solution)/shard_map/ppermute | solution.py:386
Sparse Core Ops, SparseCore 0:
  44.4 76.3 all-gather.2

commit v5 on v4

--- a/solution.py
+++ b/solution.py
@@ -1,5 +1,3 @@
-import functools
-
 import jax
 import jax.numpy as jnp
 from jax import lax
@@ -352,8 +350,8 @@
     dense = jnp.zeros((rhs_count, nblk, BLK), F32).at[:, flat_blocks, :].add(pieces)
     width = ntile * tile // ndev
     parts = dense.reshape(rhs_count, ndev, width).transpose(1, 0, 2)
-    mine = lax.all_to_all(parts, ALL, split_axis=0, concat_axis=0, tiled=True).sum(axis=0)
-    other_tile, mine = lax.optimization_barrier((other_tile, mine))
+    mine = lax.all_to_all(parts, ALL, split_axis=0, concat_axis=0, tiled=True)
+    mine = mine.sum(axis=0)
     share = jnp.where(my_col < in_half, own_tile, other_tile)
     share = with_layout_constraint(share, ROWS)
     tiles = lax.all_gather(share, PLANE)

time: 220 us -> 216 us (0.982)
  blocking collectives: 27.7 us -> 65.1 us
  starting transfers between devices: 35.8 us -> 15.3 us
  waiting for transfers between devices: 93.3 us -> 73.5 us
    all_to_all x0 -> x1, blocking collectives: none -> 37.7 us  [per_device(): mine = lax.all_to_all(parts, ALL, split_axis=0, concat_axis=0, tiled=True)]
    all_gather x1, waiting for transfers between devices: 53.9 us -> 30 us  [per_device(): tiles = lax.all_gather(share, PLANE)]
    ppermute x1, waiting for transfers between devices: 0.01 us -> 13.6 us  [per_device(): other_tile = lax.ppermute(own_tile, ALL, plane_pairs())]
    all_to_all x1 -> x0, starting transfers between devices: 12.7 us -> none  [per_device(): lax.all_to_all(parts, ALL, split_axis=0, concat_axis=0, tiled=True)]
    all_to_all x1 -> x0, waiting for transfers between devices: 10.6 us -> none  [per_device(): lax.all_to_all(parts, ALL, split_axis=0, concat_axis=0, tiled=True)]
    all_to_all x2, starting transfers between devices: 15.3 us -> 7.99 us  [copies(): lax.all_to_all(stacked, axis, split_axis=0, concat_axis=0, tiled=True)]
  transfers between devices with their start and end apart: 8 -> 7, of which waited for: 7 -> 7; matrix products, arithmetic and copies ran while one was open for 4% -> 4% of each run, Pallas kernels for 0% -> 0%
where the time goes in v5:
time: 216 us; the launch traced here: 215 us
  waiting for transfers between devices  73.5 us (34%)
  blocking collectives  65.1 us (30%)
  Pallas kernels  30.1 us (14%)
  starting transfers between devices  15.3 us (7%)
  between operations  14.4 us (7%)
  local copies, waits for them, and re-layouts  7.31 us (3%)
  other arithmetic  6.85 us (3%)
  matrix products  2.77 us (1%)
    all_to_all x1, blocking collectives, per_device(): mine = lax.all_to_all(parts, ALL, split_axis=0, concat_axis=0, tiled=True)  37.7 us
    all_gather x1, waiting for transfers between devices, per_device(): tiles = lax.all_gather(share, PLANE)  30 us
    all_to_all x3, blocking collectives, copies(): lax.all_to_all(stacked, axis, split_axis=0, concat_axis=0, tiled=True)  27.5 us
    pallas_call x2, Pallas kernels, solve(): pl.pallas_call(body, out_shape=jax.ShapeDtypeStruct(rhs.shape, F32), in_s...  18.8 us
    all_to_all x2, waiting for transfers between devices, copies(): lax.all_to_all(stacked, axis, split_axis=0, concat_axis=0, tiled=True)  16.1 us
    ppermute x1, waiting for transfers between devices, per_device(): other_tile = lax.ppermute(own_tile, ALL, plane_pairs())  13.6 us
    pallas_call x1, Pallas kernels, load_and_forward(): pl.pallas_call(load_kernel, out_shape=(jax.ShapeDtypeStruct(rhs.shape, F3...  11.3 us
    all_to_all x2, starting transfers between devices, copies(): lax.all_to_all(stacked, axis, split_axis=0, concat_axis=0, tiled=True)  7.99 us
  transfers between devices with their start and end apart: 7, of which 7 were waited for; matrix products, arithmetic and copies ran while one was open for 4% of the time, Pallas kernels for 0%

profile of v5, /device:TPU:0, one launch (start us, length us, event | category | flops | bytes accessed | tf_op | source)
XLA Modules:
  0.0 215.4 jit_solution(7907706766240213291)
XLA Ops:
  7.2 0.0 copy-start
  7.2 0.0 all-gather.3.cloned.1.call-start
  7.2 1.1 copy.27
  8.4 0.7 iota_compare_fusion
  9.1 0.0 copy-start.4
  9.1 0.1 convert_select_fusion
  9.3 1.0 fusion.19
  10.3 1.3 collective-permute-start
  11.6 13.6 %collective-permute-done = f32[256,512]{1,0:T(8,128)S(1)} collective-permute-done((f32[256,512]{1,0:T(8,128)S(1)}, f32[256,512]{1,0:T(8,128)S(1)}, u32[]{:S(2)}, u32[]{:S(2)}) %collective-permute-start) | collective-permute-done | bytes 524320 | tf_op jit(solution)/shard_map/ppermute | solution.py:342
  25.2 0.9 broadcast_select_fusion
  26.1 0.0 all-gather.3.cloned.1.call-update
  26.1 1.5 copy.35
  27.6 0.7 fusion.41
  28.3 1.1 convolution_bitcast_fusion
  29.4 0.8 scatter_fusion
  30.2 0.1 copy.29
  30.2 0.1 reshape.115
  30.4 0.3 copy.30
  30.7 0.3 reshape.138
  31.0 37.7 %all_to_all.30 = f32[128,1,512]{2,1,0:T(1,128)S(1)} all-to-all(f32[128,1,512]{2,1,0:T(1,128)S(1)} %reshape.138), channel_id=1, replica_groups=mesh['yh'=2,'yl'=2,'z'=4,'x'=4,'c'=2] {'yh','yl','z','x','c'}, dimensions={0} | all-to-all | bytes 524288 | tf_op jit(solution)/shard_map/all_to_all | solution.py:353
  68.7 0.5 broadcast.43
  69.2 1.2 reduce
  70.5 0.1 reshape.139
  70.6 0.1 reduce_sum.27
  70.8 0.8 reshape.140
  71.6 4.6 %all-to-all-start.1 = ((f32[64,1,512]{2,1,0:T(1,128)}), f32[64,1,512]{2,1,0:T(1,128)S(1)}, u32[]{:S(2)}, u32[]{:S(2)}) async-start(f32[64,1,512]{2,1,0:T(1,128)} %reshape.140), calls=%async_computation.1 | async-start | bytes 262144 | tf_op jit(solution)/shard_map/all_to_all | solution.py:27
  76.3 0.1 pad_add_fusion.place
  76.3 9.6 %all-to-all-done.1 = f32[64,1,512]{2,1,0:T(1,128)S(1)} async-done(((f32[64,1,512]{2,1,0:T(1,128)}), f32[64,1,512]{2,1,0:T(1,128)S(1)}, u32[]{:S(2)}, u32[]{:S(2)}) %all-to-all-start.1) | async-done | bytes 131104 | tf_op jit(solution)/shard_map/all_to_all | solution.py:27
  85.9 0.9 reduce.1
  86.9 0.1 reshape.141
  87.0 0.1 copy.31
  87.0 0.1 reshape.116
  87.2 0.0 copy-done.4
  87.2 0.1 fusion.20.rhs
  87.3 30.0 %all-gather.3.cloned.1.call-done = f32[8192,512]{1,0:T(8,128)} async-done(((f32[256,512]{1,0:T(8,128)}), f32[8192,512]{1,0:T(8,128)}) %all-gather.3.cloned.1.call-update) | async-done | bytes 16777232 | tf_op jit(solution)/shard_map/all_gather | solution.py:357
  117.3 0.0 copy-start.2
  117.3 11.3 %shard_map.104 = (f32[8,8,512]{2,1,0:T(8,128)S(1)}, bf16[28,128,512]{2,1,0:T(8,128)(2,1)}, bf16[28,128,512]{2,1,0:T(8,128)(2,1)}) custom-call(s32[2]{0:T(128)S(1)} %pad_add_fusion.place, f32[32,256,512]{2,1,0:T(8,128)} %bitcast.74, bf16[16,512,512]{2,1,0:T(8,128)(2,1)} %inv.5, f32[8,8,512]{2,1,0:T(8,128)S(1)} %fusion.20.rhs), custom_call_target="tpu_custom_call" | custom-call | tf_op jit(solution)/shard_map/pallas_call | solution.py:293
  128.6 4.6 %collective-permute-start.1 = (f32[8,512]{1,0:T(8,128)S(1)}, f32[8,512]{1,0:T(8,128)S(1)}, u32[]{:S(2)}, u32[]{:S(2)}) collective-permute-start(f32[8,512]{1,0:T(8,128)S(1)} %dynamic-slice_bitcast_fusion), channel_id=1, source_target_pairs={{0,64},{1,65},{2,66},{3,67},{4,68},{5,69},{6,70},{7,71},{8,72},{9,... | collective-permute-start | bytes 49160 | tf_op jit(solution)/shard_map/ppermute | solution.py:369
  133.2 1.4 collective-permute-done.1
  134.7 0.0 copy-done.2
  134.7 0.3 fusion.9
  135.0 9.9 %all_to_all.31 = f32[8,8,512]{2,1,0:T(8,128)S(1)} all-to-all(f32[8,8,512]{2,1,0:T(8,128)S(1)} %broadcast_in_dim.42), channel_id=1, replica_groups=mesh['yh'=2,'yl'=2,'z'=4,'x'=4,'c'=2] {'x','c'}, dimensions={0} | all-to-all | bytes 262144 | tf_op jit(solution)/shard_map/all_to_all | solution.py:27
  144.9 0.7 broadcast_in_dim.43
  145.6 3.4 %all-to-all-start.3 = ((f32[8,8,512]{2,1,0:T(8,128)}), f32[8,8,512]{2,1,0:T(8,128)S(1)}, u32[]{:S(2)}, u32[]{:S(2)}) async-start(f32[8,8,512]{2,1,0:T(8,128)} %broadcast_in_dim.43), calls=%async_computation.3 | async-start | bytes 262144 | tf_op jit(solution)/shard_map/all_to_all | solution.py:27
  148.9 6.5 %all-to-all-done.3 = f32[8,8,512]{2,1,0:T(8,128)S(1)} async-done(((f32[8,8,512]{2,1,0:T(8,128)}), f32[8,8,512]{2,1,0:T(8,128)S(1)}, u32[]{:S(2)}, u32[]{:S(2)}) %all-to-all-start.3) | async-done | bytes 131104 | tf_op jit(solution)/shard_map/all_to_all | solution.py:27
  155.5 11.2 %shard_map.105 = f32[8,8,512]{2,1,0:T(8,128)S(1)} custom-call(s32[2]{0:T(128)S(1)} %pad_add_fusion.place, bf16[28,128,512]{2,1,0:T(8,128)(2,1)} %get-tuple-element.5.kept_left, bf16[28,128,512]{2,1,0:T(8,128)(2,1)} %get-tuple-element.6.kept_right, bf16[16,512,512]{2,1,0:T(8,128)(2,1)} %inv.5, f32[8,8,512]{2,1,0:T(8,128)S(1)} %sub.16.rhs), custom_call_target="tpu_custom_call" | custom-call | tf_op jit(solution)/shard_map/pallas_call | solution.py:309
  166.7 0.3 fusion.10
  167.0 9.1 %all_to_all.32 = f32[8,8,512]{2,1,0:T(8,128)S(1)} all-to-all(f32[8,8,512]{2,1,0:T(8,128)S(1)} %broadcast_in_dim.44), channel_id=1, replica_groups=mesh['yh'=2,'yl'=2,'z'=4,'x'=4,'c'=2] {'yl','z'}, dimensions={0} | all-to-all | bytes 262144 | tf_op jit(solution)/shard_map/all_to_all | solution.py:27
  176.1 1.3 collective-permute-start.2
  177.4 5.8 %collective-permute-done.2 = f32[8,512]{1,0:T(8,128)S(1)} collective-permute-done((f32[8,512]{1,0:T(8,128)S(1)}, f32[8,512]{1,0:T(8,128)S(1)}, u32[]{:S(2)}, u32[]{:S(2)}) %collective-permute-start.2) | collective-permute-done | bytes 16416 | tf_op jit(solution)/shard_map/ppermute | solution.py:379
  183.2 8.5 %all_to_all.33 = f32[8,8,512]{2,1,0:T(8,128)S(1)} all-to-all(f32[8,8,512]{2,1,0:T(8,128)S(1)} %broadcast_in_dim.45), channel_id=1, replica_groups=mesh['yh'=2,'yl'=2,'z'=4,'x'=4,'c'=2] {'x','c'}, dimensions={0} | all-to-all | bytes 262144 | tf_op jit(solution)/shard_map/all_to_all | solution.py:27
  191.7 0.0 copy-start.1
  191.8 0.0 copy-start.3
  191.8 7.6 %shard_map.106 = f32[8,8,512]{2,1,0:T(8,128)S(1)} custom-call(s32[2]{0:T(128)S(1)} %pad_add_fusion.place, bf16[28,128,512]{2,1,0:T(8,128)(2,1)} %get-tuple-element.5.kept_left, bf16[28,128,512]{2,1,0:T(8,128)(2,1)} %get-tuple-element.6.kept_right, bf16[16,512,512]{2,1,0:T(8,128)(2,1)} %inv.5, f32[8,8,512]{2,1,0:T(8,128)S(1)} %sub.17.rhs), custom_call_target="tpu_custom_call" | custom-call | tf_op jit(solution)/shard_map/pallas_call | solution.py:309
  199.4 0.1 collective-permute-start.3
  199.5 6.5 %collective-permute-done.3 = f32[8,8,512]{2,1,0:T(8,128)S(1)} collective-permute-done((f32[8,8,512]{2,1,0:T(8,128)S(1)}, f32[8,8,512]{2,1,0:T(8,128)S(1)}, u32[]{:S(2)}, u32[]{:S(2)}) %collective-permute-start.3) | collective-permute-done | bytes 131104 | tf_op jit(solution)/shard_map/ppermute | solution.py:384
  206.1 0.6 gather_fusion
  206.7 0.0 copy-done
  206.7 0.0 copy-done.1
  206.7 0.0 copy-done.3
  206.7 1.1 fusion.6
  207.8 0.7 constant_dynamic-slice_fusion
  (16 shorter events, 0.4 us)
Async XLA Ops:
  7.2 199.5 %copy-start = (bf16[1,512,512]{2,1,0:T(8,128)(2,1)S(1)}, bf16[1,512,512]{2,1,0:T(8,128)(2,1)}, u32[]{:S(2)}) copy-start(bf16[1,512,512]{2,1,0:T(8,128)(2,1)} %param.16) | copy-start | bytes 1572868
  7.2 110.1 %all-gather.3.cloned.1.call-start = ((), (), s32[]{:S(2)}) async-start(), calls=%async_computation.6 | async-start | bytes 17301504 | tf_op jit(solution)/shard_map/all_gather | solution.py:357
  9.1 78.1 %copy-start.4 = (bf16[8,8192]{1,0:T(8,128)(2,1)S(1)}, bf16[8,8192]{1,0:T(8,128)(2,1)}, u32[]{:S(2)}) copy-start(bf16[8,8192]{1,0:T(8,128)(2,1)} %param.9) | copy-start | bytes 393220
  10.3 14.9 %collective-permute-start = (f32[256,512]{1,0:T(8,128)S(1)}, f32[256,512]{1,0:T(8,128)S(1)}, u32[]{:S(2)}, u32[]{:S(2)}) collective-permute-start(f32[256,512]{1,0:T(8,128)S(1)} %pad_maximum_fusion), channel_id=1, source_target_pairs={{8,47},{16,54},{17,55},{24,38},{25,63},{26,39},{32,0},{33,1},{34,2... | collective-permute-start | bytes 1572872 | tf_op jit(solution)/shard_map/ppermute | solution.py:342
  71.6 14.3 %all-to-all-start.1 = ((f32[64,1,512]{2,1,0:T(1,128)}), f32[64,1,512]{2,1,0:T(1,128)S(1)}, u32[]{:S(2)}, u32[]{:S(2)}) async-start(f32[64,1,512]{2,1,0:T(1,128)} %reshape.140), calls=%async_computation.1 | async-start | bytes 262144 | tf_op jit(solution)/shard_map/all_to_all | solution.py:27
  117.3 17.4 %copy-start.2 = (bf16[1,1,1,2,128,512]{5,4,3,2,1,0:T(8,128)(2,1)S(1)}, bf16[1,1,1,2,128,512]{5,4,3,2,1,0:T(8,128)(2,1)}, u32[]{:S(2)}) copy-start(bf16[1,1,1,2,128,512]{5,4,3,2,1,0:T(8,128)(2,1)} %param.11) | copy-start | bytes 786436
  128.6 6.0 %collective-permute-start.1 = (f32[8,512]{1,0:T(8,128)S(1)}, f32[8,512]{1,0:T(8,128)S(1)}, u32[]{:S(2)}, u32[]{:S(2)}) collective-permute-start(f32[8,512]{1,0:T(8,128)S(1)} %dynamic-slice_bitcast_fusion), channel_id=1, source_target_pairs={{0,64},{1,65},{2,66},{3,67},{4,68},{5,69},{6,70},{7,71},{8,72},{9,... | collective-permute-start | bytes 49160 | tf_op jit(solution)/shard_map/ppermute | solution.py:369
  145.6 9.9 %all-to-all-start.3 = ((f32[8,8,512]{2,1,0:T(8,128)}), f32[8,8,512]{2,1,0:T(8,128)S(1)}, u32[]{:S(2)}, u32[]{:S(2)}) async-start(f32[8,8,512]{2,1,0:T(8,128)} %broadcast_in_dim.43), calls=%async_computation.3 | async-start | bytes 262144 | tf_op jit(solution)/shard_map/all_to_all | solution.py:27
  176.1 7.1 %collective-permute-start.2 = (f32[8,512]{1,0:T(8,128)S(1)}, f32[8,512]{1,0:T(8,128)S(1)}, u32[]{:S(2)}, u32[]{:S(2)}) collective-permute-start(f32[8,512]{1,0:T(8,128)S(1)} %reduce_sum.29), channel_id=1, source_target_pairs={{64,0},{65,1},{66,2},{67,3},{68,4},{69,5},{70,6},{71,7},{72,8},{73... | collective-permute-start | bytes 49160 | tf_op jit(solution)/shard_map/ppermute | solution.py:379
  191.7 14.9 %copy-start.1 = (bf16[1,512,1024]{2,1,0:T(8,128)(2,1)S(1)}, bf16[1,512,1024]{2,1,0:T(8,128)(2,1)}, u32[]{:S(2)}) copy-start(bf16[1,512,1024]{2,1,0:T(8,128)(2,1)} %param.15) | copy-start | bytes 3145732
  191.8 14.9 %copy-start.3 = (bf16[1,8,512]{2,1,0:T(8,128)(2,1)S(1)}, bf16[1,8,512]{2,1,0:T(8,128)(2,1)}, u32[]{:S(2)}) copy-start(bf16[1,8,512]{2,1,0:T(8,128)(2,1)} %param.14) | copy-start | bytes 24580
  199.4 6.6 %collective-permute-start.3 = (f32[8,8,512]{2,1,0:T(8,128)S(1)}, f32[8,8,512]{2,1,0:T(8,128)S(1)}, u32[]{:S(2)}, u32[]{:S(2)}) collective-permute-start(f32[8,8,512]{2,1,0:T(8,128)S(1)} %broadcast_select_fusion.3), channel_id=1, source_target_pairs={{0,64},{64,0},{1,65},{65,1},{2,66},{66,2},{3,67},{67,3},{4,68},{68... | collective-permute-start | bytes 393224 | tf_op jit(solution)/shard_map/ppermute | solution.py:384
Sparse Core Ops, SparseCore 0:
  26.2 91.0 all-gather.2

commit v6 on v5

--- a/solution.py
+++ b/solution.py
@@ -188,21 +188,24 @@
     partial = rhs[0]
     last = None
     for i in range(HALF):
+        following = None
+        if i + 1 < HALF:
+            if load:
+                load(i + 1)
+            folded = dot_nt(leaf.vt(i + 1, i), leaf.diag[i]).astype(BF)
+            following = rhs[i + 1]
+            if i:
+                known = [dot_nt(narrow[k], leaf.vt(i + 1, k)).astype(BF) for k in range(i)]
+                following = following - dot_nn(jnp.concatenate(known, axis=1), leaf.u(i + 1, 0, i))
         acc = partial
         if i:
             acc = acc - dot_nn(last, leaf.u(i, i - 1))
+        if i + 1 < HALF:
+            last = dot_nt(acc.astype(BF), folded).astype(BF)
         x = exact(dot_nn, acc, leaf.diag[i])
-        if i + 1 < HALF:
-            if load:
-                load(i + 1)
-            partial = rhs[i + 1]
-            if i:
-                known = [dot_nt(narrow[k], leaf.vt(i + 1, k)).astype(BF) for k in range(i)]
-                partial = partial - dot_nn(jnp.concatenate(known, axis=1), leaf.u(i + 1, 0, i))
         solved.append(x)
         narrow.append(x.astype(BF))
-        if i + 1 < HALF:
-            last = dot_nt(narrow[i], leaf.vt(i + 1, i)).astype(BF)
+        partial = following
     return solved
 
 
@@ -213,25 +216,27 @@
     partial = rhs[HALF - 1]
     last = None
     for j in reversed(range(HALF)):
+        following = None
+        if j:
+            if load:
+                load(j - 1)
+            folded = dot_nn(leaf.u(j, j - 1), leaf.diag[j]).astype(BF)
+            following = rhs[j - 1]
+            if waiting[j - 1]:
+                known = jnp.concatenate(waiting[j - 1][::-1], axis=1)
+                following = following - dot_nn(known, leaf.vt(j + 1, j - 1, HALF - 1 - j))
         acc = partial
         if j + 1 < HALF:
             acc = acc - dot_nn(last, leaf.vt(j + 1, j))
+        if j:
+            last = dot_nt(acc.astype(BF), folded).astype(BF)
         z = exact(dot_nt, acc, leaf.diag[j])
-        if j:
-            if load:
-                load(j - 1)
-            partial = rhs[j - 1]
-            if waiting[j - 1]:
-                known = jnp.concatenate(waiting[j - 1][::-1], axis=1)
-                partial = partial - dot_nn(known, leaf.vt(j + 1, j - 1, HALF - 1 - j))
         solved[j] = z
-        narrow = z.astype(BF)
-        if j:
-            last = dot_nt(narrow, leaf.u(j, j - 1)).astype(BF)
         if j > 1:
-            others = dot_nt(narrow, leaf.u(j, 0, j - 1)).astype(BF)
+            others = dot_nt(z.astype(BF), leaf.u(j, 0, j - 1)).astype(BF)
             for k in range(j - 1):
                 waiting[k].append(others[:, k * width : (k + 1) * width])
+        partial = following
     return solved
 
 
@@ -375,8 +380,7 @@
 
     z_own = lax.dynamic_index_in_dim(z_high, in_half, 0, keepdims=False).astype(BF)
     q = dot_nt(z_own, u0).astype(BF)
-    col_sum = copies(dot_nt(q, v0), HALF_ROW).reshape(HALF, rhs_count, tile).sum(axis=0)
-    col_sum = lax.ppermute(col_sum, "yh", [(1, 0)])
+    col_sum = copies(dot_nt(q, v0), ROW).reshape(2, HALF, rhs_count, tile)[1].sum(axis=0)
     col_sums = copies(col_sum, COL).reshape(8, rhs_count, tile)
     low_rhs = x_low - col_sums
     z_low = solve(backward_kernel, place, kept_left, kept_right, diag_inv, low_rhs)

time: 216 us -> 216 us (level)
  waiting for transfers between devices: 73.5 us -> 66.2 us
  blocking collectives: 65.1 us -> 70.1 us
  Pallas kernels: 30.1 us -> 32.4 us
    ppermute x1 -> x0, waiting for transfers between devices: 5.84 us -> none  [per_device(): col_sum = lax.ppermute(col_sum, 'yh', [(1, 0)])]
    all_to_all x3, blocking collectives: 27.5 us -> 32.4 us  [copies(): lax.all_to_all(stacked, axis, split_axis=0, concat_axis=0, tiled=True)]
    pallas_call x2, Pallas kernels: 18.8 us -> 21.3 us  [solve(): pl.pallas_call(body, out_shape=jax.ShapeDtypeStruct(rhs.shape, F32), in_s...]
  transfers between devices with their start and end apart: 7 -> 6, of which waited for: 7 -> 6; matrix products, arithmetic and copies ran while one was open for 4% -> 4% of each run, Pallas kernels for 0% -> 0%
where the time goes in v6:
time: 216 us
  blocking collectives  70.1 us (32%)
  waiting for transfers between devices  66.2 us (31%)
  Pallas kernels  32.4 us (15%)
  starting transfers between devices  15.5 us (7%)
  between operations  14.4 us (7%)
  local copies, waits for them, and re-layouts  7.34 us (3%)
  other arithmetic  6.83 us (3%)
  matrix products  2.77 us (1%)
    all_to_all x1, blocking collectives, per_device(): mine = lax.all_to_all(parts, ALL, split_axis=0, concat_axis=0, tiled=True)  37.7 us
    all_to_all x3, blocking collectives, copies(): lax.all_to_all(stacked, axis, split_axis=0, concat_axis=0, tiled=True)  32.4 us
    all_gather x1, waiting for transfers between devices, per_device(): tiles = lax.all_gather(share, PLANE)  30 us
    pallas_call x2, Pallas kernels, solve(): pl.pallas_call(body, out_shape=jax.ShapeDtypeStruct(rhs.shape, F32), in_s...  21.3 us
    all_to_all x2, waiting for transfers between devices, copies(): lax.all_to_all(stacked, axis, split_axis=0, concat_axis=0, tiled=True)  15.9 us
    ppermute x1, waiting for transfers between devices, per_device(): other_tile = lax.ppermute(own_tile, ALL, plane_pairs())  13.6 us
    pallas_call x1, Pallas kernels, load_and_forward(): pl.pallas_call(load_kernel, out_shape=(jax.ShapeDtypeStruct(rhs.shape, F3...  11.1 us
    all_to_all x2, starting transfers between devices, copies(): lax.all_to_all(stacked, axis, split_axis=0, concat_axis=0, tiled=True)  8.16 us
  transfers between devices with their start and end apart: 6, of which 6 were waited for; matrix products, arithmetic and copies ran while one was open for 4% of the time, Pallas kernels for 0%

profile of v6, /device:TPU:0, one launch (start us, length us, event | category | flops | bytes accessed | tf_op | source)
XLA Modules:
  0.0 215.5 jit_solution(595662705540943600)
XLA Ops:
  7.2 0.0 copy-start
  7.2 0.0 all-gather.3.cloned.1.call-start
  7.2 1.1 copy.27
  8.4 0.7 iota_compare_fusion
  9.1 0.0 copy-start.4
  9.1 0.1 convert_select_fusion
  9.3 1.0 fusion.19
  10.3 1.3 collective-permute-start
  11.6 13.6 %collective-permute-done = f32[256,512]{1,0:T(8,128)S(1)} collective-permute-done((f32[256,512]{1,0:T(8,128)S(1)}, f32[256,512]{1,0:T(8,128)S(1)}, u32[]{:S(2)}, u32[]{:S(2)}) %collective-permute-start) | collective-permute-done | bytes 524320 | tf_op jit(solution)/shard_map/ppermute | solution.py:347
  25.2 0.9 broadcast_select_fusion
  26.1 0.0 all-gather.3.cloned.1.call-update
  26.1 1.5 copy.35
  27.6 0.7 fusion.41
  28.3 1.1 convolution_bitcast_fusion
  29.4 0.8 scatter_fusion
  30.2 0.1 copy.29
  30.2 0.1 reshape.118
  30.4 0.3 copy.30
  30.7 0.3 reshape.141
  31.0 37.7 %all_to_all.30 = f32[128,1,512]{2,1,0:T(1,128)S(1)} all-to-all(f32[128,1,512]{2,1,0:T(1,128)S(1)} %reshape.141), channel_id=1, replica_groups=mesh['yh'=2,'yl'=2,'z'=4,'x'=4,'c'=2] {'yh','yl','z','x','c'}, dimensions={0} | all-to-all | bytes 524288 | tf_op jit(solution)/shard_map/all_to_all | solution.py:358
  68.7 0.6 broadcast.43
  69.3 1.2 reduce.1
  70.5 0.1 reshape.142
  70.6 0.1 reduce_sum.27
  70.8 0.8 reshape.143
  71.6 4.6 %all-to-all-start.1 = ((f32[64,1,512]{2,1,0:T(1,128)}), f32[64,1,512]{2,1,0:T(1,128)S(1)}, u32[]{:S(2)}, u32[]{:S(2)}) async-start(f32[64,1,512]{2,1,0:T(1,128)} %reshape.143), calls=%async_computation.1 | async-start | bytes 262144 | tf_op jit(solution)/shard_map/all_to_all | solution.py:27
  76.3 0.1 pad_add_fusion.place
  76.3 9.6 %all-to-all-done.1 = f32[64,1,512]{2,1,0:T(1,128)S(1)} async-done(((f32[64,1,512]{2,1,0:T(1,128)}), f32[64,1,512]{2,1,0:T(1,128)S(1)}, u32[]{:S(2)}, u32[]{:S(2)}) %all-to-all-start.1) | async-done | bytes 131104 | tf_op jit(solution)/shard_map/all_to_all | solution.py:27
  85.9 0.9 reduce.2
  86.9 0.1 reshape.144
  87.0 0.1 copy.31
  87.0 0.1 reshape.119
  87.2 0.0 copy-done.4
  87.2 0.1 fusion.20.rhs
  87.3 30.0 %all-gather.3.cloned.1.call-done = f32[8192,512]{1,0:T(8,128)} async-done(((f32[256,512]{1,0:T(8,128)}), f32[8192,512]{1,0:T(8,128)}) %all-gather.3.cloned.1.call-update) | async-done | bytes 16777232 | tf_op jit(solution)/shard_map/all_gather | solution.py:362
  117.3 0.0 copy-start.2
  117.3 11.1 %shard_map.104 = (f32[8,8,512]{2,1,0:T(8,128)S(1)}, bf16[28,128,512]{2,1,0:T(8,128)(2,1)}, bf16[28,128,512]{2,1,0:T(8,128)(2,1)}) custom-call(s32[2]{0:T(128)S(1)} %pad_add_fusion.place, f32[32,256,512]{2,1,0:T(8,128)} %bitcast.74, bf16[16,512,512]{2,1,0:T(8,128)(2,1)} %inv.5, f32[8,8,512]{2,1,0:T(8,128)S(1)} %fusion.20.rhs), custom_call_target="tpu_custom_call" | custom-call | tf_op jit(solution)/shard_map/pallas_call | solution.py:298
  128.4 4.6 %collective-permute-start.1 = (f32[8,512]{1,0:T(8,128)S(1)}, f32[8,512]{1,0:T(8,128)S(1)}, u32[]{:S(2)}, u32[]{:S(2)}) collective-permute-start(f32[8,512]{1,0:T(8,128)S(1)} %dynamic-slice_bitcast_fusion), channel_id=1, source_target_pairs={{0,64},{1,65},{2,66},{3,67},{4,68},{5,69},{6,70},{7,71},{8,72},{9,... | collective-permute-start | bytes 49160 | tf_op jit(solution)/shard_map/ppermute | solution.py:374
  133.1 1.4 collective-permute-done.1
  134.5 0.0 copy-done.2
  134.5 0.3 fusion.9
  134.8 9.9 %all_to_all.31 = f32[8,8,512]{2,1,0:T(8,128)S(1)} all-to-all(f32[8,8,512]{2,1,0:T(8,128)S(1)} %broadcast_in_dim.42), channel_id=1, replica_groups=mesh['yh'=2,'yl'=2,'z'=4,'x'=4,'c'=2] {'x','c'}, dimensions={0} | all-to-all | bytes 262144 | tf_op jit(solution)/shard_map/all_to_all | solution.py:27
  144.8 0.6 broadcast_in_dim.43
  145.4 3.5 %all-to-all-start.3 = ((f32[8,8,512]{2,1,0:T(8,128)}), f32[8,8,512]{2,1,0:T(8,128)S(1)}, u32[]{:S(2)}, u32[]{:S(2)}) async-start(f32[8,8,512]{2,1,0:T(8,128)} %broadcast_in_dim.43), calls=%async_computation.3 | async-start | bytes 262144 | tf_op jit(solution)/shard_map/all_to_all | solution.py:27
  149.0 6.3 %all-to-all-done.3 = f32[8,8,512]{2,1,0:T(8,128)S(1)} async-done(((f32[8,8,512]{2,1,0:T(8,128)}), f32[8,8,512]{2,1,0:T(8,128)S(1)}, u32[]{:S(2)}, u32[]{:S(2)}) %all-to-all-start.3) | async-done | bytes 131104 | tf_op jit(solution)/shard_map/all_to_all | solution.py:27
  155.3 12.7 %shard_map.105 = f32[8,8,512]{2,1,0:T(8,128)S(1)} custom-call(s32[2]{0:T(128)S(1)} %pad_add_fusion.place, bf16[28,128,512]{2,1,0:T(8,128)(2,1)} %get-tuple-element.5.kept_left, bf16[28,128,512]{2,1,0:T(8,128)(2,1)} %get-tuple-element.6.kept_right, bf16[16,512,512]{2,1,0:T(8,128)(2,1)} %inv.5, f32[8,8,512]{2,1,0:T(8,128)S(1)} %sub.16.rhs), custom_call_target="tpu_custom_call" | custom-call | tf_op jit(solution)/shard_map/pallas_call | solution.py:314
  168.0 0.3 fusion.10
  168.3 0.1 broadcast_in_dim.44
  168.3 14.0 %all_to_all.32 = f32[16,8,512]{2,1,0:T(8,128)S(1)} all-to-all(f32[16,8,512]{2,1,0:T(8,128)S(1)} %broadcast_in_dim.44), channel_id=1, replica_groups=mesh['yh'=2,'yl'=2,'z'=4,'x'=4,'c'=2] {'yh','yl','z'}, dimensions={0} | all-to-all | bytes 524288 | tf_op jit(solution)/shard_map/all_to_all | solution.py:27
  182.3 8.5 %all_to_all.33 = f32[8,8,512]{2,1,0:T(8,128)S(1)} all-to-all(f32[8,8,512]{2,1,0:T(8,128)S(1)} %broadcast_in_dim.45), channel_id=1, replica_groups=mesh['yh'=2,'yl'=2,'z'=4,'x'=4,'c'=2] {'x','c'}, dimensions={0} | all-to-all | bytes 262144 | tf_op jit(solution)/shard_map/all_to_all | solution.py:27
  190.9 0.0 copy-start.1
  190.9 0.0 copy-start.3
  190.9 8.7 %shard_map.106 = f32[8,8,512]{2,1,0:T(8,128)S(1)} custom-call(s32[2]{0:T(128)S(1)} %pad_add_fusion.place, bf16[28,128,512]{2,1,0:T(8,128)(2,1)} %get-tuple-element.5.kept_left, bf16[28,128,512]{2,1,0:T(8,128)(2,1)} %get-tuple-element.6.kept_right, bf16[16,512,512]{2,1,0:T(8,128)(2,1)} %inv.5, f32[8,8,512]{2,1,0:T(8,128)S(1)} %sub.17.rhs), custom_call_target="tpu_custom_call" | custom-call | tf_op jit(solution)/shard_map/pallas_call | solution.py:314
  199.6 1.4 collective-permute-start.2
  201.0 5.2 %collective-permute-done.2 = f32[8,8,512]{2,1,0:T(8,128)S(1)} collective-permute-done((f32[8,8,512]{2,1,0:T(8,128)S(1)}, f32[8,8,512]{2,1,0:T(8,128)S(1)}, u32[]{:S(2)}, u32[]{:S(2)}) %collective-permute-start.2) | collective-permute-done | bytes 131104 | tf_op jit(solution)/shard_map/ppermute | solution.py:388
  206.3 0.6 gather_fusion
  206.8 0.0 copy-done
  206.8 0.0 copy-done.1
  206.8 0.0 copy-done.3
  206.8 1.1 fusion.6
  208.0 0.7 constant_dynamic-slice_fusion
  (15 shorter events, 0.3 us)
Async XLA Ops:
  7.2 199.7 %copy-start = (bf16[1,512,512]{2,1,0:T(8,128)(2,1)S(1)}, bf16[1,512,512]{2,1,0:T(8,128)(2,1)}, u32[]{:S(2)}) copy-start(bf16[1,512,512]{2,1,0:T(8,128)(2,1)} %param.16) | copy-start | bytes 1572868
  7.2 110.1 %all-gather.3.cloned.1.call-start = ((), (), s32[]{:S(2)}) async-start(), calls=%async_computation.6 | async-start | bytes 17301504 | tf_op jit(solution)/shard_map/all_gather | solution.py:362
  9.1 78.1 %copy-start.4 = (bf16[8,8192]{1,0:T(8,128)(2,1)S(1)}, bf16[8,8192]{1,0:T(8,128)(2,1)}, u32[]{:S(2)}) copy-start(bf16[8,8192]{1,0:T(8,128)(2,1)} %param.9) | copy-start | bytes 393220
  10.3 14.9 %collective-permute-start = (f32[256,512]{1,0:T(8,128)S(1)}, f32[256,512]{1,0:T(8,128)S(1)}, u32[]{:S(2)}, u32[]{:S(2)}) collective-permute-start(f32[256,512]{1,0:T(8,128)S(1)} %pad_maximum_fusion), channel_id=1, source_target_pairs={{8,47},{16,54},{17,55},{24,38},{25,63},{26,39},{32,0},{33,1},{34,2... | collective-permute-start | bytes 1572872 | tf_op jit(solution)/shard_map/ppermute | solution.py:347
  71.6 14.3 %all-to-all-start.1 = ((f32[64,1,512]{2,1,0:T(1,128)}), f32[64,1,512]{2,1,0:T(1,128)S(1)}, u32[]{:S(2)}, u32[]{:S(2)}) async-start(f32[64,1,512]{2,1,0:T(1,128)} %reshape.143), calls=%async_computation.1 | async-start | bytes 262144 | tf_op jit(solution)/shard_map/all_to_all | solution.py:27
  117.3 17.2 %copy-start.2 = (bf16[1,1,1,2,128,512]{5,4,3,2,1,0:T(8,128)(2,1)S(1)}, bf16[1,1,1,2,128,512]{5,4,3,2,1,0:T(8,128)(2,1)}, u32[]{:S(2)}) copy-start(bf16[1,1,1,2,128,512]{5,4,3,2,1,0:T(8,128)(2,1)} %param.11) | copy-start | bytes 786436
  128.4 6.0 %collective-permute-start.1 = (f32[8,512]{1,0:T(8,128)S(1)}, f32[8,512]{1,0:T(8,128)S(1)}, u32[]{:S(2)}, u32[]{:S(2)}) collective-permute-start(f32[8,512]{1,0:T(8,128)S(1)} %dynamic-slice_bitcast_fusion), channel_id=1, source_target_pairs={{0,64},{1,65},{2,66},{3,67},{4,68},{5,69},{6,70},{7,71},{8,72},{9,... | collective-permute-start | bytes 49160 | tf_op jit(solution)/shard_map/ppermute | solution.py:374
  145.4 9.9 %all-to-all-start.3 = ((f32[8,8,512]{2,1,0:T(8,128)}), f32[8,8,512]{2,1,0:T(8,128)S(1)}, u32[]{:S(2)}, u32[]{:S(2)}) async-start(f32[8,8,512]{2,1,0:T(8,128)} %broadcast_in_dim.43), calls=%async_computation.3 | async-start | bytes 262144 | tf_op jit(solution)/shard_map/all_to_all | solution.py:27
  190.9 16.0 %copy-start.1 = (bf16[1,512,1024]{2,1,0:T(8,128)(2,1)S(1)}, bf16[1,512,1024]{2,1,0:T(8,128)(2,1)}, u32[]{:S(2)}) copy-start(bf16[1,512,1024]{2,1,0:T(8,128)(2,1)} %param.15) | copy-start | bytes 3145732
  190.9 16.0 %copy-start.3 = (bf16[1,8,512]{2,1,0:T(8,128)(2,1)S(1)}, bf16[1,8,512]{2,1,0:T(8,128)(2,1)}, u32[]{:S(2)}) copy-start(bf16[1,8,512]{2,1,0:T(8,128)(2,1)} %param.14) | copy-start | bytes 24580
  199.6 6.6 %collective-permute-start.2 = (f32[8,8,512]{2,1,0:T(8,128)S(1)}, f32[8,8,512]{2,1,0:T(8,128)S(1)}, u32[]{:S(2)}, u32[]{:S(2)}) collective-permute-start(f32[8,8,512]{2,1,0:T(8,128)S(1)} %broadcast_select_fusion.3), channel_id=1, source_target_pairs={{0,64},{64,0},{1,65},{65,1},{2,66},{66,2},{3,67},{67,3},{4,68},{68... | collective-permute-start | bytes 393224 | tf_op jit(solution)/shard_map/ppermute | solution.py:388
Sparse Core Ops, SparseCore 0:
  26.2 91.0 all-gather.2

commit v7 on v4

--- a/solution.py
+++ b/solution.py
@@ -351,9 +351,10 @@
     flat_blocks = child_blocks.reshape(-1)
     dense = jnp.zeros((rhs_count, nblk, BLK), F32).at[:, flat_blocks, :].add(pieces)
     width = ntile * tile // ndev
-    parts = dense.reshape(rhs_count, ndev, width).transpose(1, 0, 2)
-    mine = lax.all_to_all(parts, ALL, split_axis=0, concat_axis=0, tiled=True).sum(axis=0)
-    other_tile, mine = lax.optimization_barrier((other_tile, mine))
+    parts = dense.reshape(rhs_count, 4, ntile * tile // 4).transpose(1, 0, 2)
+    mine = lax.all_to_all(parts, ("yh", "yl"), split_axis=0, concat_axis=0, tiled=True)
+    mine = mine.sum(axis=0).reshape(rhs_count, ndev // 4, width).transpose(1, 0, 2)
+    mine = lax.all_to_all(mine, PLANE, split_axis=0, concat_axis=0, tiled=True).sum(axis=0)
     share = jnp.where(my_col < in_half, own_tile, other_tile)
     share = with_layout_constraint(share, ROWS)
     tiles = lax.all_gather(share, PLANE)
@@ -377,8 +378,7 @@
 
     z_own = lax.dynamic_index_in_dim(z_high, in_half, 0, keepdims=False).astype(BF)
     q = dot_nt(z_own, u0).astype(BF)
-    col_sum = copies(dot_nt(q, v0), HALF_ROW).reshape(HALF, rhs_count, tile).sum(axis=0)
-    col_sum = lax.ppermute(col_sum, "yh", [(1, 0)])
+    col_sum = copies(dot_nt(q, v0), ROW).reshape(2, HALF, rhs_count, tile)[1].sum(axis=0)
     col_sums = copies(col_sum, COL).reshape(8, rhs_count, tile)
     low_rhs = x_low - col_sums
     z_low = solve(backward_kernel, place, kept_left, kept_right, diag_inv, low_rhs)

time: 220 us -> 213 us (0.968)
  blocking collectives: 27.7 us -> 71.9 us
  waiting for transfers between devices: 93.3 us -> 63.9 us
  starting transfers between devices: 35.8 us -> 15.6 us
    all_to_all x0 -> x2, blocking collectives: none -> 39.3 us  [the longest x1 27.5 us: per_device(): lax.all_to_all(mine, PLANE, split_axis=0, concat_axis=0, tiled=True)]
    all_gather x1, waiting for transfers between devices: 53.9 us -> 27.2 us  [per_device(): tiles = lax.all_gather(share, PLANE)]
    ppermute x1, waiting for transfers between devices: 0.01 us -> 13.6 us  [per_device(): other_tile = lax.ppermute(own_tile, ALL, plane_pairs())]
    all_to_all x1 -> x0, starting transfers between devices: 12.7 us -> none  [per_device(): lax.all_to_all(parts, ALL, split_axis=0, concat_axis=0, tiled=True)]
    all_to_all x1 -> x0, waiting for transfers between devices: 10.6 us -> none  [per_device(): lax.all_to_all(parts, ALL, split_axis=0, concat_axis=0, tiled=True)]
    all_to_all x2, starting transfers between devices: 15.3 us -> 7.98 us  [copies(): lax.all_to_all(stacked, axis, split_axis=0, concat_axis=0, tiled=True)]
    ppermute x1 -> x0, waiting for transfers between devices: 5.84 us -> none  [per_device(): col_sum = lax.ppermute(col_sum, 'yh', [(1, 0)])]
    all_to_all x3, blocking collectives: 27.7 us -> 32.6 us  [copies(): lax.all_to_all(stacked, axis, split_axis=0, concat_axis=0, tiled=True)]
  transfers between devices with their start and end apart: 8 -> 6, of which waited for: 7 -> 6; matrix products, arithmetic and copies ran while one was open for 4% -> 4% of each run, Pallas kernels for 0% -> 0%
where the time goes in v7:
time: 213 us; the launch traced here: 212 us
  blocking collectives  71.9 us (34%)
  waiting for transfers between devices  63.9 us (30%)
  Pallas kernels  30.1 us (14%)
  starting transfers between devices  15.6 us (7%)
  between operations  14.4 us (7%)
  local copies, waits for them, and re-layouts  7.06 us (3%)
  other arithmetic  6.29 us (3%)
  matrix products  2.77 us (1%)
    all_to_all x3, blocking collectives, copies(): lax.all_to_all(stacked, axis, split_axis=0, concat_axis=0, tiled=True)  32.6 us
    all_to_all x1, blocking collectives, per_device(): lax.all_to_all(mine, PLANE, split_axis=0, concat_axis=0, tiled=True)  27.5 us
    all_gather x1, waiting for transfers between devices, per_device(): tiles = lax.all_gather(share, PLANE)  27.2 us
    pallas_call x2, Pallas kernels, solve(): pl.pallas_call(body, out_shape=jax.ShapeDtypeStruct(rhs.shape, F32), in_s...  18.8 us
    all_to_all x2, waiting for transfers between devices, copies(): lax.all_to_all(stacked, axis, split_axis=0, concat_axis=0, tiled=True)  16.5 us
    ppermute x1, waiting for transfers between devices, per_device(): other_tile = lax.ppermute(own_tile, ALL, plane_pairs())  13.6 us
    all_to_all x1, blocking collectives, per_device(): lax.all_to_all(parts, ('yh', 'yl'), split_axis=0, concat_axis=0, tiled=True)  11.7 us
    pallas_call x1, Pallas kernels, load_and_forward(): pl.pallas_call(load_kernel, out_shape=(jax.ShapeDtypeStruct(rhs.shape, F3...  11.3 us
  transfers between devices with their start and end apart: 6, of which 6 were waited for; matrix products, arithmetic and copies ran while one was open for 4% of the time, Pallas kernels for 0%

profile of v7, /device:TPU:0, one launch (start us, length us, event | category | flops | bytes accessed | tf_op | source)
XLA Modules:
  0.0 212.0 jit_solution(11669282537848605369)
XLA Ops:
  7.2 0.0 copy-start
  7.2 0.0 copy-start.4
  7.2 0.0 all-gather.3.cloned.1.call-start
  7.2 1.1 copy.36
  8.4 0.7 iota_compare_fusion
  9.1 0.1 convert_select_fusion
  9.3 1.0 fusion.19
  10.3 1.3 collective-permute-start
  11.6 13.6 %collective-permute-done = f32[256,512]{1,0:T(8,128)S(1)} collective-permute-done((f32[256,512]{1,0:T(8,128)S(1)}, f32[256,512]{1,0:T(8,128)S(1)}, u32[]{:S(2)}, u32[]{:S(2)}) %collective-permute-start) | collective-permute-done | bytes 524320 | tf_op jit(solution)/shard_map/ppermute | solution.py:344
  25.2 0.9 broadcast_select_fusion
  26.1 0.0 all-gather.3.cloned.1.call-update
  26.1 1.5 copy.45
  27.6 0.7 fusion.41
  28.3 1.1 convolution_bitcast_fusion
  29.4 0.8 scatter_fusion
  30.2 0.1 copy.38
  30.2 0.1 reshape.121
  30.3 0.2 copy.39
  30.5 11.7 %all_to_all.35 = f32[4,8,2048]{2,1,0:T(8,128)S(1)} all-to-all(f32[4,8,2048]{2,1,0:T(8,128)S(1)} %copy.39), channel_id=1, replica_groups=mesh['yh'=2,'yl'=2,'z'=4,'x'=4,'c'=2] {'yh','yl'}, dimensions={0} | all-to-all | bytes 524288 | tf_op jit(solution)/shard_map/all_to_all | solution.py:355
  42.2 0.1 reshape.122
  42.3 0.1 copy.40
  42.4 0.1 reshape.145
  42.6 27.5 %all_to_all.36 = f32[32,1,512]{2,1,0:T(1,128)S(1)} all-to-all(f32[32,1,512]{2,1,0:T(1,128)S(1)} %reshape.145), channel_id=1, replica_groups=mesh['yh'=2,'yl'=2,'z'=4,'x'=4,'c'=2] {'z','x','c'}, dimensions={0} | all-to-all | bytes 131072 | tf_op jit(solution)/shard_map/all_to_all | solution.py:357
  70.1 0.6 broadcast.43
  70.7 0.8 reduce.1
  71.4 0.1 reshape.146
  71.6 0.8 reshape.147
  72.4 4.6 %all-to-all-start.2 = ((f32[64,1,512]{2,1,0:T(1,128)}), f32[64,1,512]{2,1,0:T(1,128)S(1)}, u32[]{:S(2)}, u32[]{:S(2)}) async-start(f32[64,1,512]{2,1,0:T(1,128)} %reshape.147), calls=%async_computation.2 | async-start | bytes 262144 | tf_op jit(solution)/shard_map/all_to_all | solution.py:29
  77.1 0.1 pad_add_fusion.place
  77.1 9.9 %all-to-all-done.2 = f32[64,1,512]{2,1,0:T(1,128)S(1)} async-done(((f32[64,1,512]{2,1,0:T(1,128)}), f32[64,1,512]{2,1,0:T(1,128)S(1)}, u32[]{:S(2)}, u32[]{:S(2)}) %all-to-all-start.2) | async-done | bytes 131104 | tf_op jit(solution)/shard_map/all_to_all | solution.py:29
  87.1 0.9 reduce.2
  88.0 0.1 reshape.148
  88.1 0.1 copy.41
  88.2 0.1 reshape.123
  88.3 0.0 copy-done.4
  88.3 0.1 fusion.20.rhs
  88.4 27.2 %all-gather.3.cloned.1.call-done = f32[8192,512]{1,0:T(8,128)} async-done(((f32[256,512]{1,0:T(8,128)}), f32[8192,512]{1,0:T(8,128)}) %all-gather.3.cloned.1.call-update) | async-done | bytes 16777232 | tf_op jit(solution)/shard_map/all_gather | solution.py:360
  115.6 0.0 copy-start.2
  115.6 11.3 %shard_map.104 = (f32[8,8,512]{2,1,0:T(8,128)S(1)}, bf16[28,128,512]{2,1,0:T(8,128)(2,1)}, bf16[28,128,512]{2,1,0:T(8,128)(2,1)}) custom-call(s32[2]{0:T(128)S(1)} %pad_add_fusion.place, f32[32,256,512]{2,1,0:T(8,128)} %bitcast.75, bf16[16,512,512]{2,1,0:T(8,128)(2,1)} %inv.5, f32[8,8,512]{2,1,0:T(8,128)S(1)} %fusion.20.rhs), custom_call_target="tpu_custom_call" | custom-call | tf_op jit(solution)/shard_map/pallas_call | solution.py:295
  127.0 4.9 %collective-permute-start.1 = (f32[8,512]{1,0:T(8,128)S(1)}, f32[8,512]{1,0:T(8,128)S(1)}, u32[]{:S(2)}, u32[]{:S(2)}) collective-permute-start(f32[8,512]{1,0:T(8,128)S(1)} %dynamic-slice_bitcast_fusion), channel_id=1, source_target_pairs={{0,64},{1,65},{2,66},{3,67},{4,68},{5,69},{6,70},{7,71},{8,72},{9,... | collective-permute-start | bytes 49160 | tf_op jit(solution)/shard_map/ppermute | solution.py:372
  131.9 1.4 collective-permute-done.1
  133.3 0.0 copy-done.2
  133.3 0.3 fusion.9
  133.6 10.2 %all_to_all.37 = f32[8,8,512]{2,1,0:T(8,128)S(1)} all-to-all(f32[8,8,512]{2,1,0:T(8,128)S(1)} %broadcast_in_dim.42), channel_id=1, replica_groups=mesh['yh'=2,'yl'=2,'z'=4,'x'=4,'c'=2] {'x','c'}, dimensions={0} | all-to-all | bytes 262144 | tf_op jit(solution)/shard_map/all_to_all | solution.py:29
  143.8 0.6 broadcast_in_dim.43
  144.4 3.4 %all-to-all-start.4 = ((f32[8,8,512]{2,1,0:T(8,128)}), f32[8,8,512]{2,1,0:T(8,128)S(1)}, u32[]{:S(2)}, u32[]{:S(2)}) async-start(f32[8,8,512]{2,1,0:T(8,128)} %broadcast_in_dim.43), calls=%async_computation.4 | async-start | bytes 262144 | tf_op jit(solution)/shard_map/all_to_all | solution.py:29
  147.8 6.5 %all-to-all-done.4 = f32[8,8,512]{2,1,0:T(8,128)S(1)} async-done(((f32[8,8,512]{2,1,0:T(8,128)}), f32[8,8,512]{2,1,0:T(8,128)S(1)}, u32[]{:S(2)}, u32[]{:S(2)}) %all-to-all-start.4) | async-done | bytes 131104 | tf_op jit(solution)/shard_map/all_to_all | solution.py:29
  154.4 11.2 %shard_map.105 = f32[8,8,512]{2,1,0:T(8,128)S(1)} custom-call(s32[2]{0:T(128)S(1)} %pad_add_fusion.place, bf16[28,128,512]{2,1,0:T(8,128)(2,1)} %get-tuple-element.5.kept_left, bf16[28,128,512]{2,1,0:T(8,128)(2,1)} %get-tuple-element.6.kept_right, bf16[16,512,512]{2,1,0:T(8,128)(2,1)} %inv.5, f32[8,8,512]{2,1,0:T(8,128)S(1)} %sub.16.rhs), custom_call_target="tpu_custom_call" | custom-call | tf_op jit(solution)/shard_map/pallas_call | solution.py:311
  165.5 0.3 fusion.10
  165.8 0.1 broadcast_in_dim.44
  165.9 14.0 %all_to_all.38 = f32[16,8,512]{2,1,0:T(8,128)S(1)} all-to-all(f32[16,8,512]{2,1,0:T(8,128)S(1)} %broadcast_in_dim.44), channel_id=1, replica_groups=mesh['yh'=2,'yl'=2,'z'=4,'x'=4,'c'=2] {'yh','yl','z'}, dimensions={0} | all-to-all | bytes 524288 | tf_op jit(solution)/shard_map/all_to_all | solution.py:29
  179.9 8.5 %all_to_all.39 = f32[8,8,512]{2,1,0:T(8,128)S(1)} all-to-all(f32[8,8,512]{2,1,0:T(8,128)S(1)} %broadcast_in_dim.45), channel_id=1, replica_groups=mesh['yh'=2,'yl'=2,'z'=4,'x'=4,'c'=2] {'x','c'}, dimensions={0} | all-to-all | bytes 262144 | tf_op jit(solution)/shard_map/all_to_all | solution.py:29
  188.4 0.0 copy-start.1
  188.4 0.0 copy-start.3
  188.4 7.6 %shard_map.106 = f32[8,8,512]{2,1,0:T(8,128)S(1)} custom-call(s32[2]{0:T(128)S(1)} %pad_add_fusion.place, bf16[28,128,512]{2,1,0:T(8,128)(2,1)} %get-tuple-element.5.kept_left, bf16[28,128,512]{2,1,0:T(8,128)(2,1)} %get-tuple-element.6.kept_right, bf16[16,512,512]{2,1,0:T(8,128)(2,1)} %inv.5, f32[8,8,512]{2,1,0:T(8,128)S(1)} %sub.17.rhs), custom_call_target="tpu_custom_call" | custom-call | tf_op jit(solution)/shard_map/pallas_call | solution.py:311
  196.1 1.4 collective-permute-start.2
  197.5 5.2 %collective-permute-done.2 = f32[8,8,512]{2,1,0:T(8,128)S(1)} collective-permute-done((f32[8,8,512]{2,1,0:T(8,128)S(1)}, f32[8,8,512]{2,1,0:T(8,128)S(1)}, u32[]{:S(2)}, u32[]{:S(2)}) %collective-permute-start.2) | collective-permute-done | bytes 131104 | tf_op jit(solution)/shard_map/ppermute | solution.py:386
  202.8 0.6 gather_fusion
  203.4 0.0 copy-done
  203.4 0.0 copy-done.1
  203.4 0.0 copy-done.3
  203.4 1.1 fusion.6
  204.5 0.7 constant_dynamic-slice_fusion
  (17 shorter events, 0.4 us)
Async XLA Ops:
  7.2 196.2 %copy-start = (bf16[1,512,512]{2,1,0:T(8,128)(2,1)S(1)}, bf16[1,512,512]{2,1,0:T(8,128)(2,1)}, u32[]{:S(2)}) copy-start(bf16[1,512,512]{2,1,0:T(8,128)(2,1)} %param.16) | copy-start | bytes 1572868
  7.2 81.1 %copy-start.4 = (bf16[8,8192]{1,0:T(8,128)(2,1)S(1)}, bf16[8,8192]{1,0:T(8,128)(2,1)}, u32[]{:S(2)}) copy-start(bf16[8,8192]{1,0:T(8,128)(2,1)} %param.9) | copy-start | bytes 393220
  7.2 108.4 %all-gather.3.cloned.1.call-start = ((), (), s32[]{:S(2)}) async-start(), calls=%async_computation.7 | async-start | bytes 17301504 | tf_op jit(solution)/shard_map/all_gather | solution.py:360
  10.3 14.9 %collective-permute-start = (f32[256,512]{1,0:T(8,128)S(1)}, f32[256,512]{1,0:T(8,128)S(1)}, u32[]{:S(2)}, u32[]{:S(2)}) collective-permute-start(f32[256,512]{1,0:T(8,128)S(1)} %pad_maximum_fusion), channel_id=1, source_target_pairs={{8,47},{16,54},{17,55},{24,38},{25,63},{26,39},{32,0},{33,1},{34,2... | collective-permute-start | bytes 1572872 | tf_op jit(solution)/shard_map/ppermute | solution.py:344
  72.4 14.6 %all-to-all-start.2 = ((f32[64,1,512]{2,1,0:T(1,128)}), f32[64,1,512]{2,1,0:T(1,128)S(1)}, u32[]{:S(2)}, u32[]{:S(2)}) async-start(f32[64,1,512]{2,1,0:T(1,128)} %reshape.147), calls=%async_computation.2 | async-start | bytes 262144 | tf_op jit(solution)/shard_map/all_to_all | solution.py:29
  115.6 17.7 %copy-start.2 = (bf16[1,1,1,2,128,512]{5,4,3,2,1,0:T(8,128)(2,1)S(1)}, bf16[1,1,1,2,128,512]{5,4,3,2,1,0:T(8,128)(2,1)}, u32[]{:S(2)}) copy-start(bf16[1,1,1,2,128,512]{5,4,3,2,1,0:T(8,128)(2,1)} %param.11) | copy-start | bytes 786436
  127.0 6.4 %collective-permute-start.1 = (f32[8,512]{1,0:T(8,128)S(1)}, f32[8,512]{1,0:T(8,128)S(1)}, u32[]{:S(2)}, u32[]{:S(2)}) collective-permute-start(f32[8,512]{1,0:T(8,128)S(1)} %dynamic-slice_bitcast_fusion), channel_id=1, source_target_pairs={{0,64},{1,65},{2,66},{3,67},{4,68},{5,69},{6,70},{7,71},{8,72},{9,... | collective-permute-start | bytes 49160 | tf_op jit(solution)/shard_map/ppermute | solution.py:372
  144.4 9.9 %all-to-all-start.4 = ((f32[8,8,512]{2,1,0:T(8,128)}), f32[8,8,512]{2,1,0:T(8,128)S(1)}, u32[]{:S(2)}, u32[]{:S(2)}) async-start(f32[8,8,512]{2,1,0:T(8,128)} %broadcast_in_dim.43), calls=%async_computation.4 | async-start | bytes 262144 | tf_op jit(solution)/shard_map/all_to_all | solution.py:29
  188.4 14.9 %copy-start.1 = (bf16[1,512,1024]{2,1,0:T(8,128)(2,1)S(1)}, bf16[1,512,1024]{2,1,0:T(8,128)(2,1)}, u32[]{:S(2)}) copy-start(bf16[1,512,1024]{2,1,0:T(8,128)(2,1)} %param.15) | copy-start | bytes 3145732
  188.4 14.9 %copy-start.3 = (bf16[1,8,512]{2,1,0:T(8,128)(2,1)S(1)}, bf16[1,8,512]{2,1,0:T(8,128)(2,1)}, u32[]{:S(2)}) copy-start(bf16[1,8,512]{2,1,0:T(8,128)(2,1)} %param.14) | copy-start | bytes 24580
  196.1 6.6 %collective-permute-start.2 = (f32[8,8,512]{2,1,0:T(8,128)S(1)}, f32[8,8,512]{2,1,0:T(8,128)S(1)}, u32[]{:S(2)}, u32[]{:S(2)}) collective-permute-start(f32[8,8,512]{2,1,0:T(8,128)S(1)} %broadcast_select_fusion.3), channel_id=1, source_target_pairs={{0,64},{64,0},{1,65},{65,1},{2,66},{66,2},{3,67},{67,3},{4,68},{68... | collective-permute-start | bytes 393224 | tf_op jit(solution)/shard_map/ppermute | solution.py:386
Sparse Core Ops, SparseCore 0:
  26.2 89.3 all-gather.2

commit v8 on v7

--- a/solution.py
+++ b/solution.py
@@ -76,8 +76,8 @@
 
 
 class Leaf:
-    def __init__(self, left, right, diag):
-        self.left, self.right, self.diag = left, right, diag
+    def __init__(self, left, right, diag=None, flipped=None):
+        self.left, self.right, self.diag, self.flipped = left, right, diag, flipped
 
     def column(self, j):
         return sum(HALF - 1 - m for m in range(j))
@@ -104,10 +104,10 @@
             move.wait()
 
 
-def inverse_moves(leaf, first, inv, sems):
+def inverse_moves(target, first, source, sems):
     return Moves(
         {
-            n: [pltpu.make_async_copy(inv.at[first + n], leaf.diag.at[n], sems.at[n])]
+            n: [pltpu.make_async_copy(source.at[first + n], target.at[n], sems.at[n])]
             for n in range(HALF)
         }
     )
@@ -128,7 +128,7 @@
 
 
 class Loader:
-    def __init__(self, leaf, place, tiles, inv, kept, stage, sems, dsems, lsems, rsems):
+    def __init__(self, leaf, place, tiles, stage, sems, kept=None, inverse=None):
         self.leaf, self.stage = leaf, stage
         rows = {}
         for i in range(1, HALF):
@@ -143,8 +143,8 @@
                     )
                 )
         self.tiles = Moves(rows)
-        self.inverse = inverse_moves(leaf, HALF * place[1], inv, dsems)
-        self.kept = factor_moves(leaf, *kept, lsems, rsems, True)
+        self.inverse = inverse or Moves({})
+        self.kept = kept or Moves({})
         for i in range(SLOTS):
             self.start(i)
         self(0)
@@ -165,19 +165,13 @@
         if i + SLOTS < HALF:
             self.start(i + SLOTS)
 
-    def finish(self):
-        self.kept.start(HALF - 1)
-        for i in range(HALF):
-            self.kept.wait(i)
-
 
 class Reloader:
-    def __init__(self, leaf, place, inv, kept, dsems, lsems, rsems, order):
-        self.inverse = inverse_moves(leaf, HALF * place[1], inv, dsems)
-        self.factors = factor_moves(leaf, *kept, lsems, rsems, False)
+    def __init__(self, inverse, factors, order):
+        self.inverse, self.factors = inverse, factors
         for i in order:
-            self.inverse.start(i)
-            self.factors.start(i)
+            inverse.start(i)
+            factors.start(i)
         self(order[0])
 
     def __call__(self, i):
@@ -218,7 +212,7 @@
         acc = partial
         if j + 1 < HALF:
             acc = acc - dot_nn(last, leaf.vt(j + 1, j))
-        z = exact(dot_nt, acc, leaf.diag[j])
+        z = exact(dot_nn, acc, leaf.flipped[j])
         if j:
             if load:
                 load(j - 1)
@@ -242,25 +236,74 @@
         out[i] = values[i]
 
 
-def load_kernel(place, tiles, inv, rhs, out, kept_left, kept_right, stage, *scratch):
+def values(ref):
+    return [ref[i] for i in range(HALF)]
+
+
+def keep_tiles(leaf, place, tiles, stage, sems, kept, lsems, rsems):
+    moves = factor_moves(leaf, *kept, lsems, rsems, True)
+    load = Loader(leaf, place, tiles, stage, sems, kept=moves)
+    for i in range(1, HALF):
+        load(i)
+    moves.start(HALF - 1)
+    for i in range(HALF):
+        moves.wait(i)
+
+
+def first_kernel(place, tiles, inv, rhs, out, kept_left, kept_right, stage, *scratch):
     left, right, diag, sems, dsems, lsems, rsems = scratch
     leaf = Leaf(left, right, diag)
-    kept = (kept_left, kept_right)
-    load = Loader(leaf, place, tiles, inv, kept, stage, sems, dsems, lsems, rsems)
-    put(out, forward(leaf, [rhs[i] for i in range(HALF)], load))
-    load.finish()
-
-
-def both_kernel(place, kept_left, kept_right, inv, rhs, out, left, right, diag, *sems):
-    leaf = Leaf(left, right, diag)
-    load = Reloader(leaf, place, inv, (kept_left, kept_right), *sems, range(HALF))
-    put(out, backward(leaf, forward(leaf, [rhs[i] for i in range(HALF)], load)))
-
-
-def backward_kernel(place, kept_left, kept_right, inv, rhs, out, left, right, diag, *sems):
-    leaf = Leaf(left, right, diag)
-    load = Reloader(leaf, place, inv, (kept_left, kept_right), *sems, range(HALF)[::-1])
-    put(out, backward(leaf, [rhs[i] for i in range(HALF)], load))
+
+    @pl.when(place[1] == 0)
+    def _():
+        inverse = inverse_moves(diag, 0, inv, dsems)
+        load = Loader(leaf, place, tiles, stage, sems, inverse=inverse)
+        put(out, forward(leaf, values(rhs), load))
+
+    @pl.when(place[1] == 1)
+    def _():
+        out[...] = jnp.zeros(out.shape, F32)
+        keep_tiles(leaf, place, tiles, stage, sems, (kept_left, kept_right), lsems, rsems)
+
+
+def second_kernel(place, tiles, kept_left, kept_right, inv, turned, rhs, *refs):
+    out, next_left, next_right, stage, left, right, diag, flipped = refs[:8]
+    sems, dsems, tsems, lsems, rsems = refs[8:]
+    leaf = Leaf(left, right, diag, flipped)
+
+    @pl.when(place[1] == 0)
+    def _():
+        out[...] = jnp.zeros(out.shape, F32)
+        keep_tiles(leaf, place, tiles, stage, sems, (next_left, next_right), lsems, rsems)
+
+    @pl.when(place[1] == 1)
+    def _():
+        inverse = inverse_moves(diag, HALF, inv, dsems)
+        factors = factor_moves(leaf, kept_left, kept_right, lsems, rsems, False)
+        load = Reloader(inverse, factors, range(HALF))
+        turn = inverse_moves(flipped, 0, turned, tsems)
+        for n in range(HALF):
+            turn.start(n)
+        solved = forward(leaf, values(rhs), load)
+        for n in range(HALF):
+            turn.wait(n)
+        put(out, backward(leaf, solved))
+
+
+def third_kernel(place, kept_left, kept_right, turned, rhs, out, left, right, flipped, *sems):
+    tsems, lsems, rsems = sems
+    leaf = Leaf(left, right, flipped=flipped)
+
+    @pl.when(place[1] == 0)
+    def _():
+        turn = inverse_moves(flipped, 0, turned, tsems)
+        factors = factor_moves(leaf, kept_left, kept_right, lsems, rsems, False)
+        load = Reloader(turn, factors, range(HALF)[::-1])
+        put(out, backward(leaf, values(rhs), load))
+
+    @pl.when(place[1] == 1)
+    def _():
+        out[...] = jnp.zeros(out.shape, F32)
 
 
 IN_SMEM = pl.BlockSpec(memory_space=pltpu.SMEM)
@@ -276,46 +319,28 @@
     return pltpu.with_memory_space_constraint(v, pltpu.HBM)
 
 
-def leaf_scratch(rank, tile):
-    return [
-        pltpu.VMEM((TILES, rank, tile), BF),
-        pltpu.VMEM((TILES, rank, tile), BF),
-        pltpu.VMEM((HALF, tile, tile), BF),
-    ]
-
-
-def leaf_sems():
+def solve(body, place, hbm, rhs, keeps, loads, inverses):
+    tile = rhs.shape[2]
+    rank = tile // 4
     dma = pltpu.SemaphoreType.DMA
-    return [dma((HALF,)), dma((HALF,)), dma((TILES,))]
-
-
-def load_and_forward(place, tiles, inv, rhs):
-    rank, tile = tiles.shape[1] // 2, tiles.shape[2]
+    solved = jax.ShapeDtypeStruct(rhs.shape, F32)
     factors = pltpu.HBM((TILES, rank, tile), BF)
     return pl.pallas_call(
-        load_kernel,
-        out_shape=(jax.ShapeDtypeStruct(rhs.shape, F32), factors, factors),
-        in_specs=[IN_SMEM, IN_HBM, IN_HBM, IN_VMEM],
-        out_specs=(IN_VMEM, IN_HBM, IN_HBM),
+        body,
+        out_shape=(solved, factors, factors) if keeps else solved,
+        in_specs=[IN_SMEM, *[IN_HBM] * len(hbm), IN_VMEM],
+        out_specs=(IN_VMEM, IN_HBM, IN_HBM) if keeps else IN_VMEM,
         scratch_shapes=[
-            pltpu.VMEM((SLOTS, HALF - 1, 2 * rank, tile), F32),
-            *leaf_scratch(rank, tile),
-            pltpu.SemaphoreType.DMA((TILES,)),
-            *leaf_sems(),
+            *[pltpu.VMEM((SLOTS, HALF - 1, 2 * rank, tile), F32)] * loads,
+            *[pltpu.VMEM((TILES, rank, tile), BF)] * 2,
+            *[pltpu.VMEM((HALF, tile, tile), BF)] * inverses,
+            *[dma((TILES,))] * loads,
+            *[dma((HALF,))] * inverses,
+            dma((HALF,)),
+            dma((TILES,)),
         ],
-        compiler_params=limit(36),
-    )(place, in_hbm(tiles), in_hbm(inv), rhs)
-
-
-def solve(body, place, left, right, inv, rhs):
-    return pl.pallas_call(
-        body,
-        out_shape=jax.ShapeDtypeStruct(rhs.shape, F32),
-        in_specs=[IN_SMEM, IN_HBM, IN_HBM, IN_HBM, IN_VMEM],
-        out_specs=IN_VMEM,
-        scratch_shapes=[*leaf_scratch(*left.shape[1:]), *leaf_sems()],
-        compiler_params=limit(24),
-    )(place, in_hbm(left), in_hbm(right), in_hbm(inv), rhs)
+        compiler_params=limit(40),
+    )(place, *[in_hbm(v) for v in hbm], rhs)
 
 
 def per_device(
@@ -351,10 +376,12 @@
     flat_blocks = child_blocks.reshape(-1)
     dense = jnp.zeros((rhs_count, nblk, BLK), F32).at[:, flat_blocks, :].add(pieces)
     width = ntile * tile // ndev
-    parts = dense.reshape(rhs_count, 4, ntile * tile // 4).transpose(1, 0, 2)
-    mine = lax.all_to_all(parts, ("yh", "yl"), split_axis=0, concat_axis=0, tiled=True)
-    mine = mine.sum(axis=0).reshape(rhs_count, ndev // 4, width).transpose(1, 0, 2)
-    mine = lax.all_to_all(mine, PLANE, split_axis=0, concat_axis=0, tiled=True).sum(axis=0)
+    parts = dense.reshape(rhs_count * 4, ndev // 4, width).transpose(1, 0, 2)
+    mine = lax.all_to_all(parts, PLANE, split_axis=0, concat_axis=0, tiled=True).sum(axis=0)
+    other_tile, mine = lax.optimization_barrier((other_tile, mine))
+    mine = mine.reshape(rhs_count, 4, width).transpose(1, 0, 2)
+    mine = lax.all_to_all(mine, ("yh", "yl"), split_axis=0, concat_axis=0, tiled=True)
+    mine = mine.sum(axis=0)
     share = jnp.where(my_col < in_half, own_tile, other_tile)
     share = with_layout_constraint(share, ROWS)
     tiles = lax.all_gather(share, PLANE)
@@ -364,8 +391,10 @@
     given = root_rhs.reshape(rhs_count, ntile, tile)
     given = lax.dynamic_slice_in_dim(given, HALF * half, HALF, 1)
     own_rhs = given.transpose(1, 0, 2).astype(F32) - child_sum
-
-    x_low, kept_left, kept_right = load_and_forward(place, tiles, diag_inv, own_rhs)
+    begin, own_rhs = lax.optimization_barrier((HALF * half, own_rhs))
+    turned = lax.dynamic_slice_in_dim(diag_inv, begin, HALF, 0).transpose(0, 2, 1)
+
+    x_low, *kept = solve(first_kernel, place, [tiles, diag_inv], own_rhs, True, 1, 1)
     v0 = right[0].astype(BF)
     u0 = left[0]
     x_col = lax.dynamic_index_in_dim(x_low, my_col, 0, keepdims=False)
@@ -374,14 +403,15 @@
     p = dot_nn(x_own.astype(BF), v0).astype(BF)
     row_sum = copies(dot_nn(p, u0), COL).reshape(8, rhs_count, tile).sum(axis=0)
     row_sums = copies(row_sum, HALF_ROW).reshape(HALF, rhs_count, tile)
-    z_high = solve(both_kernel, place, kept_left, kept_right, diag_inv, own_rhs - row_sums)
+    arrays = [tiles, *kept, diag_inv, turned]
+    z_high, *kept = solve(second_kernel, place, arrays, own_rhs - row_sums, True, 1, 2)
 
     z_own = lax.dynamic_index_in_dim(z_high, in_half, 0, keepdims=False).astype(BF)
     q = dot_nt(z_own, u0).astype(BF)
     col_sum = copies(dot_nt(q, v0), ROW).reshape(2, HALF, rhs_count, tile)[1].sum(axis=0)
     col_sums = copies(col_sum, COL).reshape(8, rhs_count, tile)
     low_rhs = x_low - col_sums
-    z_low = solve(backward_kernel, place, kept_left, kept_right, diag_inv, low_rhs)
+    z_low = solve(third_kernel, place, [*kept, turned], low_rhs, False, 0, 1)
     z_mine = jnp.where(upper, z_high, z_low)
     z_other = lax.ppermute(z_mine, "yh", [(0, 1), (1, 0)])
     low_part = jnp.where(upper, z_other, z_mine)

time: 213 us -> 222 us (1.042)
  blocking collectives: 71.9 us -> 36 us
  starting transfers between devices: 15.6 us -> 34.2 us
  local copies, waits for them, and re-layouts: 7.06 us -> 20.9 us
  waiting for transfers between devices: 63.9 us -> 77.2 us
  Pallas kernels: 30.1 us -> 25.9 us
  other arithmetic: 6.29 us -> 10 us
    all_to_all x2 -> x1, blocking collectives: 39.3 us -> 9.27 us  [per_device(): lax.all_to_all(mine, ('yh', 'yl'), split_axis=0, concat_axis=0, tiled=True)]
    all_gather x1, waiting for transfers between devices: 27.2 us -> 45.3 us  [per_device(): tiles = lax.all_gather(share, PLANE)]
    ppermute x1, waiting for transfers between devices: 13.6 us -> 0.01 us  [per_device(): other_tile = lax.ppermute(own_tile, ALL, plane_pairs())]
    all_to_all x0 -> x1, starting transfers between devices: none -> 10.8 us  [per_device(): lax.all_to_all(parts, PLANE, split_axis=0, concat_axis=0, tiled=True)]
    unnamed x15 -> x20, local copies, waits for them, and re-layouts: 2.32 us -> 11.1 us
    all_to_all x0 -> x1, waiting for transfers between devices: none -> 8.71 us  [per_device(): lax.all_to_all(parts, PLANE, split_axis=0, concat_axis=0, tiled=True)]
    all_to_all x2 -> x3, starting transfers between devices: 7.98 us -> 16 us  [copies(): lax.all_to_all(stacked, axis, split_axis=0, concat_axis=0, tiled=True)]
    all_to_all x3 -> x2, blocking collectives: 32.6 us -> 26.7 us  [copies(): lax.all_to_all(stacked, axis, split_axis=0, concat_axis=0, tiled=True)]
  transfers between devices with their start and end apart: 6 -> 8, of which waited for: 6 -> 6; matrix products, arithmetic and copies ran while one was open for 4% -> 10% of each run, Pallas kernels for 0% -> 0%
where the time goes in v8:
time: 222 us; the launch traced here: 221 us
  waiting for transfers between devices  77.2 us (35%)
  blocking collectives  36 us (16%)
  starting transfers between devices  34.2 us (15%)
  Pallas kernels  25.9 us (12%)
  local copies, waits for them, and re-layouts  20.9 us (9%)
  between operations  14.4 us (6%)
  other arithmetic  10 us (5%)
    all_gather x1, waiting for transfers between devices, per_device(): tiles = lax.all_gather(share, PLANE)  45.3 us
    all_to_all x2, blocking collectives, copies(): lax.all_to_all(stacked, axis, split_axis=0, concat_axis=0, tiled=True)  26.7 us
    pallas_call x3, Pallas kernels, solve(): pl.pallas_call(body, out_shape=(solved, factors, factors) if keeps else s...  25.9 us
    all_to_all x3, starting transfers between devices, copies(): lax.all_to_all(stacked, axis, split_axis=0, concat_axis=0, tiled=True)  16 us
    all_to_all x3, waiting for transfers between devices, copies(): lax.all_to_all(stacked, axis, split_axis=0, concat_axis=0, tiled=True)  15.2 us
    unnamed x20, local copies, waits for them, and re-layouts  11.1 us
    all_to_all x1, starting transfers between devices, per_device(): lax.all_to_all(parts, PLANE, split_axis=0, concat_axis=0, tiled=True)  10.8 us
    all_to_all x1, blocking collectives, per_device(): lax.all_to_all(mine, ('yh', 'yl'), split_axis=0, concat_axis=0, tiled=True)  9.27 us
  transfers between devices with their start and end apart: 8, of which 6 were waited for; matrix products, arithmetic and copies ran while one was open for 10% of the time, Pallas kernels for 0%

profile of v8, /device:TPU:0, one launch (start us, length us, event | category | flops | bytes accessed | tf_op | source)
XLA Modules:
  0.0 220.6 jit_solution(12268022671806538351)
XLA Ops:
  7.2 0.0 copy-start
  7.2 0.0 copy-start.1
  7.2 1.2 copy.40
  8.4 0.7 iota_compare_fusion
  9.1 0.1 convert_select_fusion
  9.3 1.1 fusion.19
  10.4 0.8 pad_maximum_fusion
  11.2 1.3 collective-permute-start
  12.5 0.7 fusion.41
  13.2 0.0 copy-done.2
  13.2 0.5 copy.50
  13.7 0.4 convolution_bitcast_fusion
  14.2 0.8 scatter_fusion
  14.9 0.1 copy.42
  15.0 0.1 reshape.120
  15.2 1.1 copy.43
  16.3 2.1 reshape.145
  18.4 10.8 %all-to-all-start = ((f32[32,1,2048]{2,1,0:T(1,128)}), f32[32,1,2048]{2,1,0:T(1,128)S(1)}, u32[]{:S(2)}, u32[]{:S(2)}) async-start(f32[32,1,2048]{2,1,0:T(1,128)} %reshape.145), calls=%async_computation | async-start | bytes 524288 | tf_op jit(solution)/shard_map/all_to_all | solution.py:380
  29.2 0.0 all-gather.3.cloned.1.call-start
  29.3 8.7 %all-to-all-done = f32[32,1,2048]{2,1,0:T(1,128)S(1)} async-done(((f32[32,1,2048]{2,1,0:T(1,128)}), f32[32,1,2048]{2,1,0:T(1,128)S(1)}, u32[]{:S(2)}, u32[]{:S(2)}) %all-to-all-start) | async-done | bytes 262176 | tf_op jit(solution)/shard_map/all_to_all | solution.py:380
  38.0 0.5 broadcast.43
  38.5 1.2 reduce.1
  39.7 0.2 reshape.146
  39.9 0.1 reduce_sum.36
  40.0 0.0 collective-permute-done
  40.0 1.9 broadcast_select_fusion
  41.9 0.0 all-gather.3.cloned.1.call-update
  42.0 0.1 reshape.147
  42.1 9.3 %all_to_all.35 = f32[4,1,512]{2,1,0:T(1,128)S(1)} all-to-all(f32[4,1,512]{2,1,0:T(1,128)S(1)} %reshape.147), channel_id=1, replica_groups=mesh['yh'=2,'yl'=2,'z'=4,'x'=4,'c'=2] {'yh','yl'}, dimensions={0} | all-to-all | bytes 16384 | tf_op jit(solution)/shard_map/all_to_all | solution.py:383
  51.3 0.6 reduce.2
  51.9 0.1 reshape.148
  52.0 0.8 reshape.149
  52.9 8.4 %all-to-all-start.2 = ((f32[64,1,512]{2,1,0:T(1,128)}), f32[64,1,512]{2,1,0:T(1,128)S(1)}, u32[]{:S(2)}, u32[]{:S(2)}) async-start(f32[64,1,512]{2,1,0:T(1,128)} %reshape.149), calls=%async_computation.2 | async-start | bytes 262144 | tf_op jit(solution)/shard_map/all_to_all | solution.py:29
  61.3 0.1 pad_add_fusion.place
  61.4 9.1 %all-to-all-done.2 = f32[64,1,512]{2,1,0:T(1,128)S(1)} async-done(((f32[64,1,512]{2,1,0:T(1,128)}), f32[64,1,512]{2,1,0:T(1,128)S(1)}, u32[]{:S(2)}, u32[]{:S(2)}) %all-to-all-start.2) | async-done | bytes 131104 | tf_op jit(solution)/shard_map/all_to_all | solution.py:29
  70.5 0.9 reduce.3
  71.4 0.1 reshape.150
  71.5 0.1 copy.45
  71.5 0.1 reshape.123
  71.6 0.9 fusion.20.rhs
  72.6 45.3 %all-gather.3.cloned.1.call-done = f32[8192,512]{1,0:T(8,128)} async-done(((f32[256,512]{1,0:T(8,128)}), f32[8192,512]{1,0:T(8,128)}) %all-gather.3.cloned.1.call-update) | async-done | bytes 16777232 | tf_op jit(solution)/shard_map/all_gather | solution.py:387
  117.9 8.7 %shard_map.104 = (f32[8,8,512]{2,1,0:T(8,128)S(1)}, bf16[28,128,512]{2,1,0:T(8,128)(2,1)}, bf16[28,128,512]{2,1,0:T(8,128)(2,1)}) custom-call(s32[2]{0:T(128)S(1)} %pad_add_fusion.place, f32[32,256,512]{2,1,0:T(8,128)} %bitcast.78, bf16[16,512,512]{2,1,0:T(8,128)(2,1)} %inv.3, f32[8,8,512]{2,1,0:T(8,128)S(1)} %fusion.20.rhs), custom_call_target="tpu_custom_call" | custom-call | tf_op jit(solution)/shard_map/pallas_call | solution.py:328
  126.6 5.9 %collective-permute-start.1 = (f32[8,512]{1,0:T(8,128)S(1)}, f32[8,512]{1,0:T(8,128)S(1)}, u32[]{:S(2)}, u32[]{:S(2)}) collective-permute-start(f32[8,512]{1,0:T(8,128)S(1)} %dynamic-slice_bitcast_fusion), channel_id=1, source_target_pairs={{0,64},{1,65},{2,66},{3,67},{4,68},{5,69},{6,70},{7,71},{8,72},{9,... | collective-permute-start | bytes 49160 | tf_op jit(solution)/shard_map/ppermute | solution.py:401
  132.6 1.4 collective-permute-done.1
  134.0 0.3 fusion.9
  134.3 0.7 broadcast_in_dim.42
  135.0 4.3 %all-to-all-start.3 = ((f32[8,8,512]{2,1,0:T(8,128)}), f32[8,8,512]{2,1,0:T(8,128)S(1)}, u32[]{:S(2)}, u32[]{:S(2)}) async-start(f32[8,8,512]{2,1,0:T(8,128)} %broadcast_in_dim.42), calls=%async_computation.3 | async-start | bytes 262144 | tf_op jit(solution)/shard_map/all_to_all | solution.py:29
  139.2 6.1 %all-to-all-done.3 = f32[8,8,512]{2,1,0:T(8,128)S(1)} async-done(((f32[8,8,512]{2,1,0:T(8,128)}), f32[8,8,512]{2,1,0:T(8,128)S(1)}, u32[]{:S(2)}, u32[]{:S(2)}) %all-to-all-start.3) | async-done | bytes 131104 | tf_op jit(solution)/shard_map/all_to_all | solution.py:29
  145.3 0.7 broadcast_in_dim.43
  146.0 3.4 %all-to-all-start.4 = ((f32[8,8,512]{2,1,0:T(8,128)}), f32[8,8,512]{2,1,0:T(8,128)S(1)}, u32[]{:S(2)}, u32[]{:S(2)}) async-start(f32[8,8,512]{2,1,0:T(8,128)} %broadcast_in_dim.43), calls=%async_computation.4 | async-start | bytes 262144 | tf_op jit(solution)/shard_map/all_to_all | solution.py:29
  149.4 4.5 %constant_dynamic-slice_fusion.1 = bf16[8,512,512]{2,1,0:T(8,128)(2,1)} fusion(bf16[16,512,512]{2,1,0:T(8,128)(2,1)} %inv.3, s32[]{:T(128)S(6)} %select_n.101), kind=kLoop, calls=%fused_computation.46 | loop fusion | bytes 8388612 | tf_op jit(solution)/shard_map/dynamic_slice | solution.py:395
  153.9 6.5 %copy.51 = bf16[8,512,512]{1,2,0:T(8,128)(2,1)} copy(bf16[8,512,512]{2,1,0:T(8,128)(2,1)} %constant_dynamic-slice_fusion.1) | data formatting | bytes 8388608
  160.4 0.0 all-to-all-done.4
  160.4 9.8 %shard_map.105 = (f32[8,8,512]{2,1,0:T(8,128)S(1)}, bf16[28,128,512]{2,1,0:T(8,128)(2,1)}, bf16[28,128,512]{2,1,0:T(8,128)(2,1)}) custom-call(s32[2]{0:T(128)S(1)} %pad_add_fusion.place, f32[32,256,512]{2,1,0:T(8,128)} %bitcast.79, bf16[28,128,512]{2,1,0:T(8,128)(2,1)} %get-tuple-element.15.kept_left, bf16[28,128,512]{2,1,0:T(8,128)(2,1)} %get-tuple-element.16.kept_right, ...), custom_call_target="tpu_custom_call" | custom-call | tf_op jit(solution)/shard_map/pallas_call | solution.py:328
  170.2 0.3 fusion.10
  170.5 0.1 broadcast_in_dim.44
  170.5 18.2 %all_to_all.36 = f32[16,8,512]{2,1,0:T(8,128)S(1)} all-to-all(f32[16,8,512]{2,1,0:T(8,128)S(1)} %broadcast_in_dim.44), channel_id=1, replica_groups=mesh['yh'=2,'yl'=2,'z'=4,'x'=4,'c'=2] {'yh','yl','z'}, dimensions={0} | all-to-all | bytes 524288 | tf_op jit(solution)/shard_map/all_to_all | solution.py:29
  188.8 8.5 %all_to_all.37 = f32[8,8,512]{2,1,0:T(8,128)S(1)} all-to-all(f32[8,8,512]{2,1,0:T(8,128)S(1)} %broadcast_in_dim.45), channel_id=1, replica_groups=mesh['yh'=2,'yl'=2,'z'=4,'x'=4,'c'=2] {'x','c'}, dimensions={0} | all-to-all | bytes 262144 | tf_op jit(solution)/shard_map/all_to_all | solution.py:29
  197.3 7.4 %shard_map.106 = f32[8,8,512]{2,1,0:T(8,128)S(1)} custom-call(s32[2]{0:T(128)S(1)} %pad_add_fusion.place, bf16[28,128,512]{2,1,0:T(8,128)(2,1)} %get-tuple-element.20.kept_left, bf16[28,128,512]{2,1,0:T(8,128)(2,1)} %get-tuple-element.21.kept_right, bf16[8,512,512]{2,1,0:T(8,128)(2,1)} %bitcast.81, f32[8,8,512]{2,1,0:T(8,128)S(1)} %sub.18.rhs), custom_call_target="tpu_custom_call" | custom-call | tf_op jit(solution)/shard_map/pallas_call | solution.py:328
  204.7 0.1 collective-permute-start.2
  204.8 6.5 %collective-permute-done.2 = f32[8,8,512]{2,1,0:T(8,128)S(1)} collective-permute-done((f32[8,8,512]{2,1,0:T(8,128)S(1)}, f32[8,8,512]{2,1,0:T(8,128)S(1)}, u32[]{:S(2)}, u32[]{:S(2)}) %collective-permute-start.2) | collective-permute-done | bytes 131104 | tf_op jit(solution)/shard_map/ppermute | solution.py:416
  211.4 0.6 gather_fusion
  212.0 1.1 fusion.6
  213.1 0.7 constant_dynamic-slice_fusion
  (24 shorter events, 0.3 us)
Async XLA Ops:
  7.2 204.8 %copy-start = (bf16[1,512,512]{2,1,0:T(8,128)(2,1)S(1)}, bf16[1,512,512]{2,1,0:T(8,128)(2,1)}, u32[]{:S(2)}) copy-start(bf16[1,512,512]{2,1,0:T(8,128)(2,1)} %param.16) | copy-start | bytes 1572868
  7.2 6.0 %copy-start.1 = (bf16[1,512,1024]{2,1,0:T(8,128)(2,1)S(1)}, bf16[1,512,1024]{2,1,0:T(8,128)(2,1)}, u32[]{:S(2)}) copy-start(bf16[1,512,1024]{2,1,0:T(8,128)(2,1)} %param.15) | copy-start | bytes 3145732
  7.2 6.6 %copy-start.5 = (bf16[1,8,512]{2,1,0:T(8,128)(2,1)S(1)}, bf16[1,8,512]{2,1,0:T(8,128)(2,1)}, u32[]{:S(2)}) copy-start(bf16[1,8,512]{2,1,0:T(8,128)(2,1)} %param.14) | copy-start | bytes 24580
  9.3 3.9 %copy-start.2 = (f32[128,512]{1,0:T(8,128)}, f32[128,512]{1,0:T(8,128)S(1)}, u32[]{:S(2)}) copy-start(f32[128,512]{1,0:T(8,128)S(1)} %fusion.14) | copy-start | bytes 786436
  11.2 28.7 %collective-permute-start = (f32[256,512]{1,0:T(8,128)}, f32[256,512]{1,0:T(8,128)}, u32[]{:S(2)}, u32[]{:S(2)}) collective-permute-start(f32[256,512]{1,0:T(8,128)} %pad_maximum_fusion), channel_id=1, source_target_pairs={{8,47},{16,54},{17,55},{24,38},{25,63},{26,39},{32,0},{33,1},{34,2... | collective-permute-start | bytes 1572872 | tf_op jit(solution)/shard_map/ppermute | solution.py:369
  14.1 25.9 %copy-start.3 = (f32[128,512]{1,0:T(8,128)S(1)}, f32[128,512]{1,0:T(8,128)}, u32[]{:S(2)}) copy-start(f32[128,512]{1,0:T(8,128)} %copy-done.2) | copy-start | bytes 786436
  18.4 19.6 %all-to-all-start = ((f32[32,1,2048]{2,1,0:T(1,128)}), f32[32,1,2048]{2,1,0:T(1,128)S(1)}, u32[]{:S(2)}, u32[]{:S(2)}) async-start(f32[32,1,2048]{2,1,0:T(1,128)} %reshape.145), calls=%async_computation | async-start | bytes 524288 | tf_op jit(solution)/shard_map/all_to_all | solution.py:380
  29.2 88.7 %all-gather.3.cloned.1.call-start = ((), (), s32[]{:S(2)}) async-start(), calls=%async_computation.7 | async-start | bytes 17301504 | tf_op jit(solution)/shard_map/all_gather | solution.py:387
  52.9 17.6 %all-to-all-start.2 = ((f32[64,1,512]{2,1,0:T(1,128)}), f32[64,1,512]{2,1,0:T(1,128)S(1)}, u32[]{:S(2)}, u32[]{:S(2)}) async-start(f32[64,1,512]{2,1,0:T(1,128)} %reshape.149), calls=%async_computation.2 | async-start | bytes 262144 | tf_op jit(solution)/shard_map/all_to_all | solution.py:29
  117.9 16.1 %copy-start.4 = (bf16[1,1,1,2,128,512]{5,4,3,2,1,0:T(8,128)(2,1)S(1)}, bf16[1,1,1,2,128,512]{5,4,3,2,1,0:T(8,128)(2,1)}, u32[]{:S(2)}) copy-start(bf16[1,1,1,2,128,512]{5,4,3,2,1,0:T(8,128)(2,1)} %param.11) | copy-start | bytes 786436
  126.6 7.4 %collective-permute-start.1 = (f32[8,512]{1,0:T(8,128)S(1)}, f32[8,512]{1,0:T(8,128)S(1)}, u32[]{:S(2)}, u32[]{:S(2)}) collective-permute-start(f32[8,512]{1,0:T(8,128)S(1)} %dynamic-slice_bitcast_fusion), channel_id=1, source_target_pairs={{0,64},{1,65},{2,66},{3,67},{4,68},{5,69},{6,70},{7,71},{8,72},{9,... | collective-permute-start | bytes 49160 | tf_op jit(solution)/shard_map/ppermute | solution.py:401
  135.0 10.4 %all-to-all-start.3 = ((f32[8,8,512]{2,1,0:T(8,128)}), f32[8,8,512]{2,1,0:T(8,128)S(1)}, u32[]{:S(2)}, u32[]{:S(2)}) async-start(f32[8,8,512]{2,1,0:T(8,128)} %broadcast_in_dim.42), calls=%async_computation.3 | async-start | bytes 262144 | tf_op jit(solution)/shard_map/all_to_all | solution.py:29
  146.0 14.4 %all-to-all-start.4 = ((f32[8,8,512]{2,1,0:T(8,128)}), f32[8,8,512]{2,1,0:T(8,128)S(1)}, u32[]{:S(2)}, u32[]{:S(2)}) async-start(f32[8,8,512]{2,1,0:T(8,128)} %broadcast_in_dim.43), calls=%async_computation.4 | async-start | bytes 262144 | tf_op jit(solution)/shard_map/all_to_all | solution.py:29
  204.7 6.6 %collective-permute-start.2 = (f32[8,8,512]{2,1,0:T(8,128)S(1)}, f32[8,8,512]{2,1,0:T(8,128)S(1)}, u32[]{:S(2)}, u32[]{:S(2)}) collective-permute-start(f32[8,8,512]{2,1,0:T(8,128)S(1)} %broadcast_select_fusion.3), channel_id=1, source_target_pairs={{0,64},{64,0},{1,65},{65,1},{2,66},{66,2},{3,67},{67,3},{4,68},{68... | collective-permute-start | bytes 393224 | tf_op jit(solution)/shard_map/ppermute | solution.py:416
Sparse Core Ops, SparseCore 0:
  42.1 75.7 all-gather.2

commit v9 on v8

--- a/solution.py
+++ b/solution.py
@@ -76,8 +76,8 @@
 
 
 class Leaf:
-    def __init__(self, left, right, diag=None, flipped=None):
-        self.left, self.right, self.diag, self.flipped = left, right, diag, flipped
+    def __init__(self, left, right, diag):
+        self.left, self.right, self.diag = left, right, diag
 
     def column(self, j):
         return sum(HALF - 1 - m for m in range(j))
@@ -212,7 +212,7 @@
         acc = partial
         if j + 1 < HALF:
             acc = acc - dot_nn(last, leaf.vt(j + 1, j))
-        z = exact(dot_nn, acc, leaf.flipped[j])
+        z = exact(dot_nt, acc, leaf.diag[j])
         if j:
             if load:
                 load(j - 1)
@@ -266,10 +266,9 @@
         keep_tiles(leaf, place, tiles, stage, sems, (kept_left, kept_right), lsems, rsems)
 
 
-def second_kernel(place, tiles, kept_left, kept_right, inv, turned, rhs, *refs):
-    out, next_left, next_right, stage, left, right, diag, flipped = refs[:8]
-    sems, dsems, tsems, lsems, rsems = refs[8:]
-    leaf = Leaf(left, right, diag, flipped)
+def second_kernel(place, tiles, kept_left, kept_right, inv, rhs, *refs):
+    out, next_left, next_right, stage, left, right, diag, sems, dsems, lsems, rsems = refs
+    leaf = Leaf(left, right, diag)
 
     @pl.when(place[1] == 0)
     def _():
@@ -281,24 +280,18 @@
         inverse = inverse_moves(diag, HALF, inv, dsems)
         factors = factor_moves(leaf, kept_left, kept_right, lsems, rsems, False)
         load = Reloader(inverse, factors, range(HALF))
-        turn = inverse_moves(flipped, 0, turned, tsems)
-        for n in range(HALF):
-            turn.start(n)
-        solved = forward(leaf, values(rhs), load)
-        for n in range(HALF):
-            turn.wait(n)
-        put(out, backward(leaf, solved))
-
-
-def third_kernel(place, kept_left, kept_right, turned, rhs, out, left, right, flipped, *sems):
-    tsems, lsems, rsems = sems
-    leaf = Leaf(left, right, flipped=flipped)
+        put(out, backward(leaf, forward(leaf, values(rhs), load)))
+
+
+def third_kernel(place, kept_left, kept_right, inv, rhs, out, left, right, diag, *sems):
+    dsems, lsems, rsems = sems
+    leaf = Leaf(left, right, diag)
 
     @pl.when(place[1] == 0)
     def _():
-        turn = inverse_moves(flipped, 0, turned, tsems)
+        inverse = inverse_moves(diag, 0, inv, dsems)
         factors = factor_moves(leaf, kept_left, kept_right, lsems, rsems, False)
-        load = Reloader(turn, factors, range(HALF)[::-1])
+        load = Reloader(inverse, factors, range(HALF)[::-1])
         put(out, backward(leaf, values(rhs), load))
 
     @pl.when(place[1] == 1)
@@ -319,7 +312,7 @@
     return pltpu.with_memory_space_constraint(v, pltpu.HBM)
 
 
-def solve(body, place, hbm, rhs, keeps, loads, inverses):
+def solve(body, place, hbm, rhs, keeps, loads):
     tile = rhs.shape[2]
     rank = tile // 4
     dma = pltpu.SemaphoreType.DMA
@@ -333,9 +326,9 @@
         scratch_shapes=[
             *[pltpu.VMEM((SLOTS, HALF - 1, 2 * rank, tile), F32)] * loads,
             *[pltpu.VMEM((TILES, rank, tile), BF)] * 2,
-            *[pltpu.VMEM((HALF, tile, tile), BF)] * inverses,
+            pltpu.VMEM((HALF, tile, tile), BF),
             *[dma((TILES,))] * loads,
-            *[dma((HALF,))] * inverses,
+            dma((HALF,)),
             dma((HALF,)),
             dma((TILES,)),
         ],
@@ -376,12 +369,10 @@
     flat_blocks = child_blocks.reshape(-1)
     dense = jnp.zeros((rhs_count, nblk, BLK), F32).at[:, flat_blocks, :].add(pieces)
     width = ntile * tile // ndev
-    parts = dense.reshape(rhs_count * 4, ndev // 4, width).transpose(1, 0, 2)
-    mine = lax.all_to_all(parts, PLANE, split_axis=0, concat_axis=0, tiled=True).sum(axis=0)
-    other_tile, mine = lax.optimization_barrier((other_tile, mine))
-    mine = mine.reshape(rhs_count, 4, width).transpose(1, 0, 2)
-    mine = lax.all_to_all(mine, ("yh", "yl"), split_axis=0, concat_axis=0, tiled=True)
-    mine = mine.sum(axis=0)
+    parts = dense.reshape(rhs_count, 4, ntile * tile // 4).transpose(1, 0, 2)
+    mine = lax.all_to_all(parts, ("yh", "yl"), split_axis=0, concat_axis=0, tiled=True)
+    mine = mine.sum(axis=0).reshape(rhs_count, ndev // 4, width).transpose(1, 0, 2)
+    mine = lax.all_to_all(mine, PLANE, split_axis=0, concat_axis=0, tiled=True).sum(axis=0)
     share = jnp.where(my_col < in_half, own_tile, other_tile)
     share = with_layout_constraint(share, ROWS)
     tiles = lax.all_gather(share, PLANE)
@@ -391,10 +382,8 @@
     given = root_rhs.reshape(rhs_count, ntile, tile)
     given = lax.dynamic_slice_in_dim(given, HALF * half, HALF, 1)
     own_rhs = given.transpose(1, 0, 2).astype(F32) - child_sum
-    begin, own_rhs = lax.optimization_barrier((HALF * half, own_rhs))
-    turned = lax.dynamic_slice_in_dim(diag_inv, begin, HALF, 0).transpose(0, 2, 1)
-
-    x_low, *kept = solve(first_kernel, place, [tiles, diag_inv], own_rhs, True, 1, 1)
+
+    x_low, *kept = solve(first_kernel, place, [tiles, diag_inv], own_rhs, True, 1)
     v0 = right[0].astype(BF)
     u0 = left[0]
     x_col = lax.dynamic_index_in_dim(x_low, my_col, 0, keepdims=False)
@@ -403,15 +392,15 @@
     p = dot_nn(x_own.astype(BF), v0).astype(BF)
     row_sum = copies(dot_nn(p, u0), COL).reshape(8, rhs_count, tile).sum(axis=0)
     row_sums = copies(row_sum, HALF_ROW).reshape(HALF, rhs_count, tile)
-    arrays = [tiles, *kept, diag_inv, turned]
-    z_high, *kept = solve(second_kernel, place, arrays, own_rhs - row_sums, True, 1, 2)
+    arrays = [tiles, *kept, diag_inv]
+    z_high, *kept = solve(second_kernel, place, arrays, own_rhs - row_sums, True, 1)
 
     z_own = lax.dynamic_index_in_dim(z_high, in_half, 0, keepdims=False).astype(BF)
     q = dot_nt(z_own, u0).astype(BF)
     col_sum = copies(dot_nt(q, v0), ROW).reshape(2, HALF, rhs_count, tile)[1].sum(axis=0)
     col_sums = copies(col_sum, COL).reshape(8, rhs_count, tile)
     low_rhs = x_low - col_sums
-    z_low = solve(third_kernel, place, [*kept, turned], low_rhs, False, 0, 1)
+    z_low = solve(third_kernel, place, [*kept, diag_inv], low_rhs, False, 0)
     z_mine = jnp.where(upper, z_high, z_low)
     z_other = lax.ppermute(z_mine, "yh", [(0, 1), (1, 0)])
     low_part = jnp.where(upper, z_other, z_mine)

time: 222 us -> 212 us (0.955)
  blocking collectives: 36 us -> 73.3 us
  starting transfers between devices: 34.2 us -> 15 us
  local copies, waits for them, and re-layouts: 20.9 us -> 6.18 us
  waiting for transfers between devices: 77.2 us -> 68.2 us
  other arithmetic: 10 us -> 6.42 us
    all_to_all x1 -> x2, blocking collectives: 9.27 us -> 39.4 us  [the longest x1 27.6 us: per_device(): lax.all_to_all(mine, PLANE, split_axis=0, concat_axis=0, tiled=True)]
    all_gather x1, waiting for transfers between devices: 45.3 us -> 30.5 us  [per_device(): tiles = lax.all_gather(share, PLANE)]
    ppermute x1, waiting for transfers between devices: 0.01 us -> 13.8 us  [per_device(): other_tile = lax.ppermute(own_tile, ALL, plane_pairs())]
    all_to_all x1 -> x0, starting transfers between devices: 10.8 us -> none  [per_device(): lax.all_to_all(parts, PLANE, split_axis=0, concat_axis=0, tiled=True)]
    unnamed x20 -> x17, local copies, waits for them, and re-layouts: 11.1 us -> 2.37 us
    all_to_all x1 -> x0, waiting for transfers between devices: 8.71 us -> none  [per_device(): lax.all_to_all(parts, PLANE, split_axis=0, concat_axis=0, tiled=True)]
    all_to_all x3 -> x2, starting transfers between devices: 16 us -> 7.98 us  [copies(): lax.all_to_all(stacked, axis, split_axis=0, concat_axis=0, tiled=True)]
    all_to_all x2 -> x3, blocking collectives: 26.7 us -> 34 us  [copies(): lax.all_to_all(stacked, axis, split_axis=0, concat_axis=0, tiled=True)]
  transfers between devices with their start and end apart: 8 -> 6, of which waited for: 6 -> 6; matrix products, arithmetic and copies ran while one was open for 10% -> 3% of each run, Pallas kernels for 0% -> 0%
where the time goes in v9:
time: 212 us
  blocking collectives  73.3 us (35%)
  waiting for transfers between devices  68.2 us (32%)
  Pallas kernels  26.1 us (12%)
  starting transfers between devices  15 us (7%)
  between operations  14.4 us (7%)
  other arithmetic  6.42 us (3%)
  local copies, waits for them, and re-layouts  6.18 us (3%)
    all_to_all x3, blocking collectives, copies(): lax.all_to_all(stacked, axis, split_axis=0, concat_axis=0, tiled=True)  34 us
    all_gather x1, waiting for transfers between devices, per_device(): tiles = lax.all_gather(share, PLANE)  30.5 us
    all_to_all x1, blocking collectives, per_device(): lax.all_to_all(mine, PLANE, split_axis=0, concat_axis=0, tiled=True)  27.6 us
    pallas_call x3, Pallas kernels, solve(): pl.pallas_call(body, out_shape=(solved, factors, factors) if keeps else s...  26.1 us
    all_to_all x2, waiting for transfers between devices, copies(): lax.all_to_all(stacked, axis, split_axis=0, concat_axis=0, tiled=True)  16 us
    ppermute x1, waiting for transfers between devices, per_device(): other_tile = lax.ppermute(own_tile, ALL, plane_pairs())  13.8 us
    all_to_all x1, blocking collectives, per_device(): lax.all_to_all(parts, ('yh', 'yl'), split_axis=0, concat_axis=0, tiled=True)  11.7 us
    all_to_all x2, starting transfers between devices, copies(): lax.all_to_all(stacked, axis, split_axis=0, concat_axis=0, tiled=True)  7.98 us
  transfers between devices with their start and end apart: 6, of which 6 were waited for; matrix products, arithmetic and copies ran while one was open for 3% of the time, Pallas kernels for 0%

profile of v9, /device:TPU:0, one launch (start us, length us, event | category | flops | bytes accessed | tf_op | source)
XLA Modules:
  0.0 211.7 jit_solution(2663051132788595565)
XLA Ops:
  7.2 0.0 copy-start
  7.2 0.0 copy-start.1
  7.2 0.0 all-gather.3.cloned.1.call-start
  7.2 1.2 copy.36
  8.4 0.7 iota_compare_fusion
  9.2 0.0 copy-start.5
  9.2 0.0 copy-start.3
  9.2 0.1 convert_select_fusion
  9.3 1.0 fusion.19
  10.3 0.8 pad_maximum_fusion
  11.2 1.3 collective-permute-start
  12.5 13.8 %collective-permute-done = f32[256,512]{1,0:T(8,128)S(1)} collective-permute-done((f32[256,512]{1,0:T(8,128)}, f32[256,512]{1,0:T(8,128)S(1)}, u32[]{:S(2)}, u32[]{:S(2)}) %collective-permute-start) | collective-permute-done | bytes 524320 | tf_op jit(solution)/shard_map/ppermute | solution.py:362
  26.2 0.9 broadcast_select_fusion
  27.1 0.0 all-gather.3.cloned.1.call-update
  27.2 0.0 copy-done.1
  27.2 0.5 copy.45
  27.7 0.0 copy-done.5
  27.7 0.0 copy-done.3
  27.8 0.4 convolution_bitcast_fusion
  28.1 0.0 copy-start.4
  28.2 0.8 scatter_fusion
  29.0 0.1 copy.38
  29.0 0.1 reshape.121
  29.1 0.2 copy.39
  29.3 11.7 %all_to_all.35 = f32[4,8,2048]{2,1,0:T(8,128)S(1)} all-to-all(f32[4,8,2048]{2,1,0:T(8,128)S(1)} %copy.39), channel_id=1, replica_groups=mesh['yh'=2,'yl'=2,'z'=4,'x'=4,'c'=2] {'yh','yl'}, dimensions={0} | all-to-all | bytes 524288 | tf_op jit(solution)/shard_map/all_to_all | solution.py:373
  41.0 0.1 reshape.122
  41.1 0.1 copy.40
  41.2 0.1 reshape.145
  41.3 27.6 %all_to_all.36 = f32[32,1,512]{2,1,0:T(1,128)S(1)} all-to-all(f32[32,1,512]{2,1,0:T(1,128)S(1)} %reshape.145), channel_id=1, replica_groups=mesh['yh'=2,'yl'=2,'z'=4,'x'=4,'c'=2] {'z','x','c'}, dimensions={0} | all-to-all | bytes 131072 | tf_op jit(solution)/shard_map/all_to_all | solution.py:375
  69.0 0.6 broadcast.43
  69.5 0.8 reduce.1
  70.3 0.1 reshape.146
  70.4 0.8 reshape.147
  71.3 4.6 %all-to-all-start.2 = ((f32[64,1,512]{2,1,0:T(1,128)}), f32[64,1,512]{2,1,0:T(1,128)S(1)}, u32[]{:S(2)}, u32[]{:S(2)}) async-start(f32[64,1,512]{2,1,0:T(1,128)} %reshape.147), calls=%async_computation.2 | async-start | bytes 262144 | tf_op jit(solution)/shard_map/all_to_all | solution.py:29
  75.9 0.1 pad_add_fusion.place
  76.0 9.5 %all-to-all-done.2 = f32[64,1,512]{2,1,0:T(1,128)S(1)} async-done(((f32[64,1,512]{2,1,0:T(1,128)}), f32[64,1,512]{2,1,0:T(1,128)S(1)}, u32[]{:S(2)}, u32[]{:S(2)}) %all-to-all-start.2) | async-done | bytes 131104 | tf_op jit(solution)/shard_map/all_to_all | solution.py:29
  85.5 0.9 reduce.2
  86.4 0.1 reshape.148
  86.5 0.1 copy.41
  86.6 0.1 reshape.123
  86.7 0.0 copy-done.4
  86.7 0.1 fusion.20.rhs
  86.8 30.5 %all-gather.3.cloned.1.call-done = f32[8192,512]{1,0:T(8,128)} async-done(((f32[256,512]{1,0:T(8,128)}), f32[8192,512]{1,0:T(8,128)}) %all-gather.3.cloned.1.call-update) | async-done | bytes 16777232 | tf_op jit(solution)/shard_map/all_gather | solution.py:378
  117.3 8.7 %shard_map.104 = (f32[8,8,512]{2,1,0:T(8,128)S(1)}, bf16[28,128,512]{2,1,0:T(8,128)(2,1)}, bf16[28,128,512]{2,1,0:T(8,128)(2,1)}) custom-call(s32[2]{0:T(128)S(1)} %pad_add_fusion.place, f32[32,256,512]{2,1,0:T(8,128)} %bitcast.75, bf16[16,512,512]{2,1,0:T(8,128)(2,1)} %inv.5, f32[8,8,512]{2,1,0:T(8,128)S(1)} %fusion.20.rhs), custom_call_target="tpu_custom_call" | custom-call | tf_op jit(solution)/shard_map/pallas_call | solution.py:321
  126.0 5.6 %collective-permute-start.1 = (f32[8,512]{1,0:T(8,128)S(1)}, f32[8,512]{1,0:T(8,128)S(1)}, u32[]{:S(2)}, u32[]{:S(2)}) collective-permute-start(f32[8,512]{1,0:T(8,128)S(1)} %dynamic-slice_bitcast_fusion), channel_id=1, source_target_pairs={{0,64},{1,65},{2,66},{3,67},{4,68},{5,69},{6,70},{7,71},{8,72},{9,... | collective-permute-start | bytes 49160 | tf_op jit(solution)/shard_map/ppermute | solution.py:390
  131.6 1.4 collective-permute-done.1
  133.0 0.0 copy-done.2
  133.0 0.3 fusion.9
  133.4 9.6 %all_to_all.37 = f32[8,8,512]{2,1,0:T(8,128)S(1)} all-to-all(f32[8,8,512]{2,1,0:T(8,128)S(1)} %broadcast_in_dim.42), channel_id=1, replica_groups=mesh['yh'=2,'yl'=2,'z'=4,'x'=4,'c'=2] {'x','c'}, dimensions={0} | all-to-all | bytes 262144 | tf_op jit(solution)/shard_map/all_to_all | solution.py:29
  143.0 0.7 broadcast_in_dim.43
  143.7 3.4 %all-to-all-start.4 = ((f32[8,8,512]{2,1,0:T(8,128)}), f32[8,8,512]{2,1,0:T(8,128)S(1)}, u32[]{:S(2)}, u32[]{:S(2)}) async-start(f32[8,8,512]{2,1,0:T(8,128)} %broadcast_in_dim.43), calls=%async_computation.4 | async-start | bytes 262144 | tf_op jit(solution)/shard_map/all_to_all | solution.py:29
  147.1 6.5 %all-to-all-done.4 = f32[8,8,512]{2,1,0:T(8,128)S(1)} async-done(((f32[8,8,512]{2,1,0:T(8,128)}), f32[8,8,512]{2,1,0:T(8,128)S(1)}, u32[]{:S(2)}, u32[]{:S(2)}) %all-to-all-start.4) | async-done | bytes 131104 | tf_op jit(solution)/shard_map/all_to_all | solution.py:29
  153.6 9.8 %shard_map.105 = (f32[8,8,512]{2,1,0:T(8,128)S(1)}, bf16[28,128,512]{2,1,0:T(8,128)(2,1)}, bf16[28,128,512]{2,1,0:T(8,128)(2,1)}) custom-call(s32[2]{0:T(128)S(1)} %pad_add_fusion.place, f32[32,256,512]{2,1,0:T(8,128)} %bitcast.76, bf16[28,128,512]{2,1,0:T(8,128)(2,1)} %get-tuple-element.8.kept_left, bf16[28,128,512]{2,1,0:T(8,128)(2,1)} %get-tuple-element.9.kept_right, ...), custom_call_target="tpu_custom_call" | custom-call | tf_op jit(solution)/shard_map/pallas_call | solution.py:321
  163.4 0.3 fusion.10
  163.6 0.1 broadcast_in_dim.44
  163.7 15.8 %all_to_all.38 = f32[16,8,512]{2,1,0:T(8,128)S(1)} all-to-all(f32[16,8,512]{2,1,0:T(8,128)S(1)} %broadcast_in_dim.44), channel_id=1, replica_groups=mesh['yh'=2,'yl'=2,'z'=4,'x'=4,'c'=2] {'yh','yl','z'}, dimensions={0} | all-to-all | bytes 524288 | tf_op jit(solution)/shard_map/all_to_all | solution.py:29
  179.6 8.5 %all_to_all.39 = f32[8,8,512]{2,1,0:T(8,128)S(1)} all-to-all(f32[8,8,512]{2,1,0:T(8,128)S(1)} %broadcast_in_dim.45), channel_id=1, replica_groups=mesh['yh'=2,'yl'=2,'z'=4,'x'=4,'c'=2] {'x','c'}, dimensions={0} | all-to-all | bytes 262144 | tf_op jit(solution)/shard_map/all_to_all | solution.py:29
  188.1 7.6 %shard_map.106 = f32[8,8,512]{2,1,0:T(8,128)S(1)} custom-call(s32[2]{0:T(128)S(1)} %pad_add_fusion.place, bf16[28,128,512]{2,1,0:T(8,128)(2,1)} %get-tuple-element.12.kept_left, bf16[28,128,512]{2,1,0:T(8,128)(2,1)} %get-tuple-element.13.kept_right, bf16[16,512,512]{2,1,0:T(8,128)(2,1)} %inv.5, f32[8,8,512]{2,1,0:T(8,128)S(1)} %sub.17.rhs), custom_call_target="tpu_custom_call" | custom-call | tf_op jit(solution)/shard_map/pallas_call | solution.py:321
  195.8 0.1 collective-permute-start.2
  195.9 6.5 %collective-permute-done.2 = f32[8,8,512]{2,1,0:T(8,128)S(1)} collective-permute-done((f32[8,8,512]{2,1,0:T(8,128)S(1)}, f32[8,8,512]{2,1,0:T(8,128)S(1)}, u32[]{:S(2)}, u32[]{:S(2)}) %collective-permute-start.2) | collective-permute-done | bytes 131104 | tf_op jit(solution)/shard_map/ppermute | solution.py:405
  202.4 0.6 gather_fusion
  203.0 0.0 copy-done
  203.0 1.1 fusion.6
  204.2 0.7 constant_dynamic-slice_fusion
  (18 shorter events, 0.4 us)
Async XLA Ops:
  7.2 195.9 %copy-start = (bf16[1,512,512]{2,1,0:T(8,128)(2,1)S(1)}, bf16[1,512,512]{2,1,0:T(8,128)(2,1)}, u32[]{:S(2)}) copy-start(bf16[1,512,512]{2,1,0:T(8,128)(2,1)} %param.16) | copy-start | bytes 1572868
  7.2 20.0 %copy-start.1 = (bf16[1,512,1024]{2,1,0:T(8,128)(2,1)S(1)}, bf16[1,512,1024]{2,1,0:T(8,128)(2,1)}, u32[]{:S(2)}) copy-start(bf16[1,512,1024]{2,1,0:T(8,128)(2,1)} %param.15) | copy-start | bytes 3145732
  7.2 110.1 %all-gather.3.cloned.1.call-start = ((), (), s32[]{:S(2)}) async-start(), calls=%async_computation.7 | async-start | bytes 17301504 | tf_op jit(solution)/shard_map/all_gather | solution.py:378
  9.2 18.5 %copy-start.5 = (s32[1,8]{1,0:T(1,128)S(1)}, s32[1,8]{1,0:T(1,128)}, u32[]{:S(2)}) copy-start(s32[1,8]{1,0:T(1,128)} %param.17) | copy-start | bytes 100
  9.2 18.6 %copy-start.3 = (bf16[1,8,512]{2,1,0:T(8,128)(2,1)S(1)}, bf16[1,8,512]{2,1,0:T(8,128)(2,1)}, u32[]{:S(2)}) copy-start(bf16[1,8,512]{2,1,0:T(8,128)(2,1)} %param.14) | copy-start | bytes 24580
  11.2 15.1 %collective-permute-start = (f32[256,512]{1,0:T(8,128)}, f32[256,512]{1,0:T(8,128)S(1)}, u32[]{:S(2)}, u32[]{:S(2)}) collective-permute-start(f32[256,512]{1,0:T(8,128)} %pad_maximum_fusion), channel_id=1, source_target_pairs={{8,47},{16,54},{17,55},{24,38},{25,63},{26,39},{32,0},{33,1},{34,2... | collective-permute-start | bytes 1572872 | tf_op jit(solution)/shard_map/ppermute | solution.py:362
  28.1 58.6 %copy-start.4 = (bf16[8,8192]{1,0:T(8,128)(2,1)S(1)}, bf16[8,8192]{1,0:T(8,128)(2,1)}, u32[]{:S(2)}) copy-start(bf16[8,8192]{1,0:T(8,128)(2,1)} %param.9) | copy-start | bytes 393220
  71.3 14.2 %all-to-all-start.2 = ((f32[64,1,512]{2,1,0:T(1,128)}), f32[64,1,512]{2,1,0:T(1,128)S(1)}, u32[]{:S(2)}, u32[]{:S(2)}) async-start(f32[64,1,512]{2,1,0:T(1,128)} %reshape.147), calls=%async_computation.2 | async-start | bytes 262144 | tf_op jit(solution)/shard_map/all_to_all | solution.py:29
  117.3 15.7 %copy-start.2 = (bf16[1,1,1,2,128,512]{5,4,3,2,1,0:T(8,128)(2,1)S(1)}, bf16[1,1,1,2,128,512]{5,4,3,2,1,0:T(8,128)(2,1)}, u32[]{:S(2)}) copy-start(bf16[1,1,1,2,128,512]{5,4,3,2,1,0:T(8,128)(2,1)} %param.11) | copy-start | bytes 786436
  126.0 7.0 %collective-permute-start.1 = (f32[8,512]{1,0:T(8,128)S(1)}, f32[8,512]{1,0:T(8,128)S(1)}, u32[]{:S(2)}, u32[]{:S(2)}) collective-permute-start(f32[8,512]{1,0:T(8,128)S(1)} %dynamic-slice_bitcast_fusion), channel_id=1, source_target_pairs={{0,64},{1,65},{2,66},{3,67},{4,68},{5,69},{6,70},{7,71},{8,72},{9,... | collective-permute-start | bytes 49160 | tf_op jit(solution)/shard_map/ppermute | solution.py:390
  143.7 9.9 %all-to-all-start.4 = ((f32[8,8,512]{2,1,0:T(8,128)}), f32[8,8,512]{2,1,0:T(8,128)S(1)}, u32[]{:S(2)}, u32[]{:S(2)}) async-start(f32[8,8,512]{2,1,0:T(8,128)} %broadcast_in_dim.43), calls=%async_computation.4 | async-start | bytes 262144 | tf_op jit(solution)/shard_map/all_to_all | solution.py:29
  195.8 6.6 %collective-permute-start.2 = (f32[8,8,512]{2,1,0:T(8,128)S(1)}, f32[8,8,512]{2,1,0:T(8,128)S(1)}, u32[]{:S(2)}, u32[]{:S(2)}) collective-permute-start(f32[8,8,512]{2,1,0:T(8,128)S(1)} %broadcast_select_fusion.3), channel_id=1, source_target_pairs={{0,64},{64,0},{1,65},{65,1},{2,66},{66,2},{3,67},{67,3},{4,68},{68... | collective-permute-start | bytes 393224 | tf_op jit(solution)/shard_map/ppermute | solution.py:405
Sparse Core Ops, SparseCore 0:
  27.3 89.9 all-gather.2

commit v10 on v7

--- a/solution.py
+++ b/solution.py
@@ -353,8 +353,10 @@
     width = ntile * tile // ndev
     parts = dense.reshape(rhs_count, 4, ntile * tile // 4).transpose(1, 0, 2)
     mine = lax.all_to_all(parts, ("yh", "yl"), split_axis=0, concat_axis=0, tiled=True)
-    mine = mine.sum(axis=0).reshape(rhs_count, ndev // 4, width).transpose(1, 0, 2)
-    mine = lax.all_to_all(mine, PLANE, split_axis=0, concat_axis=0, tiled=True).sum(axis=0)
+    mine = mine.sum(axis=0).reshape(rhs_count, 4, tile).transpose(1, 0, 2)
+    mine = lax.all_to_all(mine, "z", split_axis=0, concat_axis=0, tiled=True).sum(axis=0)
+    mine = mine.reshape(rhs_count, 8, width).transpose(1, 0, 2)
+    mine = lax.all_to_all(mine, COL, split_axis=0, concat_axis=0, tiled=True).sum(axis=0)
     share = jnp.where(my_col < in_half, own_tile, other_tile)
     share = with_layout_constraint(share, ROWS)
     tiles = lax.all_gather(share, PLANE)

time: 213 us -> 213 us (level)
  blocking collectives: 71.9 us -> 77 us
  waiting for transfers between devices: 63.9 us -> 59.1 us
    all_to_all x1 -> x2, blocking collectives: 27.5 us -> 32.7 us  [the longest x1 17.5 us: per_device(): lax.all_to_all(mine, 'z', split_axis=0, concat_axis=0, tiled=True)]
    all_gather x1, waiting for transfers between devices: 27.2 us -> 22.5 us  [per_device(): tiles = lax.all_gather(share, PLANE)]
where the time goes in v10:
time: 213 us; the launch traced here: 212 us
  blocking collectives  77 us (36%)
  waiting for transfers between devices  59.1 us (28%)
  Pallas kernels  30.1 us (14%)
  starting transfers between devices  15.6 us (7%)
  between operations  14.4 us (7%)
  local copies, waits for them, and re-layouts  6.93 us (3%)
  other arithmetic  6.16 us (3%)
  matrix products  2.77 us (1%)
    all_to_all x3, blocking collectives, copies(): lax.all_to_all(stacked, axis, split_axis=0, concat_axis=0, tiled=True)  32.6 us
    all_gather x1, waiting for transfers between devices, per_device(): tiles = lax.all_gather(share, PLANE)  22.5 us
    pallas_call x2, Pallas kernels, solve(): pl.pallas_call(body, out_shape=jax.ShapeDtypeStruct(rhs.shape, F32), in_s...  18.8 us
    all_to_all x1, blocking collectives, per_device(): lax.all_to_all(mine, 'z', split_axis=0, concat_axis=0, tiled=True)  17.5 us
    all_to_all x2, waiting for transfers between devices, copies(): lax.all_to_all(stacked, axis, split_axis=0, concat_axis=0, tiled=True)  16.5 us
    all_to_all x1, blocking collectives, per_device(): lax.all_to_all(mine, COL, split_axis=0, concat_axis=0, tiled=True)  15.2 us
    ppermute x1, waiting for transfers between devices, per_device(): other_tile = lax.ppermute(own_tile, ALL, plane_pairs())  13.6 us
    all_to_all x1, blocking collectives, per_device(): lax.all_to_all(parts, ('yh', 'yl'), split_axis=0, concat_axis=0, tiled=True)  11.7 us
  transfers between devices with their start and end apart: 6, of which 6 were waited for; matrix products, arithmetic and copies ran while one was open for 4% of the time, Pallas kernels for 0%

profile of v10, /device:TPU:0, one launch (start us, length us, event | category | flops | bytes accessed | tf_op | source)
XLA Modules:
  0.0 212.1 jit_solution(15009385691243887423)
XLA Ops:
  7.2 0.0 copy-start
  7.2 0.0 copy-start.4
  7.2 0.0 all-gather.3.cloned.1.call-start
  7.2 1.1 copy.36
  8.4 0.7 iota_compare_fusion
  9.1 0.1 convert_select_fusion
  9.3 1.0 fusion.19
  10.3 1.3 collective-permute-start
  11.6 13.6 %collective-permute-done = f32[256,512]{1,0:T(8,128)S(1)} collective-permute-done((f32[256,512]{1,0:T(8,128)S(1)}, f32[256,512]{1,0:T(8,128)S(1)}, u32[]{:S(2)}, u32[]{:S(2)}) %collective-permute-start) | collective-permute-done | bytes 524320 | tf_op jit(solution)/shard_map/ppermute | solution.py:344
  25.2 0.9 broadcast_select_fusion
  26.1 0.0 all-gather.3.cloned.1.call-update
  26.1 1.5 copy.45
  27.6 0.7 fusion.41
  28.3 1.1 convolution_bitcast_fusion
  29.4 0.8 scatter_fusion
  30.2 0.1 copy.38
  30.2 0.1 reshape.124
  30.3 0.2 copy.39
  30.5 11.7 %all_to_all.40 = f32[4,8,2048]{2,1,0:T(8,128)S(1)} all-to-all(f32[4,8,2048]{2,1,0:T(8,128)S(1)} %copy.39), channel_id=1, replica_groups=mesh['yh'=2,'yl'=2,'z'=4,'x'=4,'c'=2] {'yh','yl'}, dimensions={0} | all-to-all | bytes 524288 | tf_op jit(solution)/shard_map/all_to_all | solution.py:355
  42.2 17.5 %all_to_all.41 = f32[4,8,512]{2,1,0:T(8,128)S(1)} all-to-all(f32[4,8,512]{2,1,0:T(8,128)S(1)} %bitcast.85), channel_id=1, replica_groups=mesh['yh'=2,'yl'=2,'z'=4,'x'=4,'c'=2] {'z'}, dimensions={0} | all-to-all | bytes 131072 | tf_op jit(solution)/shard_map/all_to_all | solution.py:357
  59.7 0.1 reshape.126
  59.8 0.1 reshape.149
  59.9 15.2 %all_to_all.42 = f32[8,1,512]{2,1,0:T(1,128)S(1)} all-to-all(f32[8,1,512]{2,1,0:T(1,128)S(1)} %reshape.149), channel_id=1, replica_groups=mesh['yh'=2,'yl'=2,'z'=4,'x'=4,'c'=2] {'x','c'}, dimensions={0} | all-to-all | bytes 32768 | tf_op jit(solution)/shard_map/all_to_all | solution.py:359
  75.1 0.6 broadcast.43
  75.7 0.7 reduce.1
  76.3 0.1 reshape.150
  76.5 0.8 reshape.151
  77.3 4.6 %all-to-all-start.3 = ((f32[64,1,512]{2,1,0:T(1,128)}), f32[64,1,512]{2,1,0:T(1,128)S(1)}, u32[]{:S(2)}, u32[]{:S(2)}) async-start(f32[64,1,512]{2,1,0:T(1,128)} %reshape.151), calls=%async_computation.3 | async-start | bytes 262144 | tf_op jit(solution)/shard_map/all_to_all | solution.py:29
  81.9 0.1 pad_add_fusion.place
  82.0 9.9 %all-to-all-done.3 = f32[64,1,512]{2,1,0:T(1,128)S(1)} async-done(((f32[64,1,512]{2,1,0:T(1,128)}), f32[64,1,512]{2,1,0:T(1,128)S(1)}, u32[]{:S(2)}, u32[]{:S(2)}) %all-to-all-start.3) | async-done | bytes 131104 | tf_op jit(solution)/shard_map/all_to_all | solution.py:29
  91.9 0.9 reduce.2
  92.9 0.1 reshape.152
  93.0 0.1 copy.41
  93.0 0.1 reshape.127
  93.2 0.0 copy-done.4
  93.2 0.1 fusion.20.rhs
  93.3 22.5 %all-gather.3.cloned.1.call-done = f32[8192,512]{1,0:T(8,128)} async-done(((f32[256,512]{1,0:T(8,128)}), f32[8192,512]{1,0:T(8,128)}) %all-gather.3.cloned.1.call-update) | async-done | bytes 16777232 | tf_op jit(solution)/shard_map/all_gather | solution.py:362
  115.7 0.0 copy-start.2
  115.7 11.3 %shard_map.104 = (f32[8,8,512]{2,1,0:T(8,128)S(1)}, bf16[28,128,512]{2,1,0:T(8,128)(2,1)}, bf16[28,128,512]{2,1,0:T(8,128)(2,1)}) custom-call(s32[2]{0:T(128)S(1)} %pad_add_fusion.place, f32[32,256,512]{2,1,0:T(8,128)} %bitcast.78, bf16[16,512,512]{2,1,0:T(8,128)(2,1)} %inv.5, f32[8,8,512]{2,1,0:T(8,128)S(1)} %fusion.20.rhs), custom_call_target="tpu_custom_call" | custom-call | tf_op jit(solution)/shard_map/pallas_call | solution.py:295
  127.0 4.9 %collective-permute-start.1 = (f32[8,512]{1,0:T(8,128)S(1)}, f32[8,512]{1,0:T(8,128)S(1)}, u32[]{:S(2)}, u32[]{:S(2)}) collective-permute-start(f32[8,512]{1,0:T(8,128)S(1)} %dynamic-slice_bitcast_fusion), channel_id=1, source_target_pairs={{0,64},{1,65},{2,66},{3,67},{4,68},{5,69},{6,70},{7,71},{8,72},{9,... | collective-permute-start | bytes 49160 | tf_op jit(solution)/shard_map/ppermute | solution.py:374
  132.0 1.4 collective-permute-done.1
  133.4 0.0 copy-done.2
  133.4 0.3 fusion.9
  133.7 10.2 %all_to_all.43 = f32[8,8,512]{2,1,0:T(8,128)S(1)} all-to-all(f32[8,8,512]{2,1,0:T(8,128)S(1)} %broadcast_in_dim.42), channel_id=1, replica_groups=mesh['yh'=2,'yl'=2,'z'=4,'x'=4,'c'=2] {'x','c'}, dimensions={0} | all-to-all | bytes 262144 | tf_op jit(solution)/shard_map/all_to_all | solution.py:29
  143.9 0.6 broadcast_in_dim.43
  144.5 3.4 %all-to-all-start.5 = ((f32[8,8,512]{2,1,0:T(8,128)}), f32[8,8,512]{2,1,0:T(8,128)S(1)}, u32[]{:S(2)}, u32[]{:S(2)}) async-start(f32[8,8,512]{2,1,0:T(8,128)} %broadcast_in_dim.43), calls=%async_computation.5 | async-start | bytes 262144 | tf_op jit(solution)/shard_map/all_to_all | solution.py:29
  147.9 6.5 %all-to-all-done.5 = f32[8,8,512]{2,1,0:T(8,128)S(1)} async-done(((f32[8,8,512]{2,1,0:T(8,128)}), f32[8,8,512]{2,1,0:T(8,128)S(1)}, u32[]{:S(2)}, u32[]{:S(2)}) %all-to-all-start.5) | async-done | bytes 131104 | tf_op jit(solution)/shard_map/all_to_all | solution.py:29
  154.5 11.2 %shard_map.105 = f32[8,8,512]{2,1,0:T(8,128)S(1)} custom-call(s32[2]{0:T(128)S(1)} %pad_add_fusion.place, bf16[28,128,512]{2,1,0:T(8,128)(2,1)} %get-tuple-element.5.kept_left, bf16[28,128,512]{2,1,0:T(8,128)(2,1)} %get-tuple-element.6.kept_right, bf16[16,512,512]{2,1,0:T(8,128)(2,1)} %inv.5, f32[8,8,512]{2,1,0:T(8,128)S(1)} %sub.16.rhs), custom_call_target="tpu_custom_call" | custom-call | tf_op jit(solution)/shard_map/pallas_call | solution.py:311
  165.6 0.3 fusion.10
  165.9 0.1 broadcast_in_dim.44
  166.0 14.0 %all_to_all.44 = f32[16,8,512]{2,1,0:T(8,128)S(1)} all-to-all(f32[16,8,512]{2,1,0:T(8,128)S(1)} %broadcast_in_dim.44), channel_id=1, replica_groups=mesh['yh'=2,'yl'=2,'z'=4,'x'=4,'c'=2] {'yh','yl','z'}, dimensions={0} | all-to-all | bytes 524288 | tf_op jit(solution)/shard_map/all_to_all | solution.py:29
  180.0 8.5 %all_to_all.45 = f32[8,8,512]{2,1,0:T(8,128)S(1)} all-to-all(f32[8,8,512]{2,1,0:T(8,128)S(1)} %broadcast_in_dim.45), channel_id=1, replica_groups=mesh['yh'=2,'yl'=2,'z'=4,'x'=4,'c'=2] {'x','c'}, dimensions={0} | all-to-all | bytes 262144 | tf_op jit(solution)/shard_map/all_to_all | solution.py:29
  188.5 0.0 copy-start.1
  188.5 0.0 copy-start.3
  188.5 7.6 %shard_map.106 = f32[8,8,512]{2,1,0:T(8,128)S(1)} custom-call(s32[2]{0:T(128)S(1)} %pad_add_fusion.place, bf16[28,128,512]{2,1,0:T(8,128)(2,1)} %get-tuple-element.5.kept_left, bf16[28,128,512]{2,1,0:T(8,128)(2,1)} %get-tuple-element.6.kept_right, bf16[16,512,512]{2,1,0:T(8,128)(2,1)} %inv.5, f32[8,8,512]{2,1,0:T(8,128)S(1)} %sub.17.rhs), custom_call_target="tpu_custom_call" | custom-call | tf_op jit(solution)/shard_map/pallas_call | solution.py:311
  196.2 1.4 collective-permute-start.2
  197.6 5.2 %collective-permute-done.2 = f32[8,8,512]{2,1,0:T(8,128)S(1)} collective-permute-done((f32[8,8,512]{2,1,0:T(8,128)S(1)}, f32[8,8,512]{2,1,0:T(8,128)S(1)}, u32[]{:S(2)}, u32[]{:S(2)}) %collective-permute-start.2) | collective-permute-done | bytes 131104 | tf_op jit(solution)/shard_map/ppermute | solution.py:388
  202.9 0.6 gather_fusion
  203.4 0.0 copy-done
  203.5 0.0 copy-done.1
  203.5 0.0 copy-done.3
  203.5 1.1 fusion.6
  204.6 0.7 constant_dynamic-slice_fusion
  (19 shorter events, 0.4 us)
Async XLA Ops:
  7.2 196.3 %copy-start = (bf16[1,512,512]{2,1,0:T(8,128)(2,1)S(1)}, bf16[1,512,512]{2,1,0:T(8,128)(2,1)}, u32[]{:S(2)}) copy-start(bf16[1,512,512]{2,1,0:T(8,128)(2,1)} %param.16) | copy-start | bytes 1572868
  7.2 86.0 %copy-start.4 = (bf16[8,8192]{1,0:T(8,128)(2,1)S(1)}, bf16[8,8192]{1,0:T(8,128)(2,1)}, u32[]{:S(2)}) copy-start(bf16[8,8192]{1,0:T(8,128)(2,1)} %param.9) | copy-start | bytes 393220
  7.2 108.5 %all-gather.3.cloned.1.call-start = ((), (), s32[]{:S(2)}) async-start(), calls=%async_computation.8 | async-start | bytes 17301504 | tf_op jit(solution)/shard_map/all_gather | solution.py:362
  10.3 14.9 %collective-permute-start = (f32[256,512]{1,0:T(8,128)S(1)}, f32[256,512]{1,0:T(8,128)S(1)}, u32[]{:S(2)}, u32[]{:S(2)}) collective-permute-start(f32[256,512]{1,0:T(8,128)S(1)} %pad_maximum_fusion), channel_id=1, source_target_pairs={{8,47},{16,54},{17,55},{24,38},{25,63},{26,39},{32,0},{33,1},{34,2... | collective-permute-start | bytes 1572872 | tf_op jit(solution)/shard_map/ppermute | solution.py:344
  77.3 14.6 %all-to-all-start.3 = ((f32[64,1,512]{2,1,0:T(1,128)}), f32[64,1,512]{2,1,0:T(1,128)S(1)}, u32[]{:S(2)}, u32[]{:S(2)}) async-start(f32[64,1,512]{2,1,0:T(1,128)} %reshape.151), calls=%async_computation.3 | async-start | bytes 262144 | tf_op jit(solution)/shard_map/all_to_all | solution.py:29
  115.7 17.7 %copy-start.2 = (bf16[1,1,1,2,128,512]{5,4,3,2,1,0:T(8,128)(2,1)S(1)}, bf16[1,1,1,2,128,512]{5,4,3,2,1,0:T(8,128)(2,1)}, u32[]{:S(2)}) copy-start(bf16[1,1,1,2,128,512]{5,4,3,2,1,0:T(8,128)(2,1)} %param.11) | copy-start | bytes 786436
  127.0 6.4 %collective-permute-start.1 = (f32[8,512]{1,0:T(8,128)S(1)}, f32[8,512]{1,0:T(8,128)S(1)}, u32[]{:S(2)}, u32[]{:S(2)}) collective-permute-start(f32[8,512]{1,0:T(8,128)S(1)} %dynamic-slice_bitcast_fusion), channel_id=1, source_target_pairs={{0,64},{1,65},{2,66},{3,67},{4,68},{5,69},{6,70},{7,71},{8,72},{9,... | collective-permute-start | bytes 49160 | tf_op jit(solution)/shard_map/ppermute | solution.py:374
  144.5 9.9 %all-to-all-start.5 = ((f32[8,8,512]{2,1,0:T(8,128)}), f32[8,8,512]{2,1,0:T(8,128)S(1)}, u32[]{:S(2)}, u32[]{:S(2)}) async-start(f32[8,8,512]{2,1,0:T(8,128)} %broadcast_in_dim.43), calls=%async_computation.5 | async-start | bytes 262144 | tf_op jit(solution)/shard_map/all_to_all | solution.py:29
  188.5 14.9 %copy-start.1 = (bf16[1,512,1024]{2,1,0:T(8,128)(2,1)S(1)}, bf16[1,512,1024]{2,1,0:T(8,128)(2,1)}, u32[]{:S(2)}) copy-start(bf16[1,512,1024]{2,1,0:T(8,128)(2,1)} %param.15) | copy-start | bytes 3145732
  188.5 14.9 %copy-start.3 = (bf16[1,8,512]{2,1,0:T(8,128)(2,1)S(1)}, bf16[1,8,512]{2,1,0:T(8,128)(2,1)}, u32[]{:S(2)}) copy-start(bf16[1,8,512]{2,1,0:T(8,128)(2,1)} %param.14) | copy-start | bytes 24580
  196.2 6.6 %collective-permute-start.2 = (f32[8,8,512]{2,1,0:T(8,128)S(1)}, f32[8,8,512]{2,1,0:T(8,128)S(1)}, u32[]{:S(2)}, u32[]{:S(2)}) collective-permute-start(f32[8,8,512]{2,1,0:T(8,128)S(1)} %broadcast_select_fusion.3), channel_id=1, source_target_pairs={{0,64},{64,0},{1,65},{65,1},{2,66},{66,2},{3,67},{67,3},{4,68},{68... | collective-permute-start | bytes 393224 | tf_op jit(solution)/shard_map/ppermute | solution.py:388
Sparse Core Ops, SparseCore 0:
  26.2 89.4 all-gather.2

commit v11 on v9

--- a/solution.py
+++ b/solution.py
@@ -240,11 +240,15 @@
     return [ref[i] for i in range(HALF)]
 
 
-def keep_tiles(leaf, place, tiles, stage, sems, kept, lsems, rsems):
+def keep_tiles(leaf, place, tiles, stage, sems, kept, lsems, rsems, out):
     moves = factor_moves(leaf, *kept, lsems, rsems, True)
     load = Loader(leaf, place, tiles, stage, sems, kept=moves)
+    total = jnp.zeros(leaf.left.shape[1:], F32)
     for i in range(1, HALF):
         load(i)
+        for k in range(i):
+            total = total + leaf.u(i, k).astype(F32) + leaf.vt(i, k).astype(F32)
+    out[0] = total.reshape(-1, *out.shape[1:]).sum(axis=0)
     moves.start(HALF - 1)
     for i in range(HALF):
         moves.wait(i)
@@ -263,7 +267,7 @@
     @pl.when(place[1] == 1)
     def _():
         out[...] = jnp.zeros(out.shape, F32)
-        keep_tiles(leaf, place, tiles, stage, sems, (kept_left, kept_right), lsems, rsems)
+        keep_tiles(leaf, place, tiles, stage, sems, (kept_left, kept_right), lsems, rsems, out)
 
 
 def second_kernel(place, tiles, kept_left, kept_right, inv, rhs, *refs):
@@ -273,7 +277,7 @@
     @pl.when(place[1] == 0)
     def _():
         out[...] = jnp.zeros(out.shape, F32)
-        keep_tiles(leaf, place, tiles, stage, sems, (next_left, next_right), lsems, rsems)
+        keep_tiles(leaf, place, tiles, stage, sems, (next_left, next_right), lsems, rsems, out)
 
     @pl.when(place[1] == 1)
     def _():
@@ -332,7 +336,7 @@
             dma((HALF,)),
             dma((TILES,)),
         ],
-        compiler_params=limit(40),
+        compiler_params=limit(28),
     )(place, *[in_hbm(v) for v in hbm], rhs)
 
 
@@ -371,8 +375,10 @@
     width = ntile * tile // ndev
     parts = dense.reshape(rhs_count, 4, ntile * tile // 4).transpose(1, 0, 2)
     mine = lax.all_to_all(parts, ("yh", "yl"), split_axis=0, concat_axis=0, tiled=True)
-    mine = mine.sum(axis=0).reshape(rhs_count, ndev // 4, width).transpose(1, 0, 2)
-    mine = lax.all_to_all(mine, PLANE, split_axis=0, concat_axis=0, tiled=True).sum(axis=0)
+    mine = mine.sum(axis=0).reshape(rhs_count, 4, tile).transpose(1, 0, 2)
+    mine = lax.all_to_all(mine, "z", split_axis=0, concat_axis=0, tiled=True).sum(axis=0)
+    mine = mine.reshape(rhs_count, 8, width).transpose(1, 0, 2)
+    mine = lax.all_to_all(mine, COL, split_axis=0, concat_axis=0, tiled=True).sum(axis=0)
     share = jnp.where(my_col < in_half, own_tile, other_tile)
     share = with_layout_constraint(share, ROWS)
     tiles = lax.all_gather(share, PLANE)

time: 212 us -> 212 us (level)
  blocking collectives: 73.3 us -> 78.8 us
  waiting for transfers between devices: 68.2 us -> 62.9 us
    all_gather x1, waiting for transfers between devices: 30.5 us -> 24.7 us  [per_device(): tiles = lax.all_gather(share, PLANE)]
    all_to_all x1 -> x2, blocking collectives: 27.6 us -> 32.6 us  [the longest x1 17.7 us: per_device(): lax.all_to_all(mine, 'z', split_axis=0, concat_axis=0, tiled=True)]
where the time goes in v11:
time: 212 us
  blocking collectives  78.8 us (37%)
  waiting for transfers between devices  62.9 us (30%)
  Pallas kernels  26.1 us (12%)
  starting transfers between devices  15.4 us (7%)
  between operations  14.4 us (7%)
  other arithmetic  6.26 us (3%)
  local copies, waits for them, and re-layouts  6.05 us (3%)
    all_to_all x3, blocking collectives, copies(): lax.all_to_all(stacked, axis, split_axis=0, concat_axis=0, tiled=True)  34.5 us
    pallas_call x3, Pallas kernels, solve(): pl.pallas_call(body, out_shape=(solved, factors, factors) if keeps else s...  26.1 us
    all_gather x1, waiting for transfers between devices, per_device(): tiles = lax.all_gather(share, PLANE)  24.7 us
    all_to_all x1, blocking collectives, per_device(): lax.all_to_all(mine, 'z', split_axis=0, concat_axis=0, tiled=True)  17.7 us
    all_to_all x2, waiting for transfers between devices, copies(): lax.all_to_all(stacked, axis, split_axis=0, concat_axis=0, tiled=True)  16.5 us
    all_to_all x1, blocking collectives, per_device(): lax.all_to_all(mine, COL, split_axis=0, concat_axis=0, tiled=True)  14.9 us
    ppermute x1, waiting for transfers between devices, per_device(): other_tile = lax.ppermute(own_tile, ALL, plane_pairs())  13.8 us
    all_to_all x1, blocking collectives, per_device(): lax.all_to_all(parts, ('yh', 'yl'), split_axis=0, concat_axis=0, tiled=True)  11.7 us
  transfers between devices with their start and end apart: 6, of which 6 were waited for; matrix products, arithmetic and copies ran while one was open for 3% of the time, Pallas kernels for 0%

profile of v11, /device:TPU:0, one launch (start us, length us, event | category | flops | bytes accessed | tf_op | source)
XLA Modules:
  0.0 211.9 jit_solution(7970699047310233215)
XLA Ops:
  7.2 0.0 copy-start
  7.2 0.0 copy-start.1
  7.2 0.0 all-gather.3.cloned.1.call-start
  7.2 1.2 copy.36
  8.4 0.7 iota_compare_fusion
  9.2 0.0 copy-start.5
  9.2 0.0 copy-start.3
  9.2 0.1 convert_select_fusion
  9.3 1.0 fusion.19
  10.3 0.8 pad_maximum_fusion
  11.2 1.3 collective-permute-start
  12.5 13.8 %collective-permute-done = f32[256,512]{1,0:T(8,128)S(1)} collective-permute-done((f32[256,512]{1,0:T(8,128)}, f32[256,512]{1,0:T(8,128)S(1)}, u32[]{:S(2)}, u32[]{:S(2)}) %collective-permute-start) | collective-permute-done | bytes 524320 | tf_op jit(solution)/shard_map/ppermute | solution.py:366
  26.2 0.9 broadcast_select_fusion
  27.1 0.0 all-gather.3.cloned.1.call-update
  27.1 0.0 copy-done.1
  27.1 0.5 copy.45
  27.7 0.0 copy-done.5
  27.7 0.0 copy-start.4
  27.7 0.0 copy-done.3
  27.7 0.4 convolution_bitcast_fusion
  28.1 0.8 scatter_fusion
  28.9 0.1 copy.38
  29.0 0.1 reshape.124
  29.1 0.2 copy.39
  29.3 11.7 %all_to_all.40 = f32[4,8,2048]{2,1,0:T(8,128)S(1)} all-to-all(f32[4,8,2048]{2,1,0:T(8,128)S(1)} %copy.39), channel_id=1, replica_groups=mesh['yh'=2,'yl'=2,'z'=4,'x'=4,'c'=2] {'yh','yl'}, dimensions={0} | all-to-all | bytes 524288 | tf_op jit(solution)/shard_map/all_to_all | solution.py:377
  41.0 17.7 %all_to_all.41 = f32[4,8,512]{2,1,0:T(8,128)S(1)} all-to-all(f32[4,8,512]{2,1,0:T(8,128)S(1)} %bitcast.86), channel_id=1, replica_groups=mesh['yh'=2,'yl'=2,'z'=4,'x'=4,'c'=2] {'z'}, dimensions={0} | all-to-all | bytes 131072 | tf_op jit(solution)/shard_map/all_to_all | solution.py:379
  58.7 0.1 reshape.126
  58.8 0.1 reshape.149
  58.9 14.9 %all_to_all.42 = f32[8,1,512]{2,1,0:T(1,128)S(1)} all-to-all(f32[8,1,512]{2,1,0:T(1,128)S(1)} %reshape.149), channel_id=1, replica_groups=mesh['yh'=2,'yl'=2,'z'=4,'x'=4,'c'=2] {'x','c'}, dimensions={0} | all-to-all | bytes 32768 | tf_op jit(solution)/shard_map/all_to_all | solution.py:381
  73.8 0.6 broadcast.43
  74.4 0.7 reduce.1
  75.0 0.1 reshape.150
  75.1 0.8 reshape.151
  76.0 4.6 %all-to-all-start.3 = ((f32[64,1,512]{2,1,0:T(1,128)}), f32[64,1,512]{2,1,0:T(1,128)S(1)}, u32[]{:S(2)}, u32[]{:S(2)}) async-start(f32[64,1,512]{2,1,0:T(1,128)} %reshape.151), calls=%async_computation.3 | async-start | bytes 262144 | tf_op jit(solution)/shard_map/all_to_all | solution.py:29
  80.6 0.1 pad_add_fusion.place
  80.7 9.9 %all-to-all-done.3 = f32[64,1,512]{2,1,0:T(1,128)S(1)} async-done(((f32[64,1,512]{2,1,0:T(1,128)}), f32[64,1,512]{2,1,0:T(1,128)S(1)}, u32[]{:S(2)}, u32[]{:S(2)}) %all-to-all-start.3) | async-done | bytes 131104 | tf_op jit(solution)/shard_map/all_to_all | solution.py:29
  90.6 0.9 reduce.2
  91.5 0.1 reshape.152
  91.7 0.1 copy.41
  91.7 0.1 reshape.127
  91.8 0.0 copy-done.4
  91.8 0.1 fusion.20.rhs
  91.9 24.7 %all-gather.3.cloned.1.call-done = f32[8192,512]{1,0:T(8,128)} async-done(((f32[256,512]{1,0:T(8,128)}), f32[8192,512]{1,0:T(8,128)}) %all-gather.3.cloned.1.call-update) | async-done | bytes 16777232 | tf_op jit(solution)/shard_map/all_gather | solution.py:384
  116.6 8.7 %shard_map.104 = (f32[8,8,512]{2,1,0:T(8,128)S(1)}, bf16[28,128,512]{2,1,0:T(8,128)(2,1)}, bf16[28,128,512]{2,1,0:T(8,128)(2,1)}) custom-call(s32[2]{0:T(128)S(1)} %pad_add_fusion.place, f32[32,256,512]{2,1,0:T(8,128)} %bitcast.78, bf16[16,512,512]{2,1,0:T(8,128)(2,1)} %inv.5, f32[8,8,512]{2,1,0:T(8,128)S(1)} %fusion.20.rhs), custom_call_target="tpu_custom_call" | custom-call | tf_op jit(solution)/shard_map/pallas_call | solution.py:325
  125.4 6.0 %collective-permute-start.1 = (f32[8,512]{1,0:T(8,128)S(1)}, f32[8,512]{1,0:T(8,128)S(1)}, u32[]{:S(2)}, u32[]{:S(2)}) collective-permute-start(f32[8,512]{1,0:T(8,128)S(1)} %dynamic-slice_bitcast_fusion), channel_id=1, source_target_pairs={{0,64},{1,65},{2,66},{3,67},{4,68},{5,69},{6,70},{7,71},{8,72},{9,... | collective-permute-start | bytes 49160 | tf_op jit(solution)/shard_map/ppermute | solution.py:396
  131.3 1.4 collective-permute-done.1
  132.8 0.0 copy-done.2
  132.8 0.3 fusion.9
  133.1 10.1 %all_to_all.43 = f32[8,8,512]{2,1,0:T(8,128)S(1)} all-to-all(f32[8,8,512]{2,1,0:T(8,128)S(1)} %broadcast_in_dim.42), channel_id=1, replica_groups=mesh['yh'=2,'yl'=2,'z'=4,'x'=4,'c'=2] {'x','c'}, dimensions={0} | all-to-all | bytes 262144 | tf_op jit(solution)/shard_map/all_to_all | solution.py:29
  143.3 0.7 broadcast_in_dim.43
  143.9 3.4 %all-to-all-start.5 = ((f32[8,8,512]{2,1,0:T(8,128)}), f32[8,8,512]{2,1,0:T(8,128)S(1)}, u32[]{:S(2)}, u32[]{:S(2)}) async-start(f32[8,8,512]{2,1,0:T(8,128)} %broadcast_in_dim.43), calls=%async_computation.5 | async-start | bytes 262144 | tf_op jit(solution)/shard_map/all_to_all | solution.py:29
  147.3 6.5 %all-to-all-done.5 = f32[8,8,512]{2,1,0:T(8,128)S(1)} async-done(((f32[8,8,512]{2,1,0:T(8,128)}), f32[8,8,512]{2,1,0:T(8,128)S(1)}, u32[]{:S(2)}, u32[]{:S(2)}) %all-to-all-start.5) | async-done | bytes 131104 | tf_op jit(solution)/shard_map/all_to_all | solution.py:29
  153.8 9.8 %shard_map.105 = (f32[8,8,512]{2,1,0:T(8,128)S(1)}, bf16[28,128,512]{2,1,0:T(8,128)(2,1)}, bf16[28,128,512]{2,1,0:T(8,128)(2,1)}) custom-call(s32[2]{0:T(128)S(1)} %pad_add_fusion.place, f32[32,256,512]{2,1,0:T(8,128)} %bitcast.79, bf16[28,128,512]{2,1,0:T(8,128)(2,1)} %get-tuple-element.8.kept_left, bf16[28,128,512]{2,1,0:T(8,128)(2,1)} %get-tuple-element.9.kept_right, ...), custom_call_target="tpu_custom_call" | custom-call | tf_op jit(solution)/shard_map/pallas_call | solution.py:325
  163.6 0.3 fusion.10
  163.9 0.1 broadcast_in_dim.44
  164.0 15.8 %all_to_all.44 = f32[16,8,512]{2,1,0:T(8,128)S(1)} all-to-all(f32[16,8,512]{2,1,0:T(8,128)S(1)} %broadcast_in_dim.44), channel_id=1, replica_groups=mesh['yh'=2,'yl'=2,'z'=4,'x'=4,'c'=2] {'yh','yl','z'}, dimensions={0} | all-to-all | bytes 524288 | tf_op jit(solution)/shard_map/all_to_all | solution.py:29
  179.8 8.5 %all_to_all.45 = f32[8,8,512]{2,1,0:T(8,128)S(1)} all-to-all(f32[8,8,512]{2,1,0:T(8,128)S(1)} %broadcast_in_dim.45), channel_id=1, replica_groups=mesh['yh'=2,'yl'=2,'z'=4,'x'=4,'c'=2] {'x','c'}, dimensions={0} | all-to-all | bytes 262144 | tf_op jit(solution)/shard_map/all_to_all | solution.py:29
  188.3 7.6 %shard_map.106 = f32[8,8,512]{2,1,0:T(8,128)S(1)} custom-call(s32[2]{0:T(128)S(1)} %pad_add_fusion.place, bf16[28,128,512]{2,1,0:T(8,128)(2,1)} %get-tuple-element.12.kept_left, bf16[28,128,512]{2,1,0:T(8,128)(2,1)} %get-tuple-element.13.kept_right, bf16[16,512,512]{2,1,0:T(8,128)(2,1)} %inv.5, f32[8,8,512]{2,1,0:T(8,128)S(1)} %sub.17.rhs), custom_call_target="tpu_custom_call" | custom-call | tf_op jit(solution)/shard_map/pallas_call | solution.py:325
  196.0 0.1 collective-permute-start.2
  196.1 6.5 %collective-permute-done.2 = f32[8,8,512]{2,1,0:T(8,128)S(1)} collective-permute-done((f32[8,8,512]{2,1,0:T(8,128)S(1)}, f32[8,8,512]{2,1,0:T(8,128)S(1)}, u32[]{:S(2)}, u32[]{:S(2)}) %collective-permute-start.2) | collective-permute-done | bytes 131104 | tf_op jit(solution)/shard_map/ppermute | solution.py:411
  202.7 0.6 gather_fusion
  203.3 0.0 copy-done
  203.3 1.1 fusion.6
  204.4 0.7 constant_dynamic-slice_fusion
  (20 shorter events, 0.3 us)
Async XLA Ops:
  7.2 196.1 %copy-start = (bf16[1,512,512]{2,1,0:T(8,128)(2,1)S(1)}, bf16[1,512,512]{2,1,0:T(8,128)(2,1)}, u32[]{:S(2)}) copy-start(bf16[1,512,512]{2,1,0:T(8,128)(2,1)} %param.16) | copy-start | bytes 1572868
  7.2 20.0 %copy-start.1 = (bf16[1,512,1024]{2,1,0:T(8,128)(2,1)S(1)}, bf16[1,512,1024]{2,1,0:T(8,128)(2,1)}, u32[]{:S(2)}) copy-start(bf16[1,512,1024]{2,1,0:T(8,128)(2,1)} %param.15) | copy-start | bytes 3145732
  7.2 109.4 %all-gather.3.cloned.1.call-start = ((), (), s32[]{:S(2)}) async-start(), calls=%async_computation.8 | async-start | bytes 17301504 | tf_op jit(solution)/shard_map/all_gather | solution.py:384
  9.2 18.5 %copy-start.5 = (s32[1,8]{1,0:T(1,128)S(1)}, s32[1,8]{1,0:T(1,128)}, u32[]{:S(2)}) copy-start(s32[1,8]{1,0:T(1,128)} %param.17) | copy-start | bytes 100
  9.2 18.6 %copy-start.3 = (bf16[1,8,512]{2,1,0:T(8,128)(2,1)S(1)}, bf16[1,8,512]{2,1,0:T(8,128)(2,1)}, u32[]{:S(2)}) copy-start(bf16[1,8,512]{2,1,0:T(8,128)(2,1)} %param.14) | copy-start | bytes 24580
  11.2 15.1 %collective-permute-start = (f32[256,512]{1,0:T(8,128)}, f32[256,512]{1,0:T(8,128)S(1)}, u32[]{:S(2)}, u32[]{:S(2)}) collective-permute-start(f32[256,512]{1,0:T(8,128)} %pad_maximum_fusion), channel_id=1, source_target_pairs={{8,47},{16,54},{17,55},{24,38},{25,63},{26,39},{32,0},{33,1},{34,2... | collective-permute-start | bytes 1572872 | tf_op jit(solution)/shard_map/ppermute | solution.py:366
  27.7 64.1 %copy-start.4 = (bf16[8,8192]{1,0:T(8,128)(2,1)S(1)}, bf16[8,8192]{1,0:T(8,128)(2,1)}, u32[]{:S(2)}) copy-start(bf16[8,8192]{1,0:T(8,128)(2,1)} %param.9) | copy-start | bytes 393220
  76.0 14.6 %all-to-all-start.3 = ((f32[64,1,512]{2,1,0:T(1,128)}), f32[64,1,512]{2,1,0:T(1,128)S(1)}, u32[]{:S(2)}, u32[]{:S(2)}) async-start(f32[64,1,512]{2,1,0:T(1,128)} %reshape.151), calls=%async_computation.3 | async-start | bytes 262144 | tf_op jit(solution)/shard_map/all_to_all | solution.py:29
  116.6 16.1 %copy-start.2 = (bf16[1,1,1,2,128,512]{5,4,3,2,1,0:T(8,128)(2,1)S(1)}, bf16[1,1,1,2,128,512]{5,4,3,2,1,0:T(8,128)(2,1)}, u32[]{:S(2)}) copy-start(bf16[1,1,1,2,128,512]{5,4,3,2,1,0:T(8,128)(2,1)} %param.11) | copy-start | bytes 786436
  125.4 7.4 %collective-permute-start.1 = (f32[8,512]{1,0:T(8,128)S(1)}, f32[8,512]{1,0:T(8,128)S(1)}, u32[]{:S(2)}, u32[]{:S(2)}) collective-permute-start(f32[8,512]{1,0:T(8,128)S(1)} %dynamic-slice_bitcast_fusion), channel_id=1, source_target_pairs={{0,64},{1,65},{2,66},{3,67},{4,68},{5,69},{6,70},{7,71},{8,72},{9,... | collective-permute-start | bytes 49160 | tf_op jit(solution)/shard_map/ppermute | solution.py:396
  143.9 9.9 %all-to-all-start.5 = ((f32[8,8,512]{2,1,0:T(8,128)}), f32[8,8,512]{2,1,0:T(8,128)S(1)}, u32[]{:S(2)}, u32[]{:S(2)}) async-start(f32[8,8,512]{2,1,0:T(8,128)} %broadcast_in_dim.43), calls=%async_computation.5 | async-start | bytes 262144 | tf_op jit(solution)/shard_map/all_to_all | solution.py:29
  196.0 6.6 %collective-permute-start.2 = (f32[8,8,512]{2,1,0:T(8,128)S(1)}, f32[8,8,512]{2,1,0:T(8,128)S(1)}, u32[]{:S(2)}, u32[]{:S(2)}) collective-permute-start(f32[8,8,512]{2,1,0:T(8,128)S(1)} %broadcast_select_fusion.3), channel_id=1, source_target_pairs={{0,64},{64,0},{1,65},{65,1},{2,66},{66,2},{3,67},{67,3},{4,68},{68... | collective-permute-start | bytes 393224 | tf_op jit(solution)/shard_map/ppermute | solution.py:411
Sparse Core Ops, SparseCore 0:
  27.3 89.3 all-gather.2
